TPU v7x, 512 devices: a 8x2x16 block of a 8x16x16 slice. The times are simulated.
512 devices in a mesh: scan: 2 (over y), ang: 32 (over z, core), row: 8 (over x).
Axes of the slice: x: 8, y: 2, z: 16, core: 2. Of those that a mesh axis runs over, the one named last changes fastest.
The devices are a block of a 8x16x16 slice.
Arguments:
- projections: bfloat16 [64, 64, 2560], P(('scan', 'ang'), 'row'), parts along dimension 0, may hold values from 0 to 2
- flats: float32 [128, 2560], P(('scan', 'row')), parts along dimension 0, may hold values from 1 to 3
- block_start: int32 [32, 32], replicated, may hold values from 0 to 2528
- bp_weights: bfloat16 [32, 32, 8192], P(None, None, 'ang'), may hold values from -0.1875 to 0.1875
Outputs:
- recon: float32 [128, 8192], P(('scan', 'row'), 'ang'), parts along dimension 0
There are 2 independent parts, one for each index of `scan`. A program takes and returns all parts, laid end to end along the dimension named above; an argument that names none is the same for every part. Nothing has to cross between parts.
Inputs may be any that keep to these rules, and one draw needn't show every extreme that they name: block_start[a, r] is the first of the 32 detector columns that pixel region r reads at angle a.
All inputs are finite; a program needn't handle non-finite values.
Results may differ from a plain program's by a relative error of at most 0.009.
Values may be sent and summed in bfloat16 or wider, within the bound.
No kernel may reach another device: no remote copies, remote signals or barrier semaphores. Data moves between devices by JAX's collectives and lax.ppermute only.
A program may use at most 64 MiB of HBM per device.

v0:
```python
from functools import partial

import jax
import jax.numpy as jnp
from jax import lax
from jax.sharding import PartitionSpec as P

HALO = 4


paganin_beta = 8.0
ramp_gain = 320.0
highest = lax.Precision.HIGHEST


def with_halo(x, sides, width):
    for axis, dim in sides:
        peers, length = (lax.axis_size(axis), x.shape[dim])
        up = [(i, (i + 1) % peers) for i in range(peers - 1)]
        down = [(j, i) for i, j in up]
        last = lax.slice_in_dim(x, length - width, length, axis=dim)
        initial = lax.slice_in_dim(x, 0, width, axis=dim)
        before = lax.ppermute(last, axis, up)
        after = lax.ppermute(initial, axis, down)
        x = jnp.concatenate([before, x, after], axis=dim)
    return x


def contract(form, left, right):
    return jnp.einsum(form, left, right, precision=highest)


def circle_table(count):
    index = jnp.arange(count, dtype=jnp.int32)
    phase = index[:, None] * index[None, :] % count
    angle = 2.0 * jnp.pi / count * phase.astype(jnp.float32)
    return (jnp.cos(angle), jnp.sin(angle))


def twiddle_table(blocks, width):
    first = jnp.arange(blocks, dtype=jnp.int32)
    second = jnp.arange(128, dtype=jnp.int32)
    phase = first[:, None] * second[None, :] % width
    angle = 2.0 * jnp.pi / width * phase.astype(jnp.float32)
    return (jnp.cos(angle), jnp.sin(angle))


def columns_forward(values, tables):
    outer_cos, outer_sin, turn_cos, turn_sin, inner_cos, inner_sin = tables
    first_re = contract("...ab,ak->...kb", values, outer_cos)
    first_im = -contract("...ab,ak->...kb", values, outer_sin)
    turned_re = first_re * turn_cos + first_im * turn_sin
    turned_im = first_im * turn_cos - first_re * turn_sin
    spec_re = contract("...kb,bm->...km", turned_re, inner_cos) + contract(
        "...kb,bm->...km", turned_im, inner_sin
    )
    spec_im = contract("...kb,bm->...km", turned_im, inner_cos) - contract(
        "...kb,bm->...km", turned_re, inner_sin
    )
    return (spec_re, spec_im)


def columns_inverse(spec_re, spec_im, tables):
    outer_cos, outer_sin, turn_cos, turn_sin, inner_cos, inner_sin = tables
    back_re = contract("...km,bm->...kb", spec_re, inner_cos) - contract(
        "...km,bm->...kb", spec_im, inner_sin
    )
    back_im = contract("...km,bm->...kb", spec_im, inner_cos) + contract(
        "...km,bm->...kb", spec_re, inner_sin
    )
    untwist_re = back_re * turn_cos - back_im * turn_sin
    untwist_im = back_im * turn_cos + back_re * turn_sin
    values = contract("...kb,ak->...ab", untwist_re, outer_cos) - contract(
        "...kb,ak->...ab", untwist_im, outer_sin
    )
    return values / (outer_cos.shape[0] * 128)


def body(projections, flats, block_start, bp_weights):
    angles_dev, rows_dev, width = projections.shape
    blocks_count = width // 128
    tile_rows = rows_dev + 2 * HALO
    cb_width = bp_weights.shape[1]
    outer_cos, outer_sin = circle_table(blocks_count)
    turn_cos, turn_sin = twiddle_table(blocks_count, width)
    inner_cos, inner_sin = circle_table(128)
    tables = (outer_cos, outer_sin, turn_cos, turn_sin, inner_cos, inner_sin)
    row_cos, row_sin = circle_table(tile_rows)
    freq_index = (
        jnp.arange(blocks_count, dtype=jnp.int32)[:, None]
        + blocks_count * jnp.arange(128, dtype=jnp.int32)[None, :]
    )
    col_freq = freq_index.astype(jnp.float32)
    row_freq = jnp.arange(tile_rows, dtype=jnp.float32)
    lam = (4.0 * jnp.sin(jnp.pi * row_freq / tile_rows) ** 2)[:, None, None] + (
        4.0 * jnp.sin(jnp.pi * col_freq / width) ** 2
    )[None, :, :]
    filt = 1.0 / (1.0 + paganin_beta * lam)
    folded = jnp.minimum(col_freq, width - col_freq)
    ramp = ramp_gain * (folded / width) * (0.5 + 0.5 * jnp.cos(2.0 * jnp.pi * folded / width))
    contrast = 1.0 - projections.astype(jnp.float32) / flats[None, :, :]
    shaped = contrast.reshape(angles_dev, rows_dev, blocks_count, 128)
    own_re, own_im = columns_forward(shaped, tables)
    stacked = with_halo(
        jnp.stack((own_re, own_im)).astype(jnp.bfloat16), (("row", 2),), HALO
    ).astype(jnp.float32)
    spec_re = stacked[0]
    spec_im = stacked[1]
    rows_re = contract("tk,atbm->akbm", row_cos, spec_re) + contract(
        "tk,atbm->akbm", row_sin, spec_im
    )
    rows_im = contract("tk,atbm->akbm", row_cos, spec_im) - contract(
        "tk,atbm->akbm", row_sin, spec_re
    )
    rows_re = rows_re * filt
    rows_im = rows_im * filt
    inner_rcos = row_cos[HALO : HALO + rows_dev]
    inner_rsin = row_sin[HALO : HALO + rows_dev]
    kept_re = (
        contract("tk,akbm->atbm", inner_rcos, rows_re)
        - contract("tk,akbm->atbm", inner_rsin, rows_im)
    ) / tile_rows
    kept_im = (
        contract("tk,akbm->atbm", inner_rcos, rows_im)
        + contract("tk,akbm->atbm", inner_rsin, rows_re)
    ) / tile_rows
    filtered = columns_inverse(kept_re * ramp, kept_im * ramp, tables)
    sinogram = filtered.reshape(angles_dev, rows_dev, width).astype(jnp.bfloat16)
    region = lax.axis_index("ang")
    region_count = lax.axis_size("ang")

    def cut_block(sheet, begin):
        return lax.dynamic_slice(sheet, (0, begin), (rows_dev, cb_width))

    my_starts = lax.dynamic_slice_in_dim(block_start, region * angles_dev, angles_dev, 0)

    def cut_angle(sheet, starts_row):
        return jax.vmap(partial(cut_block, sheet))(starts_row)

    pieces = jax.vmap(cut_angle)(sinogram, my_starts)
    outgoing = jnp.transpose(pieces, (1, 2, 0, 3)).reshape(
        region_count, rows_dev, angles_dev * cb_width
    )
    incoming = lax.all_to_all(outgoing, "ang", split_axis=0, concat_axis=0, tiled=True)
    recon = lax.dot_general(
        incoming, bp_weights, (((0, 2), (0, 1)), ((), ())), preferred_element_type=jnp.float32
    )
    return recon


def solution(mesh):
    placed = (P(("scan", "ang"), "row", None), P(("scan", "row"), None), P(), P(None, None, "ang"))
    return jax.shard_map(
        body, mesh=mesh, in_specs=placed, out_specs=P(("scan", "row"), "ang"), check_vma=False
    )
```

profile of v0, /device:TPU:70, one launch (start us, length us, event | category | flops | bytes accessed | tf_op | source)
XLA Modules:
  0.0 80.4 jit_solution(5224957624122114996)
XLA Ops:
  0.0 0.0 copy-start
  0.0 0.1 fusion.88
  0.1 1.0 %fusion.42 = f32[8,20,128]{2,0,1:T(8,128)S(1)} fusion(f32[8,2560]{1,0:T(8,128)} %param.5, bf16[1,8,2560]{2,1,0:T(8,128)(2,1)} %param.4), kind=kLoop, calls=%fused_computation.67 | loop fusion | flops 61440 | bytes 204800 | tf_op jit(solution)/shard_map/reshape
  1.0 0.4 fusion.7
  1.4 0.4 convolution_bitcast_fusion
  1.8 0.5 fusion.31
  2.3 0.5 fusion.29
  2.8 0.5 fusion.18
  3.3 0.5 fusion.19
  3.8 4.8 %collective-permute-start = (bf16[2,1,4,20,128]{4,3,2,1,0:T(8,128)(2,1)S(1)}, bf16[2,1,4,20,128]{4,3,2,1,0:T(8,128)(2,1)S(1)}, u32[]{:S(2)}, u32[]{:S(2)}) collective-permute-start(bf16[2,1,4,20,128]{4,3,2,1,0:T(8,128)(2,1)S(1)} %get-tuple-element.7), channel_id=1, source_target_pairs={{0,1},{1,2},{2,3},{3,4},{4,5},{5,6},{6,7},{8,9},{9,10},{10,11},{11... | collective-permute-start | bytes 122888 | tf_op jit(solution)/shard_map/ppermute | solution.py:23
  8.6 2.0 %collective-permute-start.1 = (bf16[2,1,4,20,128]{4,3,2,1,0:T(8,128)(2,1)S(1)}, bf16[2,1,4,20,128]{4,3,2,1,0:T(8,128)(2,1)S(1)}, u32[]{:S(2)}, u32[]{:S(2)}) collective-permute-start(bf16[2,1,4,20,128]{4,3,2,1,0:T(8,128)(2,1)S(1)} %get-tuple-element.8), channel_id=1, source_target_pairs={{1,0},{2,1},{3,2},{4,3},{5,4},{6,5},{7,6},{9,8},{10,9},{11,10},{12... | collective-permute-start | bytes 122888 | tf_op jit(solution)/shard_map/ppermute | solution.py:24
  10.5 0.1 fusion.123
  10.6 0.1 fusion.122
  10.7 0.7 fusion.130
  11.4 0.1 multiply_multiply_fusion
  11.6 0.0 collective-permute-done
  11.6 4.2 %collective-permute-done.1 = bf16[2,1,4,20,128]{4,3,2,1,0:T(8,128)(2,1)S(1)} collective-permute-done((bf16[2,1,4,20,128]{4,3,2,1,0:T(8,128)(2,1)S(1)}, bf16[2,1,4,20,128]{4,3,2,1,0:T(8,128)(2,1)S(1)}, u32[]{:S(2)}, u32[]{:S(2)}) %collective-permute-start.1) | collective-permute-done | bytes 40992 | tf_op jit(solution)/shard_map/ppermute | solution.py:24
  15.9 0.3 fusion.61
  16.2 0.3 fusion.57
  16.5 0.3 fusion.3
  16.9 0.3 fusion.5
  17.2 0.2 fusion.128
  17.4 0.2 fusion.129
  17.6 0.2 fusion.16
  17.9 0.2 fusion.14
  18.1 0.5 fusion.24
  18.6 0.5 fusion.20
  19.1 0.5 convolution_subtract_fusion.2
  19.6 0.5 convolution_add_fusion.1
  20.1 0.3 fusion.37
  20.5 0.3 fusion.17
  20.8 1.0 %copy.39 = bf16[1,8,2560]{1,0,2:T(2,128)(2,1)S(1)} copy(bf16[1,8,2560]{2,1,0:T(8,128)(2,1)S(1)} %convert_element_type.122) | data formatting | bytes 81920 | tf_op jit(solution)/shard_map/convert_element_type | solution.py:128
  21.8 1.2 %gather_fusion = bf16[32,8,32]{1,0,2:T(8,128)(2,1)S(1)} fusion(bf16[1,8,2560]{1,0,2:T(2,128)(2,1)S(1)} %copy.39, s32[32]{0:T(128)S(1)} %or_bitcast_fusion), kind=kCustom, calls=%fused_computation | custom fusion | bytes 33152 | tf_op jit(solution)/shard_map/vmap(vmap())/gather | solution.py:133
  23.0 0.3 copy.40
  23.3 0.1 reshape.258
  23.4 56.1 %all_to_all.5 = bf16[32,2,128]{2,1,0:T(2,128)(2,1)S(1)} all-to-all(bf16[32,2,128]{2,1,0:T(2,128)(2,1)S(1)} %reshape.258), channel_id=1, replica_groups=mesh['scan'=2,'ang'=32,'row'=8] {'ang'}, dimensions={0} | all-to-all | bytes 32768 | tf_op jit(solution)/shard_map/all_to_all | solution.py:144
  79.5 0.1 reshape.259
  79.6 0.0 copy-done
  79.6 0.8 %convolution_bitcast_fusion.1 = f32[8,256]{1,0:T(8,128)} fusion(bf16[32,8,32]{2,1,0:T(8,128)(2,1)S(1)} %reshape.259, bf16[32,32,256]{2,1,0:T(8,128)(2,1)S(1)} %copy-done), kind=kOutput, calls=%fused_computation.32 | convolution fusion | flops 4194304 | bytes 548864 | tf_op jit(solution)/shard_map/dot_general | solution.py:145
  (8 shorter events, 0.2 us)
Async XLA Ops:
  0.0 79.6 %copy-start = (bf16[32,32,256]{2,1,0:T(8,128)(2,1)S(1)}, bf16[32,32,256]{2,1,0:T(8,128)(2,1)}, u32[]{:S(2)}) copy-start(bf16[32,32,256]{2,1,0:T(8,128)(2,1)} %param.7) | copy-start | bytes 1572868
  3.8 7.8 %collective-permute-start = (bf16[2,1,4,20,128]{4,3,2,1,0:T(8,128)(2,1)S(1)}, bf16[2,1,4,20,128]{4,3,2,1,0:T(8,128)(2,1)S(1)}, u32[]{:S(2)}, u32[]{:S(2)}) collective-permute-start(bf16[2,1,4,20,128]{4,3,2,1,0:T(8,128)(2,1)S(1)} %get-tuple-element.7), channel_id=1, source_target_pairs={{0,1},{1,2},{2,3},{3,4},{4,5},{5,6},{6,7},{8,9},{9,10},{10,11},{11... | collective-permute-start | bytes 122888 | tf_op jit(solution)/shard_map/ppermute | solution.py:23
  8.6 7.2 %collective-permute-start.1 = (bf16[2,1,4,20,128]{4,3,2,1,0:T(8,128)(2,1)S(1)}, bf16[2,1,4,20,128]{4,3,2,1,0:T(8,128)(2,1)S(1)}, u32[]{:S(2)}, u32[]{:S(2)}) collective-permute-start(bf16[2,1,4,20,128]{4,3,2,1,0:T(8,128)(2,1)S(1)} %get-tuple-element.8), channel_id=1, source_target_pairs={{1,0},{2,1},{3,2},{4,3},{5,4},{6,5},{7,6},{9,8},{10,9},{11,10},{12... | collective-permute-start | bytes 122888 | tf_op jit(solution)/shard_map/ppermute | solution.py:24
where the time goes:
time: 80.6 us; the launch traced here: 80.4 us
  blocking collectives  56.1 us (70%)
  matrix products  8.36 us (10%)
  starting transfers between devices  6.73 us (8%)
  waiting for transfers between devices  4.23 us (5%)
  local copies, waits for them, and re-layouts  2.73 us (3%)
  other arithmetic  2.07 us (3%)
    all_to_all x1, blocking collectives, body(): lax.all_to_all(outgoing, 'ang', split_axis=0, concat_axis=0, tiled=True)  56.1 us
    dot_general x20, matrix products, contract(): return jnp.einsum(form, left, right, precision=highest)  7.51 us
    ppermute x1, starting transfers between devices, with_halo(): before = lax.ppermute(last, axis, up)  4.78 us
    ppermute x1, waiting for transfers between devices, with_halo(): after = lax.ppermute(initial, axis, down)  4.23 us
    ppermute x1, starting transfers between devices, with_halo(): after = lax.ppermute(initial, axis, down)  1.95 us
  transfers between devices with their start and end apart: 2, of which 1 were waited for; matrix products, arithmetic and copies ran while one was open for 1% of the time, Pallas kernels for 0%

commit v1 on v0

v1 whole, which is shorter than its diff:
```python
from functools import partial

import jax
import jax.numpy as jnp
import numpy as np
from jax import lax
from jax.experimental import pallas as pl
from jax.experimental.pallas import tpu as pltpu
from jax.sharding import PartitionSpec as P

HALO = 4
LANES = 128
SUB = 8

paganin_beta = 8.0
ramp_gain = 320.0
halo_type = jnp.float32
VMEM = pl.BlockSpec(memory_space=pltpu.VMEM)
ANY = pl.BlockSpec(memory_space=pl.ANY)


def tables(width, tile_rows):
    blocks = width // LANES
    half = blocks // 2
    lane = np.arange(LANES)
    ks = np.arange(half + 1)
    turn = 2.0 * np.pi / width * (ks[:, None] * lane[None, :])
    turns = np.stack((np.cos(turn), np.sin(turn))).astype(np.float32)
    angle = 2.0 * np.pi / LANES * (lane[:, None] * lane[None, :] % LANES)
    cos, sin = np.cos(angle), np.sin(angle)
    forward = np.block([[cos, -sin], [sin, cos]])

    def split(matrix):
        high = matrix.astype(jnp.bfloat16)
        low = (matrix - high.astype(np.float64)).astype(jnp.bfloat16)
        return np.stack((high, low))

    freq = (ks[:, None] + blocks * lane[None, :]).astype(np.float64)
    row = np.arange(tile_rows, dtype=np.float64)
    lam = 4.0 * np.sin(np.pi * row / tile_rows)[:, None, None] ** 2 + 4.0 * np.sin(np.pi * freq / width) ** 2
    filt = 1.0 / (1.0 + paganin_beta * lam)
    dist = np.arange(tile_rows // 2 + 1)
    gains = np.einsum("du,ukm->dkm", np.cos(2.0 * np.pi / tile_rows * dist[:, None] * row), filt) / tile_rows
    folded = np.minimum(freq, width - freq)
    ramp = ramp_gain * (folded / width) * (0.5 + 0.5 * np.cos(2.0 * np.pi * folded / width))
    twice = np.where((ks == 0) | (ks == half), 1.0, 2.0)
    gains = gains * (ramp * twice[:, None] / width)
    return turns, split(forward), split(forward.T), gains.astype(np.float32)


def plus(terms):
    return sum(terms[1:], terms[0])


def scaled(terms, weights):
    out = None
    for term, weight in zip(terms, weights):
        weight = float(weight)
        if abs(weight) < 1e-12:
            continue
        piece = term if weight == 1.0 else -term if weight == -1.0 else term * weight
        out = piece if out is None else out + piece
    return out


def cosine_sums(terms, blocks):
    half = blocks // 2
    out = [None] * (half + 1)
    for k in range(half // 2 + 1):
        wave = [np.round(np.cos(2.0 * np.pi * a * k / blocks), 15) for a in range(half + 1)]
        even = scaled(terms[0::2], wave[0::2])
        odd = scaled(terms[1::2], wave[1::2])
        out[k] = even if odd is None else even + odd
        if half - k != k:
            out[half - k] = even if odd is None else even - odd
    return out


def sine_sums(terms, blocks):
    half = blocks // 2
    out = [None] * (half + 1)
    for k in range(1, half // 2 + 1):
        wave = [np.round(np.sin(2.0 * np.pi * a * k / blocks), 15) for a in range(half)]
        even = scaled(terms[2:half:2], wave[2::2])
        odd = scaled(terms[1:half:2], wave[1::2])
        if half - k != k:
            out[k] = plus([x for x in (even, odd) if x is not None])
            out[half - k] = odd - even if even is not None else odd
        else:
            out[k] = plus([x for x in (even, odd) if x is not None])
    return out


def accurate_dot(values, matrix_ref):
    high = values.astype(jnp.bfloat16)
    low = (values - high.astype(jnp.float32)).astype(jnp.bfloat16)
    dot = partial(jnp.dot, preferred_element_type=jnp.float32)
    return dot(high, matrix_ref[0]) + dot(low, matrix_ref[0]) + dot(high, matrix_ref[1])


def spectrum(chunks, turns_ref, forward_ref):
    blocks = len(chunks)
    half = blocks // 2
    folds = [chunks[0]] + [chunks[a] + chunks[blocks - a] for a in range(1, half)] + [chunks[half]]
    skews = [None] + [chunks[a] - chunks[blocks - a] for a in range(1, half)] + [None]
    reals = cosine_sums(folds, blocks)
    imags = sine_sums(skews, blocks)
    parts = []
    for k in range(half + 1):
        cos, sin = turns_ref[0, k : k + 1, :], turns_ref[1, k : k + 1, :]
        if k == 0:
            re, im = reals[0], jnp.zeros_like(reals[0])
        elif imags[k] is None:
            re, im = reals[k] * cos, -(reals[k] * sin)
        else:
            re, im = reals[k] * cos - imags[k] * sin, -(imags[k] * cos) - reals[k] * sin
        parts.append(jnp.concatenate((re, im), axis=1))
    return accurate_dot(jnp.concatenate(parts, axis=0), forward_ref)


def columns(spec, turns_ref, inverse_ref, blocks):
    half = blocks // 2
    back = accurate_dot(spec, inverse_ref)
    reals, imags = [], []
    for k in range(half + 1):
        rows = slice(k * SUB, (k + 1) * SUB)
        re, im = back[rows, :LANES], back[rows, LANES:]
        cos, sin = turns_ref[0, k : k + 1, :], turns_ref[1, k : k + 1, :]
        if k == 0:
            reals.append(re)
            imags.append(None)
        else:
            reals.append(re * cos - im * sin)
            imags.append(im * cos + re * sin if k < half else None)
    even = cosine_sums(reals, blocks)
    odd = sine_sums(imags, blocks)
    out = [None] * blocks
    out[0], out[half] = even[0], even[half]
    for a in range(1, half):
        out[a] = even[a] - odd[a]
        out[blocks - a] = even[a] + odd[a]
    return out


def contrast_kernel(proj_ref, flat_ref, own_ref, first_ref, last_ref):
    own = 1.0 - proj_ref[0].astype(jnp.float32) / flat_ref[...]
    own_ref[...] = own
    first_ref[...] = own[:HALO].astype(first_ref.dtype)
    last_ref[...] = own[SUB - HALO :].astype(last_ref.dtype)


def lanes_of(ref, block):
    return ref[:, block * LANES : (block + 1) * LANES]


def own_kernel(own_ref, turns_ref, forward_ref, gains_ref, out_ref):
    blocks = own_ref.shape[1] // LANES
    spec = spectrum([lanes_of(own_ref, a) for a in range(blocks)], turns_ref, forward_ref)
    row = lax.broadcasted_iota(jnp.int32, (SUB, LANES), 0)
    for k in range(blocks // 2 + 1):
        rows = slice(k * SUB, (k + 1) * SUB)
        for side in (slice(0, LANES), slice(LANES, 2 * LANES)):
            here = spec[rows, side]
            moved = [here] + [pltpu.roll(here, s, axis=0) for s in range(1, SUB)]
            total = here * gains_ref[0, k : k + 1, :]
            for d in range(1, SUB):
                pair = jnp.where(row >= d, moved[d], 0.0) + jnp.where(row < SUB - d, moved[SUB - d], 0.0)
                total += pair * gains_ref[d, k : k + 1, :]
            out_ref[rows, side] = total


def halo_terms(here, row):
    moved = [here] + [pltpu.roll(here, s, axis=0) for s in range(1, SUB)]
    terms = {HALO: moved[0], 2 * HALO: moved[HALO]}
    for d in range(1, HALO):
        s, w = HALO - d, HALO + d
        near_s, near_w = row >= s + HALO, row < w - HALO
        terms[d] = jnp.where(near_s, moved[s], jnp.where(near_w, moved[w], 0.0))
        terms[HALO + s] = jnp.where(near_s, 0.0, moved[s]) + jnp.where(near_w, 0.0, moved[w])
    return terms


def tile_kernel(
    own_ref, above_ref, below_ref, starts_hbm, turns_ref, forward_ref, inverse_ref, gains_ref, out_ref,
    sheet, starts, sem
):
    copy = pltpu.make_async_copy(starts_hbm, starts, sem)
    copy.start()
    blocks = above_ref.shape[1] // LANES
    halo = [
        jnp.concatenate((lanes_of(above_ref, a), lanes_of(below_ref, a)), axis=0).astype(jnp.float32)
        for a in range(blocks)
    ]
    spec = spectrum(halo, turns_ref, forward_ref)
    row = lax.broadcasted_iota(jnp.int32, (SUB, LANES), 0)
    lane = lax.broadcasted_iota(jnp.int32, (SUB, LANES), 1)
    parts = []
    for k in range(blocks // 2 + 1):
        rows = slice(k * SUB, (k + 1) * SUB)
        both = []
        for side in (slice(0, LANES), slice(LANES, 2 * LANES)):
            total = own_ref[rows, side]
            for d, term in halo_terms(spec[rows, side], row).items():
                total += term * gains_ref[d, k : k + 1, :]
            both.append(total)
        parts.append(jnp.concatenate(both, axis=1))
    filtered = columns(jnp.concatenate(parts, axis=0), turns_ref, inverse_ref, blocks)
    for a in range(blocks):
        sheet[:, a * LANES : (a + 1) * LANES] = filtered[a]
    copy.wait()
    regions = starts.shape[1]
    cut = out_ref.shape[0] * LANES // (regions * SUB)
    per = LANES // cut
    keep = lane // cut == row % per
    packed = []
    for group in range(regions // per):
        gathered = None
        for q in range(per):
            start = starts[0, group * per + q]
            block = start // LANES
            offset = start - block * LANES
            after = jnp.minimum(block + 1, blocks - 1)
            here = sheet[:, pl.ds(pl.multiple_of(block * LANES, LANES), LANES)]
            then = sheet[:, pl.ds(pl.multiple_of(after * LANES, LANES), LANES)]
            window = jnp.where(lane >= offset, here, then)
            window = pltpu.roll(window, lax.rem(LANES + q * cut - offset, LANES), axis=1)
            gathered = window if q == 0 else jnp.where(lane // cut == q, window, gathered)
        for shift in range(per):
            moved = gathered if shift == 0 else pltpu.roll(gathered, shift * cut, axis=1)
            packed.append(jnp.where(keep, moved, 0.0).astype(jnp.bfloat16))
    lines = out_ref.shape[0]
    want = lax.broadcasted_iota(jnp.int32, (lines, regions * SUB), 0)
    have = lax.broadcasted_iota(jnp.int32, (lines, regions * SUB), 1)
    have_row, have_shift, have_group = have % SUB, have // SUB % per, have // (SUB * per)
    have_region = have_group * per + (have_row % per + per - have_shift) % per
    pick = jnp.where(have_region * (SUB // per) + have_row // per == want, 1.0, 0.0).astype(jnp.bfloat16)
    out = jnp.dot(pick, jnp.concatenate(packed, axis=0), preferred_element_type=jnp.float32)
    out_ref[...] = out.astype(jnp.bfloat16)


def make_contrast(projections, flats):
    shape = flats.shape
    edge = jax.ShapeDtypeStruct((HALO, shape[1]), halo_type)
    return pl.pallas_call(
        contrast_kernel,
        out_shape=(jax.ShapeDtypeStruct(shape, jnp.float32), edge, edge),
        in_specs=[VMEM] * 2,
        out_specs=(VMEM,) * 3,
        name="contrast",
    )(projections, flats)


def make_own(own, turns, forward, gains):
    lines = turns.shape[1] * SUB
    return pl.pallas_call(
        own_kernel,
        out_shape=jax.ShapeDtypeStruct((lines, 2 * LANES), jnp.float32),
        in_specs=[VMEM] * 4,
        out_specs=VMEM,
        name="own_rows",
    )(own, turns, forward, gains)


def make_tile(own_spec, above, below, starts, turns, forward, inverse, gains, cut):
    regions = starts.shape[1]
    return pl.pallas_call(
        tile_kernel,
        out_shape=jax.ShapeDtypeStruct((regions * SUB * cut // LANES, LANES), jnp.bfloat16),
        in_specs=[VMEM] * 3 + [ANY] + [VMEM] * 4,
        out_specs=VMEM,
        scratch_shapes=[
            pltpu.VMEM((SUB, above.shape[1]), jnp.float32),
            pltpu.SMEM(starts.shape, jnp.int32),
            pltpu.SemaphoreType.DMA,
        ],
        name="tile",
    )(own_spec, above, below, starts, turns, forward, inverse, gains)


def body(projections, flats, block_start, bp_weights):
    angles_dev, rows_dev, width = projections.shape
    assert angles_dev == 1 and rows_dev == SUB and width % (2 * LANES) == 0
    cut = bp_weights.shape[1]
    rows = lax.axis_size("row")
    up = [(i, i + 1) for i in range(rows - 1)]
    down = [(j, i) for i, j in up]
    turns, forward, inverse, gains = (jnp.asarray(t) for t in tables(width, rows_dev + 2 * HALO))
    my_starts = lax.dynamic_slice_in_dim(block_start, lax.axis_index("ang"), 1, 0)
    own, first, last = make_contrast(projections, flats)
    above = lax.ppermute(last, "row", up)
    below = lax.ppermute(first, "row", down)
    own_spec = make_own(own, turns, forward, gains)
    outgoing = make_tile(own_spec, above, below, my_starts, turns, forward, inverse, gains, cut)
    incoming = lax.all_to_all(outgoing, "ang", split_axis=0, concat_axis=0, tiled=True)
    blocks = incoming.reshape(bp_weights.shape[0], rows_dev, cut)
    return lax.dot_general(
        blocks, bp_weights, (((0, 2), (0, 1)), ((), ())), preferred_element_type=jnp.float32
    )


def solution(mesh):
    placed = (P(("scan", "ang"), "row", None), P(("scan", "row"), None), P(), P(None, None, "ang"))
    return jax.shard_map(
        body, mesh=mesh, in_specs=placed, out_specs=P(("scan", "row"), "ang"), check_vma=False
    )
```

time: 80.6 us -> 74.9 us (0.929)
  the two profiles are of different devices: /device:TPU:70 before, /device:TPU:86 now
where the time goes in v1:
time: 74.9 us; the launch traced here: 74.6 us
  blocking collectives  56.3 us (75%)
  starting transfers between devices  6.71 us (9%)
  Pallas kernels  6.64 us (9%)
  waiting for transfers between devices  2.2 us (3%)
  local copies, waits for them, and re-layouts  1.91 us (3%)
  matrix products  0.85 us (1%)
    all_to_all x1, blocking collectives, body(): lax.all_to_all(outgoing, 'ang', split_axis=0, concat_axis=0, tiled=True)  56.3 us
    ppermute x1, starting transfers between devices, body(): above = lax.ppermute(last, 'row', up)  4.76 us
    pallas_call x1, Pallas kernels, make_tile(): pl.pallas_call(tile_kernel, out_shape=jax.ShapeDtypeStruct((regions * SUB...  3.02 us
    ppermute x1, waiting for transfers between devices, body(): below = lax.ppermute(first, 'row', down)  2.2 us
    pallas_call x1, Pallas kernels, make_own(): pl.pallas_call(own_kernel, out_shape=jax.ShapeDtypeStruct((lines, 2 * LAN...  1.97 us
    ppermute x1, starting transfers between devices, body(): below = lax.ppermute(first, 'row', down)  1.95 us
    pallas_call x1, Pallas kernels, make_contrast(): pl.pallas_call(contrast_kernel, out_shape=(jax.ShapeDtypeStruct(shape, jn...  1.65 us
  transfers between devices with their start and end apart: 2, of which 1 were waited for; matrix products, arithmetic and copies ran while one was open for 2% of the time, Pallas kernels for 3%

profile of v1, /device:TPU:86, one launch (start us, length us, event | category | flops | bytes accessed | tf_op | source)
XLA Modules:
  0.0 74.6 jit_solution(1949665372419699413)
XLA Ops:
  0.0 0.0 copy-start
  0.0 1.6 %contrast.1 = (f32[8,2560]{1,0:T(8,128)}, f32[4,2560]{1,0:T(4,128)}, f32[4,2560]{1,0:T(4,128)}) custom-call(bf16[1,8,2560]{2,1,0:T(8,128)(2,1)} %proj_ref.1, f32[8,2560]{1,0:T(8,128)} %flat_ref.1), custom_call_target="tpu_custom_call" | custom-call | tf_op jit(solution)/shard_map/contrast/pallas_call | solution.py:244
  1.7 4.8 %collective-permute-start = (f32[4,2560]{1,0:T(4,128)}, f32[4,2560]{1,0:T(4,128)S(1)}, u32[]{:S(2)}, u32[]{:S(2)}) collective-permute-start(f32[4,2560]{1,0:T(4,128)} %get-tuple-element.9), channel_id=1, source_target_pairs={{0,1},{1,2},{2,3},{3,4},{4,5},{5,6},{6,7},{8,9},{9,10},{10,11},{11... | collective-permute-start | bytes 122888 | tf_op jit(solution)/shard_map/ppermute | solution.py:290
  6.4 2.0 %collective-permute-start.1 = (f32[4,2560]{1,0:T(4,128)}, f32[4,2560]{1,0:T(4,128)S(1)}, u32[]{:S(2)}, u32[]{:S(2)}) collective-permute-start(f32[4,2560]{1,0:T(4,128)} %get-tuple-element.10), channel_id=1, source_target_pairs={{1,0},{2,1},{3,2},{4,3},{5,4},{6,5},{7,6},{9,8},{10,9},{11,10},{12... | collective-permute-start | bytes 122888 | tf_op jit(solution)/shard_map/ppermute | solution.py:291
  8.4 1.2 %constant_dynamic-slice_fusion.starts_hbm = s32[1,32]{1,0:T(1,128)} fusion(s32[32,32]{1,0:T(8,128)} %param.10, s32[]{:T(128)S(6)} %select_n.3), kind=kLoop, calls=%fused_computation.1 | loop fusion | bytes 260 | tf_op jit(solution)/shard_map/dynamic_slice | solution.py:288
  9.6 2.0 %own_rows.1.own_ref = f32[88,256]{1,0:T(8,128)} custom-call(f32[8,2560]{1,0:T(8,128)} %get-tuple-element.8.own_ref, f32[2,11,128]{2,1,0:T(8,128)} %constant.18.clone.turns_ref, bf16[2,256,256]{2,1,0:T(8,128)(2,1)} %constant.19.clone.forward_ref, f32[9,11,128]{2,1,0:T(8,128)} %constant.21.clone.gains_ref), custom_call_target="tpu_custom_call" | custom-call | tf_op jit(solution)/shard_map/own_rows/pallas_call | solution.py:255
  11.6 0.0 collective-permute-done.above_ref
  11.6 0.0 copy-start.1
  11.6 2.2 %collective-permute-done.1.below_ref = f32[4,2560]{1,0:T(4,128)S(1)} collective-permute-done((f32[4,2560]{1,0:T(4,128)}, f32[4,2560]{1,0:T(4,128)S(1)}, u32[]{:S(2)}, u32[]{:S(2)}) %collective-permute-start.1) | collective-permute-done | bytes 40992 | tf_op jit(solution)/shard_map/ppermute | solution.py:291
  13.8 0.0 copy-done.1
  13.8 0.0 copy-start.2
  13.8 0.6 copy-done.2
  14.4 3.0 %tile.1 = bf16[64,128]{1,0:T(8,128)(2,1)} custom-call(f32[88,256]{1,0:T(8,128)} %own_rows.1.own_ref, f32[4,2560]{1,0:T(4,128)} %copy-done.1, f32[4,2560]{1,0:T(4,128)} %copy-done.2, s32[1,32]{1,0:T(1,128)} %constant_dynamic-slice_fusion.starts_hbm, f32[2,11,128]{2,1,0:T(8,128)} %constant.18.clone.turns_ref, bf16[2,256,256]{2,1,0:T(8,128)(2,1)} %constant.19.clone.forward_ref, ...), custom_call_target="tpu_custom_call" | custom-call | tf_op jit(solution)/shard_map/tile/pallas_call | solution.py:266
  17.4 56.3 %all_to_all.9 = bf16[32,2,128]{2,1,0:T(2,128)(2,1)S(1)} all-to-all(bf16[32,2,128]{2,1,0:T(2,128)(2,1)} %bitcast.5), channel_id=1, replica_groups=mesh['scan'=2,'ang'=32,'row'=8] {'ang'}, dimensions={0} | all-to-all | bytes 32768 | tf_op jit(solution)/shard_map/all_to_all | solution.py:294
  73.7 0.1 reshape.6
  73.8 0.0 copy-done
  73.8 0.8 %convolution_bitcast_fusion = f32[8,256]{1,0:T(8,128)} fusion(bf16[32,8,32]{2,1,0:T(8,128)(2,1)S(1)} %reshape.6, bf16[32,32,256]{2,1,0:T(8,128)(2,1)S(1)} %copy-done), kind=kOutput, calls=%fused_computation | convolution fusion | flops 4194304 | bytes 548864 | tf_op jit(solution)/shard_map/dot_general | solution.py:296
Async XLA Ops:
  0.0 73.8 %copy-start = (bf16[32,32,256]{2,1,0:T(8,128)(2,1)S(1)}, bf16[32,32,256]{2,1,0:T(8,128)(2,1)}, u32[]{:S(2)}) copy-start(bf16[32,32,256]{2,1,0:T(8,128)(2,1)} %param.11) | copy-start | bytes 1572868
  1.7 9.9 %collective-permute-start = (f32[4,2560]{1,0:T(4,128)}, f32[4,2560]{1,0:T(4,128)S(1)}, u32[]{:S(2)}, u32[]{:S(2)}) collective-permute-start(f32[4,2560]{1,0:T(4,128)} %get-tuple-element.9), channel_id=1, source_target_pairs={{0,1},{1,2},{2,3},{3,4},{4,5},{5,6},{6,7},{8,9},{9,10},{10,11},{11... | collective-permute-start | bytes 122888 | tf_op jit(solution)/shard_map/ppermute | solution.py:290
  6.4 7.3 %collective-permute-start.1 = (f32[4,2560]{1,0:T(4,128)}, f32[4,2560]{1,0:T(4,128)S(1)}, u32[]{:S(2)}, u32[]{:S(2)}) collective-permute-start(f32[4,2560]{1,0:T(4,128)} %get-tuple-element.10), channel_id=1, source_target_pairs={{1,0},{2,1},{3,2},{4,3},{5,4},{6,5},{7,6},{9,8},{10,9},{11,10},{12... | collective-permute-start | bytes 122888 | tf_op jit(solution)/shard_map/ppermute | solution.py:291
  11.6 2.2 %copy-start.1 = (f32[4,2560]{1,0:T(4,128)}, f32[4,2560]{1,0:T(4,128)S(1)}, u32[]{:S(2)}) copy-start(f32[4,2560]{1,0:T(4,128)S(1)} %collective-permute-done.above_ref) | copy-start | bytes 122884
  13.8 0.6 copy-start.2

commit v2 on v1

--- a/solution.py
+++ b/solution.py
@@ -17,6 +17,8 @@
 halo_type = jnp.float32
 VMEM = pl.BlockSpec(memory_space=pltpu.VMEM)
 ANY = pl.BlockSpec(memory_space=pl.ANY)
+HBM = pl.BlockSpec(memory_space=pltpu.HBM)
+PARAMS = pltpu.CompilerParams(vmem_limit_bytes=8 * 2**20)
 
 
 def tables(width, tile_rows):
@@ -142,8 +144,16 @@
     return out
 
 
-def contrast_kernel(proj_ref, flat_ref, own_ref, first_ref, last_ref):
-    own = 1.0 - proj_ref[0].astype(jnp.float32) / flat_ref[...]
+def contrast_kernel(proj_hbm, flat_hbm, own_ref, first_ref, last_ref, proj, flat, sems):
+    copies = [
+        pltpu.make_async_copy(proj_hbm, proj, sems.at[0]),
+        pltpu.make_async_copy(flat_hbm, flat, sems.at[1]),
+    ]
+    for copy in copies:
+        copy.start()
+    for copy in copies:
+        copy.wait()
+    own = 1.0 - proj[0].astype(jnp.float32) / flat[...]
     own_ref[...] = own
     first_ref[...] = own[:HALO].astype(first_ref.dtype)
     last_ref[...] = own[SUB - HALO :].astype(last_ref.dtype)
@@ -208,6 +218,7 @@
     for a in range(blocks):
         sheet[:, a * LANES : (a + 1) * LANES] = filtered[a]
     copy.wait()
+    mine = lax.axis_index("ang")
     regions = starts.shape[1]
     cut = out_ref.shape[0] * LANES // (regions * SUB)
     per = LANES // cut
@@ -216,7 +227,7 @@
     for group in range(regions // per):
         gathered = None
         for q in range(per):
-            start = starts[0, group * per + q]
+            start = starts[mine, group * per + q]
             block = start // LANES
             offset = start - block * LANES
             after = jnp.minimum(block + 1, blocks - 1)
@@ -244,8 +255,14 @@
     return pl.pallas_call(
         contrast_kernel,
         out_shape=(jax.ShapeDtypeStruct(shape, jnp.float32), edge, edge),
-        in_specs=[VMEM] * 2,
+        in_specs=[HBM] * 2,
         out_specs=(VMEM,) * 3,
+        scratch_shapes=[
+            pltpu.VMEM(projections.shape, projections.dtype),
+            pltpu.VMEM(flats.shape, flats.dtype),
+            pltpu.SemaphoreType.DMA((2,)),
+        ],
+        compiler_params=PARAMS,
         name="contrast",
     )(projections, flats)
 
@@ -257,6 +274,7 @@
         out_shape=jax.ShapeDtypeStruct((lines, 2 * LANES), jnp.float32),
         in_specs=[VMEM] * 4,
         out_specs=VMEM,
+        compiler_params=PARAMS,
         name="own_rows",
     )(own, turns, forward, gains)
 
@@ -273,6 +291,7 @@
             pltpu.SMEM(starts.shape, jnp.int32),
             pltpu.SemaphoreType.DMA,
         ],
+        compiler_params=PARAMS,
         name="tile",
     )(own_spec, above, below, starts, turns, forward, inverse, gains)
 
@@ -285,12 +304,12 @@
     up = [(i, i + 1) for i in range(rows - 1)]
     down = [(j, i) for i, j in up]
     turns, forward, inverse, gains = (jnp.asarray(t) for t in tables(width, rows_dev + 2 * HALO))
-    my_starts = lax.dynamic_slice_in_dim(block_start, lax.axis_index("ang"), 1, 0)
-    own, first, last = make_contrast(projections, flats)
+    in_hbm = partial(pltpu.with_memory_space_constraint, memory_space=pltpu.HBM)
+    own, first, last = make_contrast(in_hbm(projections), in_hbm(flats))
     above = lax.ppermute(last, "row", up)
     below = lax.ppermute(first, "row", down)
     own_spec = make_own(own, turns, forward, gains)
-    outgoing = make_tile(own_spec, above, below, my_starts, turns, forward, inverse, gains, cut)
+    outgoing = make_tile(own_spec, above, below, block_start, turns, forward, inverse, gains, cut)
     incoming = lax.all_to_all(outgoing, "ang", split_axis=0, concat_axis=0, tiled=True)
     blocks = incoming.reshape(bp_weights.shape[0], rows_dev, cut)
     return lax.dot_general(

time: 74.9 us -> 71.6 us (0.956)
  Pallas kernels: 6.64 us -> 2.76 us
  waiting for transfers between devices: 2.2 us -> 3.87 us
  local copies, waits for them, and re-layouts: 1.91 us -> 1.06 us
    ppermute x1, waiting for transfers between devices: 2.2 us -> 3.86 us  [body(): below = lax.ppermute(first, 'row', down)]
    pallas_call x1, Pallas kernels: 1.97 us -> 0.32 us  [make_own(): pl.pallas_call(own_kernel, out_shape=jax.ShapeDtypeStruct((lines, 2 * LAN...]
    pallas_call x1, Pallas kernels: 3.02 us -> 1.43 us  [make_tile(): pl.pallas_call(tile_kernel, out_shape=jax.ShapeDtypeStruct((regions * SUB...]
    dynamic_slice x1 -> x0, local copies, waits for them, and re-layouts: 1.21 us -> none  [body(): lax.dynamic_slice_in_dim(block_start, lax.axis_index('ang'), 1, 0)]
  transfers between devices with their start and end apart: 2 -> 2, of which waited for: 1 -> 1; matrix products, arithmetic and copies ran while one was open for 2% -> 0% of each run, Pallas kernels for 3% -> 0%
where the time goes in v2:
time: 71.6 us; the launch traced here: 71.4 us
  blocking collectives  56.1 us (78%)
  starting transfers between devices  6.73 us (9%)
  waiting for transfers between devices  3.87 us (5%)
  Pallas kernels  2.76 us (4%)
  local copies, waits for them, and re-layouts  1.06 us (1%)
  matrix products  0.85 us (1%)
    all_to_all x1, blocking collectives, body(): lax.all_to_all(outgoing, 'ang', split_axis=0, concat_axis=0, tiled=True)  56.1 us
    ppermute x1, starting transfers between devices, body(): above = lax.ppermute(last, 'row', up)  4.78 us
    ppermute x1, waiting for transfers between devices, body(): below = lax.ppermute(first, 'row', down)  3.86 us
    ppermute x1, starting transfers between devices, body(): below = lax.ppermute(first, 'row', down)  1.95 us
  transfers between devices with their start and end apart: 2, of which 1 were waited for; matrix products, arithmetic and copies ran while one was open for 0% of the time, Pallas kernels for 0%

profile of v2, /device:TPU:86, one launch (start us, length us, event | category | flops | bytes accessed | tf_op | source)
XLA Modules:
  0.0 71.4 jit_solution(7387549295530732454)
XLA Ops:
  0.0 0.0 copy-start
  0.0 0.0 copy-start.3
  0.0 0.0 copy-start.5
  0.0 0.0 copy-start.6
  0.0 1.0 %contrast.1 = (f32[8,2560]{1,0:T(8,128)S(1)}, f32[4,2560]{1,0:T(4,128)S(1)}, f32[4,2560]{1,0:T(4,128)S(1)}) custom-call(bf16[1,8,2560]{2,1,0:T(8,128)(2,1)} %proj_hbm.1, f32[8,2560]{1,0:T(8,128)} %flat_hbm.1), custom_call_target="tpu_custom_call" | custom-call | tf_op jit(solution)/shard_map/contrast/pallas_call | solution.py:255
  1.0 4.8 %collective-permute-start = (f32[4,2560]{1,0:T(4,128)S(1)}, f32[4,2560]{1,0:T(4,128)S(1)}, u32[]{:S(2)}, u32[]{:S(2)}) collective-permute-start(f32[4,2560]{1,0:T(4,128)S(1)} %get-tuple-element.9), channel_id=1, source_target_pairs={{0,1},{1,2},{2,3},{3,4},{4,5},{5,6},{6,7},{8,9},{9,10},{10,11},{11... | collective-permute-start | bytes 122888 | tf_op jit(solution)/shard_map/ppermute | solution.py:309
  5.8 2.0 %collective-permute-start.1 = (f32[4,2560]{1,0:T(4,128)S(1)}, f32[4,2560]{1,0:T(4,128)S(1)}, u32[]{:S(2)}, u32[]{:S(2)}) collective-permute-start(f32[4,2560]{1,0:T(4,128)S(1)} %get-tuple-element.10), channel_id=1, source_target_pairs={{1,0},{2,1},{3,2},{4,3},{5,4},{6,5},{7,6},{9,8},{10,9},{11,10},{12... | collective-permute-start | bytes 122888 | tf_op jit(solution)/shard_map/ppermute | solution.py:310
  7.8 0.0 copy-done.3
  7.8 0.0 copy-done.5
  7.8 0.0 copy-start.1
  7.8 0.9 %copy-done.1 = bf16[2,256,256]{2,1,0:T(8,128)(2,1)S(1)} copy-done((bf16[2,256,256]{2,1,0:T(8,128)(2,1)S(1)}, bf16[2,256,256]{2,1,0:T(8,128)(2,1)}, u32[]{:S(2)}) %copy-start.1) | copy-done | bytes 262168
  8.8 0.0 copy-start.2
  8.8 0.0 copy-start.4
  8.8 0.3 own_rows.1.own_ref
  9.1 0.0 collective-permute-done.above_ref
  9.1 3.9 %collective-permute-done.1.below_ref = f32[4,2560]{1,0:T(4,128)S(1)} collective-permute-done((f32[4,2560]{1,0:T(4,128)S(1)}, f32[4,2560]{1,0:T(4,128)S(1)}, u32[]{:S(2)}, u32[]{:S(2)}) %collective-permute-start.1) | collective-permute-done | bytes 40992 | tf_op jit(solution)/shard_map/ppermute | solution.py:310
  13.0 0.0 copy-done.6
  13.0 0.0 copy-done.2
  13.0 0.0 copy-done.4
  13.0 1.4 %tile.1 = bf16[64,128]{1,0:T(8,128)(2,1)S(1)} custom-call(f32[88,256]{1,0:T(8,128)S(1)} %own_rows.1.own_ref, f32[4,2560]{1,0:T(4,128)S(1)} %collective-permute-done.above_ref, f32[4,2560]{1,0:T(4,128)S(1)} %collective-permute-done.1.below_ref, s32[32,32]{1,0:T(8,128)S(1)} %copy-done.6, f32[2,11,128]{2,1,0:T(8,128)S(1)} %copy-done.5, ...), custom_call_target="tpu_custom_call" | custom-call | tf_op jit(solution)/shard_map/tile/pallas_call | solution.py:284
  14.4 56.1 %all_to_all.9 = bf16[32,2,128]{2,1,0:T(2,128)(2,1)S(1)} all-to-all(bf16[32,2,128]{2,1,0:T(2,128)(2,1)S(1)} %bitcast.5), channel_id=1, replica_groups=mesh['scan'=2,'ang'=32,'row'=8] {'ang'}, dimensions={0} | all-to-all | bytes 32768 | tf_op jit(solution)/shard_map/all_to_all | solution.py:313
  70.5 0.1 reshape.6
  70.6 0.0 copy-done
  70.6 0.8 %convolution_bitcast_fusion = f32[8,256]{1,0:T(8,128)} fusion(bf16[32,8,32]{2,1,0:T(8,128)(2,1)S(1)} %reshape.6, bf16[32,32,256]{2,1,0:T(8,128)(2,1)S(1)} %copy-done), kind=kOutput, calls=%fused_computation | convolution fusion | flops 4194304 | bytes 548864 | tf_op jit(solution)/shard_map/dot_general | solution.py:315
Async XLA Ops:
  0.0 70.6 %copy-start = (bf16[32,32,256]{2,1,0:T(8,128)(2,1)S(1)}, bf16[32,32,256]{2,1,0:T(8,128)(2,1)}, u32[]{:S(2)}) copy-start(bf16[32,32,256]{2,1,0:T(8,128)(2,1)} %param.11) | copy-start | bytes 1572868
  0.0 7.8 %copy-start.3 = (f32[9,11,128]{2,1,0:T(8,128)S(1)}, f32[9,11,128]{2,1,0:T(8,128)}, u32[]{:S(2)}) copy-start(f32[9,11,128]{2,1,0:T(8,128)} %constant.11.clone.gains_ref) | copy-start | bytes 152068
  0.0 7.8 %copy-start.5 = (f32[2,11,128]{2,1,0:T(8,128)S(1)}, f32[2,11,128]{2,1,0:T(8,128)}, u32[]{:S(2)}) copy-start(f32[2,11,128]{2,1,0:T(8,128)} %constant.8.clone.turns_ref) | copy-start | bytes 33796
  0.0 12.9 %copy-start.6 = (s32[32,32]{1,0:T(8,128)S(1)}, s32[32,32]{1,0:T(8,128)}, u32[]{:S(2)}) copy-start(s32[32,32]{1,0:T(8,128)} %starts_hbm.1) | copy-start | bytes 12292
  1.0 8.1 %collective-permute-start = (f32[4,2560]{1,0:T(4,128)S(1)}, f32[4,2560]{1,0:T(4,128)S(1)}, u32[]{:S(2)}, u32[]{:S(2)}) collective-permute-start(f32[4,2560]{1,0:T(4,128)S(1)} %get-tuple-element.9), channel_id=1, source_target_pairs={{0,1},{1,2},{2,3},{3,4},{4,5},{5,6},{6,7},{8,9},{9,10},{10,11},{11... | collective-permute-start | bytes 122888 | tf_op jit(solution)/shard_map/ppermute | solution.py:309
  5.8 7.1 %collective-permute-start.1 = (f32[4,2560]{1,0:T(4,128)S(1)}, f32[4,2560]{1,0:T(4,128)S(1)}, u32[]{:S(2)}, u32[]{:S(2)}) collective-permute-start(f32[4,2560]{1,0:T(4,128)S(1)} %get-tuple-element.10), channel_id=1, source_target_pairs={{1,0},{2,1},{3,2},{4,3},{5,4},{6,5},{7,6},{9,8},{10,9},{11,10},{12... | collective-permute-start | bytes 122888 | tf_op jit(solution)/shard_map/ppermute | solution.py:310
  7.8 1.0 %copy-start.1 = (bf16[2,256,256]{2,1,0:T(8,128)(2,1)S(1)}, bf16[2,256,256]{2,1,0:T(8,128)(2,1)}, u32[]{:S(2)}) copy-start(bf16[2,256,256]{2,1,0:T(8,128)(2,1)} %constant.9.clone.forward_ref) | copy-start | bytes 786436
  8.8 4.2 %copy-start.2 = (bf16[2,256,256]{2,1,0:T(8,128)(2,1)S(1)}, bf16[2,256,256]{2,1,0:T(8,128)(2,1)}, u32[]{:S(2)}) copy-start(bf16[2,256,256]{2,1,0:T(8,128)(2,1)} %constant.9.clone.forward_ref) | copy-start | bytes 786436
  8.8 4.2 %copy-start.4 = (bf16[2,256,256]{2,1,0:T(8,128)(2,1)S(1)}, bf16[2,256,256]{2,1,0:T(8,128)(2,1)}, u32[]{:S(2)}) copy-start(bf16[2,256,256]{2,1,0:T(8,128)(2,1)} %constant.10.clone.inverse_ref) | copy-start | bytes 786436

commit v3 on v2

--- a/solution.py
+++ b/solution.py
@@ -191,7 +191,7 @@
 
 
 def tile_kernel(
-    own_ref, above_ref, below_ref, starts_hbm, turns_ref, forward_ref, inverse_ref, gains_ref, out_ref,
+    own_ref, below_ref, above_ref, starts_hbm, turns_ref, forward_ref, inverse_ref, gains_ref, out_ref,
     sheet, starts, sem
 ):
     copy = pltpu.make_async_copy(starts_hbm, starts, sem)
@@ -279,7 +279,7 @@
     )(own, turns, forward, gains)
 
 
-def make_tile(own_spec, above, below, starts, turns, forward, inverse, gains, cut):
+def make_tile(own_spec, below, above, starts, turns, forward, inverse, gains, cut):
     regions = starts.shape[1]
     return pl.pallas_call(
         tile_kernel,
@@ -293,7 +293,7 @@
         ],
         compiler_params=PARAMS,
         name="tile",
-    )(own_spec, above, below, starts, turns, forward, inverse, gains)
+    )(own_spec, below, above, starts, turns, forward, inverse, gains)
 
 
 def body(projections, flats, block_start, bp_weights):
@@ -306,10 +306,10 @@
     turns, forward, inverse, gains = (jnp.asarray(t) for t in tables(width, rows_dev + 2 * HALO))
     in_hbm = partial(pltpu.with_memory_space_constraint, memory_space=pltpu.HBM)
     own, first, last = make_contrast(in_hbm(projections), in_hbm(flats))
+    below = lax.ppermute(first, "row", down)
     above = lax.ppermute(last, "row", up)
-    below = lax.ppermute(first, "row", down)
     own_spec = make_own(own, turns, forward, gains)
-    outgoing = make_tile(own_spec, above, below, block_start, turns, forward, inverse, gains, cut)
+    outgoing = make_tile(own_spec, below, above, block_start, turns, forward, inverse, gains, cut)
     incoming = lax.all_to_all(outgoing, "ang", split_axis=0, concat_axis=0, tiled=True)
     blocks = incoming.reshape(bp_weights.shape[0], rows_dev, cut)
     return lax.dot_general(

time: 71.6 us -> 69.2 us (0.966)
  the two profiles are of different devices: /device:TPU:86 before, /device:TPU:88 now
where the time goes in v3:
time: 69.2 us; the launch traced here: 69 us
  blocking collectives  56.1 us (81%)
  starting transfers between devices  5.9 us (9%)
  Pallas kernels  2.76 us (4%)
  waiting for transfers between devices  2.25 us (3%)
  local copies, waits for them, and re-layouts  1.06 us (2%)
  matrix products  0.85 us (1%)
    all_to_all x1, blocking collectives, body(): lax.all_to_all(outgoing, 'ang', split_axis=0, concat_axis=0, tiled=True)  56.1 us
    ppermute x1, starting transfers between devices, body(): above = lax.ppermute(last, 'row', up)  3.57 us
    ppermute x1, starting transfers between devices, body(): below = lax.ppermute(first, 'row', down)  2.34 us
    ppermute x1, waiting for transfers between devices, body(): above = lax.ppermute(last, 'row', up)  2.25 us
    pallas_call x1, Pallas kernels, make_tile(): pl.pallas_call(tile_kernel, out_shape=jax.ShapeDtypeStruct((regions * SUB...  1.43 us
  transfers between devices with their start and end apart: 2, of which 1 were waited for; matrix products, arithmetic and copies ran while one was open for 0% of the time, Pallas kernels for 0%

profile of v3, /device:TPU:88, one launch (start us, length us, event | category | flops | bytes accessed | tf_op | source)
XLA Modules:
  0.0 69.0 jit_solution(766592578597193139)
XLA Ops:
  0.0 0.0 copy-start
  0.0 0.0 copy-start.3
  0.0 0.0 copy-start.5
  0.0 0.0 copy-start.6
  0.0 1.0 %contrast.1 = (f32[8,2560]{1,0:T(8,128)S(1)}, f32[4,2560]{1,0:T(4,128)S(1)}, f32[4,2560]{1,0:T(4,128)S(1)}) custom-call(bf16[1,8,2560]{2,1,0:T(8,128)(2,1)} %proj_hbm.1, f32[8,2560]{1,0:T(8,128)} %flat_hbm.1), custom_call_target="tpu_custom_call" | custom-call | tf_op jit(solution)/shard_map/contrast/pallas_call | solution.py:255
  1.0 2.3 %collective-permute-start = (f32[4,2560]{1,0:T(4,128)S(1)}, f32[4,2560]{1,0:T(4,128)S(1)}, u32[]{:S(2)}, u32[]{:S(2)}) collective-permute-start(f32[4,2560]{1,0:T(4,128)S(1)} %get-tuple-element.9), channel_id=1, source_target_pairs={{1,0},{2,1},{3,2},{4,3},{5,4},{6,5},{7,6},{9,8},{10,9},{11,10},{12... | collective-permute-start | bytes 122888 | tf_op jit(solution)/shard_map/ppermute | solution.py:309
  3.4 3.6 %collective-permute-start.1 = (f32[4,2560]{1,0:T(4,128)S(1)}, f32[4,2560]{1,0:T(4,128)S(1)}, u32[]{:S(2)}, u32[]{:S(2)}) collective-permute-start(f32[4,2560]{1,0:T(4,128)S(1)} %get-tuple-element.10), channel_id=1, source_target_pairs={{0,1},{1,2},{2,3},{3,4},{4,5},{5,6},{6,7},{8,9},{9,10},{10,11},{11... | collective-permute-start | bytes 122888 | tf_op jit(solution)/shard_map/ppermute | solution.py:310
  7.0 0.0 copy-done.3
  7.0 0.0 copy-done.5
  7.0 0.0 copy-start.1
  7.0 0.9 %copy-done.1 = bf16[2,256,256]{2,1,0:T(8,128)(2,1)S(1)} copy-done((bf16[2,256,256]{2,1,0:T(8,128)(2,1)S(1)}, bf16[2,256,256]{2,1,0:T(8,128)(2,1)}, u32[]{:S(2)}) %copy-start.1) | copy-done | bytes 262168
  7.9 0.0 copy-start.2
  7.9 0.0 copy-start.4
  7.9 0.3 own_rows.1.own_ref
  8.3 0.0 collective-permute-done.below_ref
  8.3 2.3 %collective-permute-done.1.above_ref = f32[4,2560]{1,0:T(4,128)S(1)} collective-permute-done((f32[4,2560]{1,0:T(4,128)S(1)}, f32[4,2560]{1,0:T(4,128)S(1)}, u32[]{:S(2)}, u32[]{:S(2)}) %collective-permute-start.1) | collective-permute-done | bytes 40992 | tf_op jit(solution)/shard_map/ppermute | solution.py:310
  10.5 0.0 copy-done.6
  10.5 0.0 copy-done.2
  10.5 0.0 copy-done.4
  10.5 1.4 %tile.1 = bf16[64,128]{1,0:T(8,128)(2,1)S(1)} custom-call(f32[88,256]{1,0:T(8,128)S(1)} %own_rows.1.own_ref, f32[4,2560]{1,0:T(4,128)S(1)} %collective-permute-done.below_ref, f32[4,2560]{1,0:T(4,128)S(1)} %collective-permute-done.1.above_ref, s32[32,32]{1,0:T(8,128)S(1)} %copy-done.6, f32[2,11,128]{2,1,0:T(8,128)S(1)} %copy-done.5, ...), custom_call_target="tpu_custom_call" | custom-call | tf_op jit(solution)/shard_map/tile/pallas_call | solution.py:284
  12.0 56.1 %all_to_all.9 = bf16[32,2,128]{2,1,0:T(2,128)(2,1)S(1)} all-to-all(bf16[32,2,128]{2,1,0:T(2,128)(2,1)S(1)} %bitcast.5), channel_id=1, replica_groups=mesh['scan'=2,'ang'=32,'row'=8] {'ang'}, dimensions={0} | all-to-all | bytes 32768 | tf_op jit(solution)/shard_map/all_to_all | solution.py:313
  68.0 0.1 reshape.6
  68.1 0.0 copy-done
  68.1 0.8 %convolution_bitcast_fusion = f32[8,256]{1,0:T(8,128)} fusion(bf16[32,8,32]{2,1,0:T(8,128)(2,1)S(1)} %reshape.6, bf16[32,32,256]{2,1,0:T(8,128)(2,1)S(1)} %copy-done), kind=kOutput, calls=%fused_computation | convolution fusion | flops 4194304 | bytes 548864 | tf_op jit(solution)/shard_map/dot_general | solution.py:315
Async XLA Ops:
  0.0 68.1 %copy-start = (bf16[32,32,256]{2,1,0:T(8,128)(2,1)S(1)}, bf16[32,32,256]{2,1,0:T(8,128)(2,1)}, u32[]{:S(2)}) copy-start(bf16[32,32,256]{2,1,0:T(8,128)(2,1)} %param.11) | copy-start | bytes 1572868
  0.0 7.0 %copy-start.3 = (f32[9,11,128]{2,1,0:T(8,128)S(1)}, f32[9,11,128]{2,1,0:T(8,128)}, u32[]{:S(2)}) copy-start(f32[9,11,128]{2,1,0:T(8,128)} %constant.11.clone.gains_ref) | copy-start | bytes 152068
  0.0 7.0 %copy-start.5 = (f32[2,11,128]{2,1,0:T(8,128)S(1)}, f32[2,11,128]{2,1,0:T(8,128)}, u32[]{:S(2)}) copy-start(f32[2,11,128]{2,1,0:T(8,128)} %constant.8.clone.turns_ref) | copy-start | bytes 33796
  0.0 10.5 %copy-start.6 = (s32[32,32]{1,0:T(8,128)S(1)}, s32[32,32]{1,0:T(8,128)}, u32[]{:S(2)}) copy-start(s32[32,32]{1,0:T(8,128)} %starts_hbm.1) | copy-start | bytes 12292
  1.0 7.2 %collective-permute-start = (f32[4,2560]{1,0:T(4,128)S(1)}, f32[4,2560]{1,0:T(4,128)S(1)}, u32[]{:S(2)}, u32[]{:S(2)}) collective-permute-start(f32[4,2560]{1,0:T(4,128)S(1)} %get-tuple-element.9), channel_id=1, source_target_pairs={{1,0},{2,1},{3,2},{4,3},{5,4},{6,5},{7,6},{9,8},{10,9},{11,10},{12... | collective-permute-start | bytes 122888 | tf_op jit(solution)/shard_map/ppermute | solution.py:309
  3.4 7.1 %collective-permute-start.1 = (f32[4,2560]{1,0:T(4,128)S(1)}, f32[4,2560]{1,0:T(4,128)S(1)}, u32[]{:S(2)}, u32[]{:S(2)}) collective-permute-start(f32[4,2560]{1,0:T(4,128)S(1)} %get-tuple-element.10), channel_id=1, source_target_pairs={{0,1},{1,2},{2,3},{3,4},{4,5},{5,6},{6,7},{8,9},{9,10},{10,11},{11... | collective-permute-start | bytes 122888 | tf_op jit(solution)/shard_map/ppermute | solution.py:310
  7.0 1.0 %copy-start.1 = (bf16[2,256,256]{2,1,0:T(8,128)(2,1)S(1)}, bf16[2,256,256]{2,1,0:T(8,128)(2,1)}, u32[]{:S(2)}) copy-start(bf16[2,256,256]{2,1,0:T(8,128)(2,1)} %constant.9.clone.forward_ref) | copy-start | bytes 786436
  7.9 2.6 %copy-start.2 = (bf16[2,256,256]{2,1,0:T(8,128)(2,1)S(1)}, bf16[2,256,256]{2,1,0:T(8,128)(2,1)}, u32[]{:S(2)}) copy-start(bf16[2,256,256]{2,1,0:T(8,128)(2,1)} %constant.9.clone.forward_ref) | copy-start | bytes 786436
  7.9 2.6 %copy-start.4 = (bf16[2,256,256]{2,1,0:T(8,128)(2,1)S(1)}, bf16[2,256,256]{2,1,0:T(8,128)(2,1)}, u32[]{:S(2)}) copy-start(bf16[2,256,256]{2,1,0:T(8,128)(2,1)} %constant.10.clone.inverse_ref) | copy-start | bytes 786436

commit v4 on v3

--- a/solution.py
+++ b/solution.py
@@ -47,7 +47,13 @@
     ramp = ramp_gain * (folded / width) * (0.5 + 0.5 * np.cos(2.0 * np.pi * folded / width))
     twice = np.where((ks == 0) | (ks == half), 1.0, 2.0)
     gains = gains * (ramp * twice[:, None] / width)
-    return turns, split(forward), split(forward.T), gains.astype(np.float32)
+    rows_dev = tile_rows - 2 * HALO
+    out_row = np.arange(rows_dev)
+    halo_row = (out_row[None, :] - np.arange(rows_dev)[:, None]) % rows_dev
+    apart = np.abs(out_row[None, :] + HALO - np.where(halo_row < HALO, halo_row, halo_row + rows_dev))
+    apart = np.minimum(apart, tile_rows - apart)
+    halo_gains = np.transpose(gains[apart], (0, 2, 1, 3))
+    return turns, split(forward), split(forward.T), gains.astype(np.float32), halo_gains.astype(np.float32)
 
 
 def plus(terms):
@@ -97,7 +103,9 @@
     high = values.astype(jnp.bfloat16)
     low = (values - high.astype(jnp.float32)).astype(jnp.bfloat16)
     dot = partial(jnp.dot, preferred_element_type=jnp.float32)
-    return dot(high, matrix_ref[0]) + dot(low, matrix_ref[0]) + dot(high, matrix_ref[1])
+    lines = values.shape[0]
+    both = dot(jnp.concatenate((high, low), axis=0), matrix_ref[0])
+    return both[:lines] + (both[lines:] + dot(high, matrix_ref[1]))
 
 
 def spectrum(chunks, turns_ref, forward_ref):
@@ -179,17 +187,6 @@
             out_ref[rows, side] = total
 
 
-def halo_terms(here, row):
-    moved = [here] + [pltpu.roll(here, s, axis=0) for s in range(1, SUB)]
-    terms = {HALO: moved[0], 2 * HALO: moved[HALO]}
-    for d in range(1, HALO):
-        s, w = HALO - d, HALO + d
-        near_s, near_w = row >= s + HALO, row < w - HALO
-        terms[d] = jnp.where(near_s, moved[s], jnp.where(near_w, moved[w], 0.0))
-        terms[HALO + s] = jnp.where(near_s, 0.0, moved[s]) + jnp.where(near_w, 0.0, moved[w])
-    return terms
-
-
 def tile_kernel(
     own_ref, below_ref, above_ref, starts_hbm, turns_ref, forward_ref, inverse_ref, gains_ref, out_ref,
     sheet, starts, sem
@@ -202,6 +199,8 @@
         for a in range(blocks)
     ]
     spec = spectrum(halo, turns_ref, forward_ref)
+    copy.wait()
+    mine = lax.axis_index("ang")
     row = lax.broadcasted_iota(jnp.int32, (SUB, LANES), 0)
     lane = lax.broadcasted_iota(jnp.int32, (SUB, LANES), 1)
     parts = []
@@ -209,16 +208,15 @@
         rows = slice(k * SUB, (k + 1) * SUB)
         both = []
         for side in (slice(0, LANES), slice(LANES, 2 * LANES)):
-            total = own_ref[rows, side]
-            for d, term in halo_terms(spec[rows, side], row).items():
-                total += term * gains_ref[d, k : k + 1, :]
+            here = spec[rows, side]
+            total = own_ref[rows, side] + here * gains_ref[0, k]
+            for s in range(1, SUB):
+                total += pltpu.roll(here, s, axis=0) * gains_ref[s, k]
             both.append(total)
         parts.append(jnp.concatenate(both, axis=1))
     filtered = columns(jnp.concatenate(parts, axis=0), turns_ref, inverse_ref, blocks)
     for a in range(blocks):
-        sheet[:, a * LANES : (a + 1) * LANES] = filtered[a]
-    copy.wait()
-    mine = lax.axis_index("ang")
+        sheet[a] = filtered[a]
     regions = starts.shape[1]
     cut = out_ref.shape[0] * LANES // (regions * SUB)
     per = LANES // cut
@@ -228,13 +226,10 @@
         gathered = None
         for q in range(per):
             start = starts[mine, group * per + q]
-            block = start // LANES
-            offset = start - block * LANES
-            after = jnp.minimum(block + 1, blocks - 1)
-            here = sheet[:, pl.ds(pl.multiple_of(block * LANES, LANES), LANES)]
-            then = sheet[:, pl.ds(pl.multiple_of(after * LANES, LANES), LANES)]
-            window = jnp.where(lane >= offset, here, then)
-            window = pltpu.roll(window, lax.rem(LANES + q * cut - offset, LANES), axis=1)
+            block = lax.shift_right_logical(start, 7)
+            offset = start & (LANES - 1)
+            window = jnp.where(lane >= offset, sheet[block], sheet[block + 1])
+            window = pltpu.roll(window, (LANES + q * cut - offset) & (LANES - 1), axis=1)
             gathered = window if q == 0 else jnp.where(lane // cut == q, window, gathered)
         for shift in range(per):
             moved = gathered if shift == 0 else pltpu.roll(gathered, shift * cut, axis=1)
@@ -287,7 +282,7 @@
         in_specs=[VMEM] * 3 + [ANY] + [VMEM] * 4,
         out_specs=VMEM,
         scratch_shapes=[
-            pltpu.VMEM((SUB, above.shape[1]), jnp.float32),
+            pltpu.VMEM((above.shape[1] // LANES + 1, SUB, LANES), jnp.float32),
             pltpu.SMEM(starts.shape, jnp.int32),
             pltpu.SemaphoreType.DMA,
         ],
@@ -303,13 +298,13 @@
     rows = lax.axis_size("row")
     up = [(i, i + 1) for i in range(rows - 1)]
     down = [(j, i) for i, j in up]
-    turns, forward, inverse, gains = (jnp.asarray(t) for t in tables(width, rows_dev + 2 * HALO))
+    turns, forward, inverse, gains, halo_gains = (jnp.asarray(t) for t in tables(width, rows_dev + 2 * HALO))
     in_hbm = partial(pltpu.with_memory_space_constraint, memory_space=pltpu.HBM)
     own, first, last = make_contrast(in_hbm(projections), in_hbm(flats))
     below = lax.ppermute(first, "row", down)
     above = lax.ppermute(last, "row", up)
     own_spec = make_own(own, turns, forward, gains)
-    outgoing = make_tile(own_spec, below, above, block_start, turns, forward, inverse, gains, cut)
+    outgoing = make_tile(own_spec, below, above, block_start, turns, forward, inverse, halo_gains, cut)
     incoming = lax.all_to_all(outgoing, "ang", split_axis=0, concat_axis=0, tiled=True)
     blocks = incoming.reshape(bp_weights.shape[0], rows_dev, cut)
     return lax.dot_general(

time: 69.2 us -> 70.2 us (1.014)
  the two profiles are of different devices: /device:TPU:88 before, /device:TPU:72 now
where the time goes in v4:
time: 70.2 us; the launch traced here: 69.9 us
  blocking collectives  56.1 us (80%)
  starting transfers between devices  5.9 us (8%)
  Pallas kernels  2.73 us (4%)
  waiting for transfers between devices  2.25 us (3%)
  local copies, waits for them, and re-layouts  2.04 us (3%)
  matrix products  0.85 us (1%)
    all_to_all x1, blocking collectives, body(): lax.all_to_all(outgoing, 'ang', split_axis=0, concat_axis=0, tiled=True)  56.1 us
    ppermute x1, starting transfers between devices, body(): above = lax.ppermute(last, 'row', up)  3.57 us
    ppermute x1, starting transfers between devices, body(): below = lax.ppermute(first, 'row', down)  2.34 us
    ppermute x1, waiting for transfers between devices, body(): above = lax.ppermute(last, 'row', up)  2.25 us
    unnamed x16, local copies, waits for them, and re-layouts  1.95 us
  transfers between devices with their start and end apart: 2, of which 1 were waited for; matrix products, arithmetic and copies ran while one was open for 0% of the time, Pallas kernels for 0%

profile of v4, /device:TPU:72, one launch (start us, length us, event | category | flops | bytes accessed | tf_op | source)
XLA Modules:
  0.0 69.9 jit_solution(11241416392869839137)
XLA Ops:
  0.0 0.0 copy-start
  0.0 0.0 copy-start.5
  0.0 0.0 copy-start.6
  0.0 0.0 copy-start.7
  0.0 1.0 %contrast.1 = (f32[8,2560]{1,0:T(8,128)S(1)}, f32[4,2560]{1,0:T(4,128)S(1)}, f32[4,2560]{1,0:T(4,128)S(1)}) custom-call(bf16[1,8,2560]{2,1,0:T(8,128)(2,1)} %proj_hbm.1, f32[8,2560]{1,0:T(8,128)} %flat_hbm.1), custom_call_target="tpu_custom_call" | custom-call | tf_op jit(solution)/shard_map/contrast/pallas_call | solution.py:250
  1.0 2.3 %collective-permute-start = (f32[4,2560]{1,0:T(4,128)S(1)}, f32[4,2560]{1,0:T(4,128)S(1)}, u32[]{:S(2)}, u32[]{:S(2)}) collective-permute-start(f32[4,2560]{1,0:T(4,128)S(1)} %get-tuple-element.9), channel_id=1, source_target_pairs={{1,0},{2,1},{3,2},{4,3},{5,4},{6,5},{7,6},{9,8},{10,9},{11,10},{12... | collective-permute-start | bytes 122888 | tf_op jit(solution)/shard_map/ppermute | solution.py:304
  3.4 3.6 %collective-permute-start.1 = (f32[4,2560]{1,0:T(4,128)S(1)}, f32[4,2560]{1,0:T(4,128)S(1)}, u32[]{:S(2)}, u32[]{:S(2)}) collective-permute-start(f32[4,2560]{1,0:T(4,128)S(1)} %get-tuple-element.10), channel_id=1, source_target_pairs={{0,1},{1,2},{2,3},{3,4},{4,5},{5,6},{6,7},{8,9},{9,10},{10,11},{11... | collective-permute-start | bytes 122888 | tf_op jit(solution)/shard_map/ppermute | solution.py:305
  7.0 0.0 copy-done.5
  7.0 0.0 copy-done.6
  7.0 0.0 copy-start.1
  7.0 0.9 %copy-done.1 = bf16[2,256,256]{2,1,0:T(8,128)(2,1)S(1)} copy-done((bf16[2,256,256]{2,1,0:T(8,128)(2,1)S(1)}, bf16[2,256,256]{2,1,0:T(8,128)(2,1)}, u32[]{:S(2)}) %copy-start.1) | copy-done | bytes 262168
  7.9 0.0 copy-start.2
  7.9 0.0 copy-start.4
  7.9 0.3 own_rows.1.own_ref
  8.3 0.0 collective-permute-done.below_ref
  8.3 2.2 %collective-permute-done.1.above_ref = f32[4,2560]{1,0:T(4,128)S(1)} collective-permute-done((f32[4,2560]{1,0:T(4,128)S(1)}, f32[4,2560]{1,0:T(4,128)S(1)}, u32[]{:S(2)}, u32[]{:S(2)}) %collective-permute-start.1) | collective-permute-done | bytes 40992 | tf_op jit(solution)/shard_map/ppermute | solution.py:305
  10.5 0.0 copy-done.7
  10.5 0.0 copy-done.2
  10.5 0.0 copy-done.4
  10.5 0.0 copy-start.3
  10.5 1.0 %copy-done.3 = f32[8,11,8,128]{3,2,1,0:T(8,128)S(1)} copy-done((f32[8,11,8,128]{3,2,1,0:T(8,128)S(1)}, f32[8,11,8,128]{3,2,1,0:T(8,128)}, u32[]{:S(2)}) %copy-start.3) | copy-done | bytes 360472
  11.5 1.4 %tile.1 = bf16[64,128]{1,0:T(8,128)(2,1)S(1)} custom-call(f32[88,256]{1,0:T(8,128)S(1)} %own_rows.1.own_ref, f32[4,2560]{1,0:T(4,128)S(1)} %collective-permute-done.below_ref, f32[4,2560]{1,0:T(4,128)S(1)} %collective-permute-done.1.above_ref, s32[32,32]{1,0:T(8,128)S(1)} %copy-done.7, f32[2,11,128]{2,1,0:T(8,128)S(1)} %copy-done.6, ...), custom_call_target="tpu_custom_call" | custom-call | tf_op jit(solution)/shard_map/tile/pallas_call | solution.py:279
  12.9 56.1 %all_to_all.9 = bf16[32,2,128]{2,1,0:T(2,128)(2,1)S(1)} all-to-all(bf16[32,2,128]{2,1,0:T(2,128)(2,1)S(1)} %bitcast.5), channel_id=1, replica_groups=mesh['scan'=2,'ang'=32,'row'=8] {'ang'}, dimensions={0} | all-to-all | bytes 32768 | tf_op jit(solution)/shard_map/all_to_all | solution.py:308
  69.0 0.1 reshape.6
  69.1 0.0 copy-done
  69.1 0.8 %convolution_bitcast_fusion = f32[8,256]{1,0:T(8,128)} fusion(bf16[32,8,32]{2,1,0:T(8,128)(2,1)S(1)} %reshape.6, bf16[32,32,256]{2,1,0:T(8,128)(2,1)S(1)} %copy-done), kind=kOutput, calls=%fused_computation | convolution fusion | flops 4194304 | bytes 548864 | tf_op jit(solution)/shard_map/dot_general | solution.py:310
Async XLA Ops:
  0.0 69.1 %copy-start = (bf16[32,32,256]{2,1,0:T(8,128)(2,1)S(1)}, bf16[32,32,256]{2,1,0:T(8,128)(2,1)}, u32[]{:S(2)}) copy-start(bf16[32,32,256]{2,1,0:T(8,128)(2,1)} %param.12) | copy-start | bytes 1572868
  0.0 7.0 %copy-start.5 = (f32[9,11,128]{2,1,0:T(8,128)S(1)}, f32[9,11,128]{2,1,0:T(8,128)}, u32[]{:S(2)}) copy-start(f32[9,11,128]{2,1,0:T(8,128)} %constant.13.clone.gains_ref) | copy-start | bytes 152068
  0.0 7.0 %copy-start.6 = (f32[2,11,128]{2,1,0:T(8,128)S(1)}, f32[2,11,128]{2,1,0:T(8,128)}, u32[]{:S(2)}) copy-start(f32[2,11,128]{2,1,0:T(8,128)} %constant.10.clone.turns_ref) | copy-start | bytes 33796
  0.0 10.5 %copy-start.7 = (s32[32,32]{1,0:T(8,128)S(1)}, s32[32,32]{1,0:T(8,128)}, u32[]{:S(2)}) copy-start(s32[32,32]{1,0:T(8,128)} %starts_hbm.1) | copy-start | bytes 12292
  1.0 7.2 %collective-permute-start = (f32[4,2560]{1,0:T(4,128)S(1)}, f32[4,2560]{1,0:T(4,128)S(1)}, u32[]{:S(2)}, u32[]{:S(2)}) collective-permute-start(f32[4,2560]{1,0:T(4,128)S(1)} %get-tuple-element.9), channel_id=1, source_target_pairs={{1,0},{2,1},{3,2},{4,3},{5,4},{6,5},{7,6},{9,8},{10,9},{11,10},{12... | collective-permute-start | bytes 122888 | tf_op jit(solution)/shard_map/ppermute | solution.py:304
  3.4 7.1 %collective-permute-start.1 = (f32[4,2560]{1,0:T(4,128)S(1)}, f32[4,2560]{1,0:T(4,128)S(1)}, u32[]{:S(2)}, u32[]{:S(2)}) collective-permute-start(f32[4,2560]{1,0:T(4,128)S(1)} %get-tuple-element.10), channel_id=1, source_target_pairs={{0,1},{1,2},{2,3},{3,4},{4,5},{5,6},{6,7},{8,9},{9,10},{10,11},{11... | collective-permute-start | bytes 122888 | tf_op jit(solution)/shard_map/ppermute | solution.py:305
  7.0 1.0 %copy-start.1 = (bf16[2,256,256]{2,1,0:T(8,128)(2,1)S(1)}, bf16[2,256,256]{2,1,0:T(8,128)(2,1)}, u32[]{:S(2)}) copy-start(bf16[2,256,256]{2,1,0:T(8,128)(2,1)} %constant.11.clone.forward_ref) | copy-start | bytes 786436
  7.9 2.6 %copy-start.2 = (bf16[2,256,256]{2,1,0:T(8,128)(2,1)S(1)}, bf16[2,256,256]{2,1,0:T(8,128)(2,1)}, u32[]{:S(2)}) copy-start(bf16[2,256,256]{2,1,0:T(8,128)(2,1)} %constant.11.clone.forward_ref) | copy-start | bytes 786436
  7.9 2.6 %copy-start.4 = (bf16[2,256,256]{2,1,0:T(8,128)(2,1)S(1)}, bf16[2,256,256]{2,1,0:T(8,128)(2,1)}, u32[]{:S(2)}) copy-start(bf16[2,256,256]{2,1,0:T(8,128)(2,1)} %constant.12.clone.inverse_ref) | copy-start | bytes 786436
  10.5 1.0 %copy-start.3 = (f32[8,11,8,128]{3,2,1,0:T(8,128)S(1)}, f32[8,11,8,128]{3,2,1,0:T(8,128)}, u32[]{:S(2)}) copy-start(f32[8,11,8,128]{3,2,1,0:T(8,128)} %constant.14.clone.gains_ref) | copy-start | bytes 1081348

commit v5 on v4

--- a/solution.py
+++ b/solution.py
@@ -47,13 +47,7 @@
     ramp = ramp_gain * (folded / width) * (0.5 + 0.5 * np.cos(2.0 * np.pi * folded / width))
     twice = np.where((ks == 0) | (ks == half), 1.0, 2.0)
     gains = gains * (ramp * twice[:, None] / width)
-    rows_dev = tile_rows - 2 * HALO
-    out_row = np.arange(rows_dev)
-    halo_row = (out_row[None, :] - np.arange(rows_dev)[:, None]) % rows_dev
-    apart = np.abs(out_row[None, :] + HALO - np.where(halo_row < HALO, halo_row, halo_row + rows_dev))
-    apart = np.minimum(apart, tile_rows - apart)
-    halo_gains = np.transpose(gains[apart], (0, 2, 1, 3))
-    return turns, split(forward), split(forward.T), gains.astype(np.float32), halo_gains.astype(np.float32)
+    return turns, split(forward), split(forward.T), gains.astype(np.float32)
 
 
 def plus(terms):
@@ -171,10 +165,31 @@
     return ref[:, block * LANES : (block + 1) * LANES]
 
 
-def own_kernel(own_ref, turns_ref, forward_ref, gains_ref, out_ref):
+def halo_gains(gains_ref, k, row):
+    gains = [jnp.broadcast_to(gains_ref[d, k : k + 1, :], (SUB, LANES)) for d in range(2 * HALO + 1)]
+    for s in range(SUB):
+        far = gains[2 * HALO - abs(s - HALO)]
+        near = gains[abs(s - HALO)]
+        if s < HALO:
+            yield s, jnp.where(row >= s + HALO, near, far)
+        else:
+            yield s, jnp.where(row < s - HALO, near, far)
+
+
+def own_kernel(
+    own_ref, turns_ref, gains_ref, forward_hbm, inverse_hbm, out_ref, forward_ref, inverse_ref, halo_ref, sems
+):
+    forward_copy = pltpu.make_async_copy(forward_hbm, forward_ref, sems.at[0])
+    inverse_copy = pltpu.make_async_copy(inverse_hbm, inverse_ref, sems.at[1])
+    forward_copy.start()
+    inverse_copy.start()
+    row = lax.broadcasted_iota(jnp.int32, (SUB, LANES), 0)
+    for k in range(gains_ref.shape[1]):
+        for s, gain in halo_gains(gains_ref, k, row):
+            halo_ref[s, k] = gain
+    forward_copy.wait()
     blocks = own_ref.shape[1] // LANES
     spec = spectrum([lanes_of(own_ref, a) for a in range(blocks)], turns_ref, forward_ref)
-    row = lax.broadcasted_iota(jnp.int32, (SUB, LANES), 0)
     for k in range(blocks // 2 + 1):
         rows = slice(k * SUB, (k + 1) * SUB)
         for side in (slice(0, LANES), slice(LANES, 2 * LANES)):
@@ -185,6 +200,7 @@
                 pair = jnp.where(row >= d, moved[d], 0.0) + jnp.where(row < SUB - d, moved[SUB - d], 0.0)
                 total += pair * gains_ref[d, k : k + 1, :]
             out_ref[rows, side] = total
+    inverse_copy.wait()
 
 
 def tile_kernel(
@@ -199,8 +215,6 @@
         for a in range(blocks)
     ]
     spec = spectrum(halo, turns_ref, forward_ref)
-    copy.wait()
-    mine = lax.axis_index("ang")
     row = lax.broadcasted_iota(jnp.int32, (SUB, LANES), 0)
     lane = lax.broadcasted_iota(jnp.int32, (SUB, LANES), 1)
     parts = []
@@ -217,6 +231,8 @@
     filtered = columns(jnp.concatenate(parts, axis=0), turns_ref, inverse_ref, blocks)
     for a in range(blocks):
         sheet[a] = filtered[a]
+    copy.wait()
+    mine = lax.axis_index("ang")
     regions = starts.shape[1]
     cut = out_ref.shape[0] * LANES // (regions * SUB)
     per = LANES // cut
@@ -244,6 +260,10 @@
     out_ref[...] = out.astype(jnp.bfloat16)
 
 
+def in_hbm(array):
+    return pltpu.with_memory_space_constraint(array, pltpu.HBM)
+
+
 def make_contrast(projections, flats):
     shape = flats.shape
     edge = jax.ShapeDtypeStruct((HALO, shape[1]), halo_type)
@@ -259,19 +279,25 @@
         ],
         compiler_params=PARAMS,
         name="contrast",
-    )(projections, flats)
-
-
-def make_own(own, turns, forward, gains):
-    lines = turns.shape[1] * SUB
+    )(in_hbm(projections), in_hbm(flats))
+
+
+def make_own(own, turns, forward, inverse, gains):
+    groups = turns.shape[1]
     return pl.pallas_call(
         own_kernel,
-        out_shape=jax.ShapeDtypeStruct((lines, 2 * LANES), jnp.float32),
-        in_specs=[VMEM] * 4,
-        out_specs=VMEM,
+        out_shape=(
+            jax.ShapeDtypeStruct((groups * SUB, 2 * LANES), jnp.float32),
+            jax.ShapeDtypeStruct(forward.shape, forward.dtype),
+            jax.ShapeDtypeStruct(inverse.shape, inverse.dtype),
+            jax.ShapeDtypeStruct((SUB, groups, SUB, LANES), jnp.float32),
+        ),
+        in_specs=[VMEM] * 3 + [HBM] * 2,
+        out_specs=(VMEM,) * 4,
+        scratch_shapes=[pltpu.SemaphoreType.DMA((2,))],
         compiler_params=PARAMS,
         name="own_rows",
-    )(own, turns, forward, gains)
+    )(own, turns, gains, in_hbm(forward), in_hbm(inverse))
 
 
 def make_tile(own_spec, below, above, starts, turns, forward, inverse, gains, cut):
@@ -298,13 +324,12 @@
     rows = lax.axis_size("row")
     up = [(i, i + 1) for i in range(rows - 1)]
     down = [(j, i) for i, j in up]
-    turns, forward, inverse, gains, halo_gains = (jnp.asarray(t) for t in tables(width, rows_dev + 2 * HALO))
-    in_hbm = partial(pltpu.with_memory_space_constraint, memory_space=pltpu.HBM)
-    own, first, last = make_contrast(in_hbm(projections), in_hbm(flats))
+    turns, forward, inverse, gains = (jnp.asarray(t) for t in tables(width, rows_dev + 2 * HALO))
+    own, first, last = make_contrast(projections, flats)
     below = lax.ppermute(first, "row", down)
     above = lax.ppermute(last, "row", up)
-    own_spec = make_own(own, turns, forward, gains)
-    outgoing = make_tile(own_spec, below, above, block_start, turns, forward, inverse, halo_gains, cut)
+    own_spec, forward, inverse, gains = make_own(own, turns, forward, inverse, gains)
+    outgoing = make_tile(own_spec, below, above, block_start, turns, forward, inverse, gains, cut)
     incoming = lax.all_to_all(outgoing, "ang", split_axis=0, concat_axis=0, tiled=True)
     blocks = incoming.reshape(bp_weights.shape[0], rows_dev, cut)
     return lax.dot_general(

time: 70.2 us -> 68.9 us (0.981)
  the two profiles are of different devices: /device:TPU:72 before, /device:TPU:88 now
where the time goes in v5:
time: 68.9 us; the launch traced here: 68.7 us
  blocking collectives  56.1 us (81%)
  starting transfers between devices  5.9 us (9%)
  Pallas kernels  3.5 us (5%)
  waiting for transfers between devices  2.21 us (3%)
  matrix products  0.85 us (1%)
    all_to_all x1, blocking collectives, body(): lax.all_to_all(outgoing, 'ang', split_axis=0, concat_axis=0, tiled=True)  56.1 us
    ppermute x1, starting transfers between devices, body(): above = lax.ppermute(last, 'row', up)  3.57 us
    ppermute x1, starting transfers between devices, body(): below = lax.ppermute(first, 'row', down)  2.34 us
    ppermute x1, waiting for transfers between devices, body(): above = lax.ppermute(last, 'row', up)  2.21 us
  transfers between devices with their start and end apart: 2, of which 1 were waited for; matrix products, arithmetic and copies ran while one was open for 0% of the time, Pallas kernels for 2%

profile of v5, /device:TPU:88, one launch (start us, length us, event | category | flops | bytes accessed | tf_op | source)
XLA Modules:
  0.0 68.7 jit_solution(1966125605076772069)
XLA Ops:
  0.0 0.0 copy-start
  0.0 0.0 copy-start.1
  0.0 0.0 copy-start.2
  0.0 1.0 %contrast.1 = (f32[8,2560]{1,0:T(8,128)S(1)}, f32[4,2560]{1,0:T(4,128)S(1)}, f32[4,2560]{1,0:T(4,128)S(1)}) custom-call(bf16[1,8,2560]{2,1,0:T(8,128)(2,1)} %proj_hbm.1, f32[8,2560]{1,0:T(8,128)} %flat_hbm.1), custom_call_target="tpu_custom_call" | custom-call | tf_op jit(solution)/shard_map/contrast/pallas_call | solution.py:270
  1.0 2.3 %collective-permute-start = (f32[4,2560]{1,0:T(4,128)S(1)}, f32[4,2560]{1,0:T(4,128)S(1)}, u32[]{:S(2)}, u32[]{:S(2)}) collective-permute-start(f32[4,2560]{1,0:T(4,128)S(1)} %get-tuple-element.14), channel_id=1, source_target_pairs={{1,0},{2,1},{3,2},{4,3},{5,4},{6,5},{7,6},{9,8},{10,9},{11,10},{12... | collective-permute-start | bytes 122888 | tf_op jit(solution)/shard_map/ppermute | solution.py:329
  3.4 3.6 %collective-permute-start.1 = (f32[4,2560]{1,0:T(4,128)S(1)}, f32[4,2560]{1,0:T(4,128)S(1)}, u32[]{:S(2)}, u32[]{:S(2)}) collective-permute-start(f32[4,2560]{1,0:T(4,128)S(1)} %get-tuple-element.15), channel_id=1, source_target_pairs={{0,1},{1,2},{2,3},{3,4},{4,5},{5,6},{6,7},{8,9},{9,10},{10,11},{11... | collective-permute-start | bytes 122888 | tf_op jit(solution)/shard_map/ppermute | solution.py:330
  7.0 0.0 copy-done.1
  7.0 0.0 copy-done.2
  7.0 0.0 copy-start.3
  7.0 1.3 %own_rows.1 = (f32[88,256]{1,0:T(8,128)S(1)}, bf16[2,256,256]{2,1,0:T(8,128)(2,1)S(1)}, bf16[2,256,256]{2,1,0:T(8,128)(2,1)S(1)}, f32[8,11,8,128]{3,2,1,0:T(8,128)S(1)}) custom-call(f32[8,2560]{1,0:T(8,128)S(1)} %get-tuple-element.12.own_ref, f32[2,11,128]{2,1,0:T(8,128)S(1)} %copy-done.2, f32[9,11,128]{2,1,0:T(8,128)S(1)} %copy-done.1, ...), custom_call_target="tpu_custom_call" | custom-call | tf_op jit(solution)/shard_map/own_rows/pallas_call | solution.py:287
  8.3 0.0 collective-permute-done.below_ref
  8.3 2.2 %collective-permute-done.1.above_ref = f32[4,2560]{1,0:T(4,128)S(1)} collective-permute-done((f32[4,2560]{1,0:T(4,128)S(1)}, f32[4,2560]{1,0:T(4,128)S(1)}, u32[]{:S(2)}, u32[]{:S(2)}) %collective-permute-start.1) | collective-permute-done | bytes 40992 | tf_op jit(solution)/shard_map/ppermute | solution.py:330
  10.5 0.0 copy-done.3
  10.5 1.2 %tile.1 = bf16[64,128]{1,0:T(8,128)(2,1)S(1)} custom-call(f32[88,256]{1,0:T(8,128)S(1)} %get-tuple-element.13.own_ref, f32[4,2560]{1,0:T(4,128)S(1)} %collective-permute-done.below_ref, f32[4,2560]{1,0:T(4,128)S(1)} %collective-permute-done.1.above_ref, s32[32,32]{1,0:T(8,128)S(1)} %copy-done.3, f32[2,11,128]{2,1,0:T(8,128)S(1)} %copy-done.2, ...), custom_call_target="tpu_custom_call" | custom-call | tf_op jit(solution)/shard_map/tile/pallas_call | solution.py:305
  11.7 56.1 %all_to_all.9 = bf16[32,2,128]{2,1,0:T(2,128)(2,1)S(1)} all-to-all(bf16[32,2,128]{2,1,0:T(2,128)(2,1)S(1)} %bitcast.5), channel_id=1, replica_groups=mesh['scan'=2,'ang'=32,'row'=8] {'ang'}, dimensions={0} | all-to-all | bytes 32768 | tf_op jit(solution)/shard_map/all_to_all | solution.py:333
  67.8 0.1 reshape.6
  67.9 0.0 copy-done
  67.9 0.8 %convolution_bitcast_fusion = f32[8,256]{1,0:T(8,128)} fusion(bf16[32,8,32]{2,1,0:T(8,128)(2,1)S(1)} %reshape.6, bf16[32,32,256]{2,1,0:T(8,128)(2,1)S(1)} %copy-done), kind=kOutput, calls=%fused_computation | convolution fusion | flops 4194304 | bytes 548864 | tf_op jit(solution)/shard_map/dot_general | solution.py:335
Async XLA Ops:
  0.0 67.9 %copy-start = (bf16[32,32,256]{2,1,0:T(8,128)(2,1)S(1)}, bf16[32,32,256]{2,1,0:T(8,128)(2,1)}, u32[]{:S(2)}) copy-start(bf16[32,32,256]{2,1,0:T(8,128)(2,1)} %param.11) | copy-start | bytes 1572868
  0.0 6.9 %copy-start.1 = (f32[9,11,128]{2,1,0:T(8,128)S(1)}, f32[9,11,128]{2,1,0:T(8,128)}, u32[]{:S(2)}) copy-start(f32[9,11,128]{2,1,0:T(8,128)} %constant.11.clone.gains_ref) | copy-start | bytes 152068
  0.0 7.0 %copy-start.2 = (f32[2,11,128]{2,1,0:T(8,128)S(1)}, f32[2,11,128]{2,1,0:T(8,128)}, u32[]{:S(2)}) copy-start(f32[2,11,128]{2,1,0:T(8,128)} %constant.8.clone.turns_ref) | copy-start | bytes 33796
  1.0 7.3 %collective-permute-start = (f32[4,2560]{1,0:T(4,128)S(1)}, f32[4,2560]{1,0:T(4,128)S(1)}, u32[]{:S(2)}, u32[]{:S(2)}) collective-permute-start(f32[4,2560]{1,0:T(4,128)S(1)} %get-tuple-element.14), channel_id=1, source_target_pairs={{1,0},{2,1},{3,2},{4,3},{5,4},{6,5},{7,6},{9,8},{10,9},{11,10},{12... | collective-permute-start | bytes 122888 | tf_op jit(solution)/shard_map/ppermute | solution.py:329
  3.4 7.1 %collective-permute-start.1 = (f32[4,2560]{1,0:T(4,128)S(1)}, f32[4,2560]{1,0:T(4,128)S(1)}, u32[]{:S(2)}, u32[]{:S(2)}) collective-permute-start(f32[4,2560]{1,0:T(4,128)S(1)} %get-tuple-element.15), channel_id=1, source_target_pairs={{0,1},{1,2},{2,3},{3,4},{4,5},{5,6},{6,7},{8,9},{9,10},{10,11},{11... | collective-permute-start | bytes 122888 | tf_op jit(solution)/shard_map/ppermute | solution.py:330
  7.0 3.5 %copy-start.3 = (s32[32,32]{1,0:T(8,128)S(1)}, s32[32,32]{1,0:T(8,128)}, u32[]{:S(2)}) copy-start(s32[32,32]{1,0:T(8,128)} %starts_hbm.1) | copy-start | bytes 12292

commit v6 on v5

--- a/solution.py
+++ b/solution.py
@@ -16,7 +16,7 @@
 ramp_gain = 320.0
 halo_type = jnp.float32
 VMEM = pl.BlockSpec(memory_space=pltpu.VMEM)
-ANY = pl.BlockSpec(memory_space=pl.ANY)
+SMEM = pl.BlockSpec(memory_space=pltpu.SMEM)
 HBM = pl.BlockSpec(memory_space=pltpu.HBM)
 PARAMS = pltpu.CompilerParams(vmem_limit_bytes=8 * 2**20)
 
@@ -177,12 +177,15 @@
 
 
 def own_kernel(
-    own_ref, turns_ref, gains_ref, forward_hbm, inverse_hbm, out_ref, forward_ref, inverse_ref, halo_ref, sems
+    own_ref, turns_ref, gains_ref, forward_hbm, inverse_hbm, starts_hbm,
+    out_ref, forward_ref, inverse_ref, halo_ref, starts_ref, sems
 ):
     forward_copy = pltpu.make_async_copy(forward_hbm, forward_ref, sems.at[0])
     inverse_copy = pltpu.make_async_copy(inverse_hbm, inverse_ref, sems.at[1])
+    starts_copy = pltpu.make_async_copy(starts_hbm.at[pl.ds(lax.axis_index("ang"), 1)], starts_ref, sems.at[2])
     forward_copy.start()
     inverse_copy.start()
+    starts_copy.start()
     row = lax.broadcasted_iota(jnp.int32, (SUB, LANES), 0)
     for k in range(gains_ref.shape[1]):
         for s, gain in halo_gains(gains_ref, k, row):
@@ -201,14 +204,13 @@
                 total += pair * gains_ref[d, k : k + 1, :]
             out_ref[rows, side] = total
     inverse_copy.wait()
+    starts_copy.wait()
 
 
 def tile_kernel(
-    own_ref, below_ref, above_ref, starts_hbm, turns_ref, forward_ref, inverse_ref, gains_ref, out_ref,
-    sheet, starts, sem
+    own_ref, below_ref, above_ref, starts, turns_ref, forward_ref, inverse_ref, gains_ref, out_ref,
+    sheet
 ):
-    copy = pltpu.make_async_copy(starts_hbm, starts, sem)
-    copy.start()
     blocks = above_ref.shape[1] // LANES
     halo = [
         jnp.concatenate((lanes_of(above_ref, a), lanes_of(below_ref, a)), axis=0).astype(jnp.float32)
@@ -231,8 +233,6 @@
     filtered = columns(jnp.concatenate(parts, axis=0), turns_ref, inverse_ref, blocks)
     for a in range(blocks):
         sheet[a] = filtered[a]
-    copy.wait()
-    mine = lax.axis_index("ang")
     regions = starts.shape[1]
     cut = out_ref.shape[0] * LANES // (regions * SUB)
     per = LANES // cut
@@ -241,7 +241,7 @@
     for group in range(regions // per):
         gathered = None
         for q in range(per):
-            start = starts[mine, group * per + q]
+            start = starts[0, group * per + q]
             block = lax.shift_right_logical(start, 7)
             offset = start & (LANES - 1)
             window = jnp.where(lane >= offset, sheet[block], sheet[block + 1])
@@ -282,7 +282,7 @@
     )(in_hbm(projections), in_hbm(flats))
 
 
-def make_own(own, turns, forward, inverse, gains):
+def make_own(own, turns, forward, inverse, gains, starts):
     groups = turns.shape[1]
     return pl.pallas_call(
         own_kernel,
@@ -291,13 +291,14 @@
             jax.ShapeDtypeStruct(forward.shape, forward.dtype),
             jax.ShapeDtypeStruct(inverse.shape, inverse.dtype),
             jax.ShapeDtypeStruct((SUB, groups, SUB, LANES), jnp.float32),
+            pltpu.SMEM((1, starts.shape[1]), jnp.int32),
         ),
-        in_specs=[VMEM] * 3 + [HBM] * 2,
-        out_specs=(VMEM,) * 4,
-        scratch_shapes=[pltpu.SemaphoreType.DMA((2,))],
+        in_specs=[VMEM] * 3 + [HBM] * 3,
+        out_specs=(VMEM,) * 4 + (SMEM,),
+        scratch_shapes=[pltpu.SemaphoreType.DMA((3,))],
         compiler_params=PARAMS,
         name="own_rows",
-    )(own, turns, gains, in_hbm(forward), in_hbm(inverse))
+    )(own, turns, gains, in_hbm(forward), in_hbm(inverse), in_hbm(starts))
 
 
 def make_tile(own_spec, below, above, starts, turns, forward, inverse, gains, cut):
@@ -305,12 +306,10 @@
     return pl.pallas_call(
         tile_kernel,
         out_shape=jax.ShapeDtypeStruct((regions * SUB * cut // LANES, LANES), jnp.bfloat16),
-        in_specs=[VMEM] * 3 + [ANY] + [VMEM] * 4,
+        in_specs=[VMEM] * 3 + [SMEM] + [VMEM] * 4,
         out_specs=VMEM,
         scratch_shapes=[
             pltpu.VMEM((above.shape[1] // LANES + 1, SUB, LANES), jnp.float32),
-            pltpu.SMEM(starts.shape, jnp.int32),
-            pltpu.SemaphoreType.DMA,
         ],
         compiler_params=PARAMS,
         name="tile",
@@ -328,8 +327,8 @@
     own, first, last = make_contrast(projections, flats)
     below = lax.ppermute(first, "row", down)
     above = lax.ppermute(last, "row", up)
-    own_spec, forward, inverse, gains = make_own(own, turns, forward, inverse, gains)
-    outgoing = make_tile(own_spec, below, above, block_start, turns, forward, inverse, gains, cut)
+    own_spec, forward, inverse, gains, starts = make_own(own, turns, forward, inverse, gains, block_start)
+    outgoing = make_tile(own_spec, below, above, starts, turns, forward, inverse, gains, cut)
     incoming = lax.all_to_all(outgoing, "ang", split_axis=0, concat_axis=0, tiled=True)
     blocks = incoming.reshape(bp_weights.shape[0], rows_dev, cut)
     return lax.dot_general(

time: 68.9 us -> 68.5 us (level)
  no operation moved by 1% of the time
where the time goes in v6:
time: 68.5 us; the launch traced here: 68.3 us
  blocking collectives  56.1 us (82%)
  starting transfers between devices  5.9 us (9%)
  Pallas kernels  3.09 us (5%)
  waiting for transfers between devices  2.21 us (3%)
  matrix products  0.85 us (1%)
    all_to_all x1, blocking collectives, body(): lax.all_to_all(outgoing, 'ang', split_axis=0, concat_axis=0, tiled=True)  56.1 us
    ppermute x1, starting transfers between devices, body(): above = lax.ppermute(last, 'row', up)  3.57 us
    ppermute x1, starting transfers between devices, body(): below = lax.ppermute(first, 'row', down)  2.34 us
    ppermute x1, waiting for transfers between devices, body(): above = lax.ppermute(last, 'row', up)  2.2 us
  transfers between devices with their start and end apart: 2, of which 1 were waited for; matrix products, arithmetic and copies ran while one was open for 0% of the time, Pallas kernels for 2%

profile of v6, /device:TPU:88, one launch (start us, length us, event | category | flops | bytes accessed | tf_op | source)
XLA Modules:
  0.0 68.3 jit_solution(10383393433547350841)
XLA Ops:
  0.0 0.0 copy-start
  0.0 0.0 copy-start.1
  0.0 0.0 copy-start.2
  0.0 1.0 %contrast.1 = (f32[8,2560]{1,0:T(8,128)S(1)}, f32[4,2560]{1,0:T(4,128)S(1)}, f32[4,2560]{1,0:T(4,128)S(1)}) custom-call(bf16[1,8,2560]{2,1,0:T(8,128)(2,1)} %proj_hbm.1, f32[8,2560]{1,0:T(8,128)} %flat_hbm.1), custom_call_target="tpu_custom_call" | custom-call | tf_op jit(solution)/shard_map/contrast/pallas_call | solution.py:270
  1.0 2.3 %collective-permute-start = (f32[4,2560]{1,0:T(4,128)S(1)}, f32[4,2560]{1,0:T(4,128)S(1)}, u32[]{:S(2)}, u32[]{:S(2)}) collective-permute-start(f32[4,2560]{1,0:T(4,128)S(1)} %get-tuple-element.15), channel_id=1, source_target_pairs={{1,0},{2,1},{3,2},{4,3},{5,4},{6,5},{7,6},{9,8},{10,9},{11,10},{12... | collective-permute-start | bytes 122888 | tf_op jit(solution)/shard_map/ppermute | solution.py:328
  3.4 3.6 %collective-permute-start.1 = (f32[4,2560]{1,0:T(4,128)S(1)}, f32[4,2560]{1,0:T(4,128)S(1)}, u32[]{:S(2)}, u32[]{:S(2)}) collective-permute-start(f32[4,2560]{1,0:T(4,128)S(1)} %get-tuple-element.16), channel_id=1, source_target_pairs={{0,1},{1,2},{2,3},{3,4},{4,5},{5,6},{6,7},{8,9},{9,10},{10,11},{11... | collective-permute-start | bytes 122888 | tf_op jit(solution)/shard_map/ppermute | solution.py:329
  7.0 0.0 copy-done.1
  7.0 0.0 copy-done.2
  7.0 1.3 %own_rows.1 = (f32[88,256]{1,0:T(8,128)S(1)}, bf16[2,256,256]{2,1,0:T(8,128)(2,1)S(1)}, bf16[2,256,256]{2,1,0:T(8,128)(2,1)S(1)}, f32[8,11,8,128]{3,2,1,0:T(8,128)S(1)}, s32[1,32]{1,0:T(1,128)S(4)}) custom-call(f32[8,2560]{1,0:T(8,128)S(1)} %get-tuple-element.13.own_ref, f32[2,11,128]{2,1,0:T(8,128)S(1)} %copy-done.2, f32[9,11,128]{2,1,0:T(8,128)S(1)} %copy-done.1, ...), custom_call_target="tpu_custom_call" | custom-call | tf_op jit(solution)/shard_map/own_rows/pallas_call | solution.py:287
  8.3 0.0 collective-permute-done.below_ref
  8.3 2.2 %collective-permute-done.1.above_ref = f32[4,2560]{1,0:T(4,128)S(1)} collective-permute-done((f32[4,2560]{1,0:T(4,128)S(1)}, f32[4,2560]{1,0:T(4,128)S(1)}, u32[]{:S(2)}, u32[]{:S(2)}) %collective-permute-start.1) | collective-permute-done | bytes 40992 | tf_op jit(solution)/shard_map/ppermute | solution.py:329
  10.5 0.8 %tile.1 = bf16[64,128]{1,0:T(8,128)(2,1)S(1)} custom-call(f32[88,256]{1,0:T(8,128)S(1)} %get-tuple-element.14.own_ref, f32[4,2560]{1,0:T(4,128)S(1)} %collective-permute-done.below_ref, f32[4,2560]{1,0:T(4,128)S(1)} %collective-permute-done.1.above_ref, s32[1,32]{1,0:T(1,128)S(4)} %get-tuple-element.17.starts, f32[2,11,128]{2,1,0:T(8,128)S(1)} %copy-done.2, ...), custom_call_target="tpu_custom_call" | custom-call | tf_op jit(solution)/shard_map/tile/pallas_call | solution.py:306
  11.3 56.1 %all_to_all.9 = bf16[32,2,128]{2,1,0:T(2,128)(2,1)S(1)} all-to-all(bf16[32,2,128]{2,1,0:T(2,128)(2,1)S(1)} %bitcast.5), channel_id=1, replica_groups=mesh['scan'=2,'ang'=32,'row'=8] {'ang'}, dimensions={0} | all-to-all | bytes 32768 | tf_op jit(solution)/shard_map/all_to_all | solution.py:332
  67.3 0.1 reshape.6
  67.4 0.0 copy-done
  67.4 0.8 %convolution_bitcast_fusion = f32[8,256]{1,0:T(8,128)} fusion(bf16[32,8,32]{2,1,0:T(8,128)(2,1)S(1)} %reshape.6, bf16[32,32,256]{2,1,0:T(8,128)(2,1)S(1)} %copy-done), kind=kOutput, calls=%fused_computation | convolution fusion | flops 4194304 | bytes 548864 | tf_op jit(solution)/shard_map/dot_general | solution.py:334
Async XLA Ops:
  0.0 67.4 %copy-start = (bf16[32,32,256]{2,1,0:T(8,128)(2,1)S(1)}, bf16[32,32,256]{2,1,0:T(8,128)(2,1)}, u32[]{:S(2)}) copy-start(bf16[32,32,256]{2,1,0:T(8,128)(2,1)} %param.11) | copy-start | bytes 1572868
  0.0 6.9 %copy-start.1 = (f32[9,11,128]{2,1,0:T(8,128)S(1)}, f32[9,11,128]{2,1,0:T(8,128)}, u32[]{:S(2)}) copy-start(f32[9,11,128]{2,1,0:T(8,128)} %constant.11.clone.gains_ref) | copy-start | bytes 152068
  0.0 7.0 %copy-start.2 = (f32[2,11,128]{2,1,0:T(8,128)S(1)}, f32[2,11,128]{2,1,0:T(8,128)}, u32[]{:S(2)}) copy-start(f32[2,11,128]{2,1,0:T(8,128)} %constant.8.clone.turns_ref) | copy-start | bytes 33796
  1.0 7.3 %collective-permute-start = (f32[4,2560]{1,0:T(4,128)S(1)}, f32[4,2560]{1,0:T(4,128)S(1)}, u32[]{:S(2)}, u32[]{:S(2)}) collective-permute-start(f32[4,2560]{1,0:T(4,128)S(1)} %get-tuple-element.15), channel_id=1, source_target_pairs={{1,0},{2,1},{3,2},{4,3},{5,4},{6,5},{7,6},{9,8},{10,9},{11,10},{12... | collective-permute-start | bytes 122888 | tf_op jit(solution)/shard_map/ppermute | solution.py:328
  3.4 7.1 %collective-permute-start.1 = (f32[4,2560]{1,0:T(4,128)S(1)}, f32[4,2560]{1,0:T(4,128)S(1)}, u32[]{:S(2)}, u32[]{:S(2)}) collective-permute-start(f32[4,2560]{1,0:T(4,128)S(1)} %get-tuple-element.16), channel_id=1, source_target_pairs={{0,1},{1,2},{2,3},{3,4},{4,5},{5,6},{6,7},{8,9},{9,10},{10,11},{11... | collective-permute-start | bytes 122888 | tf_op jit(solution)/shard_map/ppermute | solution.py:329

commit v7 on v6

--- a/solution.py
+++ b/solution.py
@@ -260,6 +260,33 @@
     out_ref[...] = out.astype(jnp.bfloat16)
 
 
+def pixels_kernel(lines_ref, weights_ref, out_ref, lines, *, angles):
+    lines[...] = lines_ref[...].astype(jnp.float32)
+    cut = lines_ref.shape[0] * LANES // SUB // angles
+    per = LANES // cut
+    row = lax.broadcasted_iota(jnp.int32, (SUB, LANES), 0)
+    lane = lax.broadcasted_iota(jnp.int32, (SUB, LANES), 1)
+    turn = (lane // cut + per - row % per) % per
+    parts = []
+    for group in range(angles // per):
+        spread = []
+        for q in range(per):
+            at = (group * per + q) * (SUB // per)
+            low = jnp.broadcast_to(lines[at : at + 1, :], (SUB, LANES))
+            high = jnp.broadcast_to(lines[at + 1 : at + 2, :], (SUB, LANES))
+            spread.append(jnp.where(row < per, low, high))
+        part = None
+        for shift in range(per):
+            mixed = spread[shift]
+            for j in range(1, per):
+                mixed = jnp.where(row % per == j, spread[(j + shift) % per], mixed)
+            if shift > 0:
+                mixed = pltpu.roll(mixed, shift * cut, axis=1)
+            part = mixed if shift == 0 else jnp.where(turn == shift, mixed, part)
+        parts.append(part.astype(jnp.bfloat16))
+    out_ref[...] = jnp.dot(jnp.concatenate(parts, axis=1), weights_ref[...], preferred_element_type=jnp.float32)
+
+
 def in_hbm(array):
     return pltpu.with_memory_space_constraint(array, pltpu.HBM)
 
@@ -316,10 +343,23 @@
     )(own_spec, below, above, starts, turns, forward, inverse, gains)
 
 
+def make_pixels(lines, weights):
+    angles, cut, pixels = weights.shape
+    return pl.pallas_call(
+        partial(pixels_kernel, angles=angles),
+        out_shape=jax.ShapeDtypeStruct((SUB, pixels), jnp.float32),
+        in_specs=[VMEM] * 2,
+        out_specs=VMEM,
+        scratch_shapes=[pltpu.VMEM(lines.shape, jnp.float32)],
+        compiler_params=PARAMS,
+        name="pixels",
+    )(lines, weights.reshape(angles * cut, pixels))
+
+
 def body(projections, flats, block_start, bp_weights):
     angles_dev, rows_dev, width = projections.shape
-    assert angles_dev == 1 and rows_dev == SUB and width % (2 * LANES) == 0
     cut = bp_weights.shape[1]
+    assert angles_dev == 1 and rows_dev == SUB and width % (2 * LANES) == 0 and SUB * cut == 2 * LANES
     rows = lax.axis_size("row")
     up = [(i, i + 1) for i in range(rows - 1)]
     down = [(j, i) for i, j in up]
@@ -330,10 +370,7 @@
     own_spec, forward, inverse, gains, starts = make_own(own, turns, forward, inverse, gains, block_start)
     outgoing = make_tile(own_spec, below, above, starts, turns, forward, inverse, gains, cut)
     incoming = lax.all_to_all(outgoing, "ang", split_axis=0, concat_axis=0, tiled=True)
-    blocks = incoming.reshape(bp_weights.shape[0], rows_dev, cut)
-    return lax.dot_general(
-        blocks, bp_weights, (((0, 2), (0, 1)), ((), ())), preferred_element_type=jnp.float32
-    )
+    return make_pixels(incoming, bp_weights)
 
 
 def solution(mesh):

time: 68.5 us -> 68.4 us (level)
  matrix products: 0.85 us -> 0 us
  Pallas kernels: 3.09 us -> 3.9 us
    dot_general x1 -> x0, matrix products: 0.85 us -> none  [body(): lax.dot_general(blocks, bp_weights, (((0, 2), (0, 1)), ((), ())), preferr...]
    pallas_call x0 -> x1, Pallas kernels: none -> 0.84 us  [make_pixels(): pl.pallas_call(partial(pixels_kernel, angles=angles), out_shape=jax.Shape...]
where the time goes in v7:
time: 68.4 us; the launch traced here: 68.1 us
  blocking collectives  56.1 us (82%)
  starting transfers between devices  5.9 us (9%)
  Pallas kernels  3.9 us (6%)
  waiting for transfers between devices  2.21 us (3%)
    all_to_all x1, blocking collectives, body(): lax.all_to_all(outgoing, 'ang', split_axis=0, concat_axis=0, tiled=True)  56.1 us
    ppermute x1, starting transfers between devices, body(): above = lax.ppermute(last, 'row', up)  3.57 us
    ppermute x1, starting transfers between devices, body(): below = lax.ppermute(first, 'row', down)  2.34 us
    ppermute x1, waiting for transfers between devices, body(): above = lax.ppermute(last, 'row', up)  2.21 us
  transfers between devices with their start and end apart: 2, of which 1 were waited for; matrix products, arithmetic and copies ran while one was open for 0% of the time, Pallas kernels for 2%

profile of v7, /device:TPU:88, one launch (start us, length us, event | category | flops | bytes accessed | tf_op | source)
XLA Modules:
  0.0 68.1 jit_solution(13785535810655535669)
XLA Ops:
  0.0 0.0 copy-start.1
  0.0 0.0 copy-start.2
  0.0 1.0 %contrast.1 = (f32[8,2560]{1,0:T(8,128)S(1)}, f32[4,2560]{1,0:T(4,128)S(1)}, f32[4,2560]{1,0:T(4,128)S(1)}) custom-call(bf16[1,8,2560]{2,1,0:T(8,128)(2,1)} %proj_hbm.1, f32[8,2560]{1,0:T(8,128)} %flat_hbm.1), custom_call_target="tpu_custom_call" | custom-call | tf_op jit(solution)/shard_map/contrast/pallas_call | solution.py:297
  1.0 2.3 %collective-permute-start = (f32[4,2560]{1,0:T(4,128)S(1)}, f32[4,2560]{1,0:T(4,128)S(1)}, u32[]{:S(2)}, u32[]{:S(2)}) collective-permute-start(f32[4,2560]{1,0:T(4,128)S(1)} %get-tuple-element.15), channel_id=1, source_target_pairs={{1,0},{2,1},{3,2},{4,3},{5,4},{6,5},{7,6},{9,8},{10,9},{11,10},{12... | collective-permute-start | bytes 122888 | tf_op jit(solution)/shard_map/ppermute | solution.py:368
  3.3 3.6 %collective-permute-start.1 = (f32[4,2560]{1,0:T(4,128)S(1)}, f32[4,2560]{1,0:T(4,128)S(1)}, u32[]{:S(2)}, u32[]{:S(2)}) collective-permute-start(f32[4,2560]{1,0:T(4,128)S(1)} %get-tuple-element.16), channel_id=1, source_target_pairs={{0,1},{1,2},{2,3},{3,4},{4,5},{5,6},{6,7},{8,9},{9,10},{10,11},{11... | collective-permute-start | bytes 122888 | tf_op jit(solution)/shard_map/ppermute | solution.py:369
  6.9 0.0 copy-done.1
  6.9 0.0 copy-done.2
  6.9 1.3 %own_rows.1 = (f32[88,256]{1,0:T(8,128)S(1)}, bf16[2,256,256]{2,1,0:T(8,128)(2,1)S(1)}, bf16[2,256,256]{2,1,0:T(8,128)(2,1)S(1)}, f32[8,11,8,128]{3,2,1,0:T(8,128)S(1)}, s32[1,32]{1,0:T(1,128)S(4)}) custom-call(f32[8,2560]{1,0:T(8,128)S(1)} %get-tuple-element.13.own_ref, f32[2,11,128]{2,1,0:T(8,128)S(1)} %copy-done.2, f32[9,11,128]{2,1,0:T(8,128)S(1)} %copy-done.1, ...), custom_call_target="tpu_custom_call" | custom-call | tf_op jit(solution)/shard_map/own_rows/pallas_call | solution.py:314
  8.3 0.0 collective-permute-done.below_ref
  8.3 2.2 %collective-permute-done.1.above_ref = f32[4,2560]{1,0:T(4,128)S(1)} collective-permute-done((f32[4,2560]{1,0:T(4,128)S(1)}, f32[4,2560]{1,0:T(4,128)S(1)}, u32[]{:S(2)}, u32[]{:S(2)}) %collective-permute-start.1) | collective-permute-done | bytes 40992 | tf_op jit(solution)/shard_map/ppermute | solution.py:369
  10.5 0.0 copy-start
  10.5 0.8 %tile.1 = bf16[64,128]{1,0:T(8,128)(2,1)S(1)} custom-call(f32[88,256]{1,0:T(8,128)S(1)} %get-tuple-element.14.own_ref, f32[4,2560]{1,0:T(4,128)S(1)} %collective-permute-done.below_ref, f32[4,2560]{1,0:T(4,128)S(1)} %collective-permute-done.1.above_ref, s32[1,32]{1,0:T(1,128)S(4)} %get-tuple-element.17.starts, f32[2,11,128]{2,1,0:T(8,128)S(1)} %copy-done.2, ...), custom_call_target="tpu_custom_call" | custom-call | tf_op jit(solution)/shard_map/tile/pallas_call | solution.py:333
  11.2 56.1 %all_to_all.11 = bf16[32,2,128]{2,1,0:T(2,128)(2,1)S(1)} all-to-all(bf16[32,2,128]{2,1,0:T(2,128)(2,1)S(1)} %bitcast.4), channel_id=1, replica_groups=mesh['scan'=2,'ang'=32,'row'=8] {'ang'}, dimensions={0} | all-to-all | bytes 32768 | tf_op jit(solution)/shard_map/all_to_all | solution.py:372
  67.3 0.0 copy-done
  67.3 0.8 %pixels.1 = f32[8,256]{1,0:T(8,128)} custom-call(bf16[64,128]{1,0:T(8,128)(2,1)S(1)} %bitcast.5, bf16[1024,256]{1,0:T(8,128)(2,1)S(1)} %bitcast.3), custom_call_target="tpu_custom_call" | custom-call | tf_op jit(solution)/shard_map/pixels/pallas_call | solution.py:348
Async XLA Ops:
  0.0 6.9 %copy-start.1 = (f32[9,11,128]{2,1,0:T(8,128)S(1)}, f32[9,11,128]{2,1,0:T(8,128)}, u32[]{:S(2)}) copy-start(f32[9,11,128]{2,1,0:T(8,128)} %constant.11.clone.gains_ref) | copy-start | bytes 152068
  0.0 6.9 %copy-start.2 = (f32[2,11,128]{2,1,0:T(8,128)S(1)}, f32[2,11,128]{2,1,0:T(8,128)}, u32[]{:S(2)}) copy-start(f32[2,11,128]{2,1,0:T(8,128)} %constant.8.clone.turns_ref) | copy-start | bytes 33796
  1.0 7.3 %collective-permute-start = (f32[4,2560]{1,0:T(4,128)S(1)}, f32[4,2560]{1,0:T(4,128)S(1)}, u32[]{:S(2)}, u32[]{:S(2)}) collective-permute-start(f32[4,2560]{1,0:T(4,128)S(1)} %get-tuple-element.15), channel_id=1, source_target_pairs={{1,0},{2,1},{3,2},{4,3},{5,4},{6,5},{7,6},{9,8},{10,9},{11,10},{12... | collective-permute-start | bytes 122888 | tf_op jit(solution)/shard_map/ppermute | solution.py:368
  3.3 7.1 %collective-permute-start.1 = (f32[4,2560]{1,0:T(4,128)S(1)}, f32[4,2560]{1,0:T(4,128)S(1)}, u32[]{:S(2)}, u32[]{:S(2)}) collective-permute-start(f32[4,2560]{1,0:T(4,128)S(1)} %get-tuple-element.16), channel_id=1, source_target_pairs={{0,1},{1,2},{2,3},{3,4},{4,5},{5,6},{6,7},{8,9},{9,10},{10,11},{11... | collective-permute-start | bytes 122888 | tf_op jit(solution)/shard_map/ppermute | solution.py:369
  10.5 56.8 %copy-start = (bf16[32,32,256]{2,1,0:T(8,128)(2,1)S(1)}, bf16[32,32,256]{2,1,0:T(8,128)(2,1)}, u32[]{:S(2)}) copy-start(bf16[32,32,256]{2,1,0:T(8,128)(2,1)} %param.11) | copy-start | bytes 1572868

commit v8 on v7

--- a/solution.py
+++ b/solution.py
@@ -260,9 +260,87 @@
     out_ref[...] = out.astype(jnp.bfloat16)
 
 
-def pixels_kernel(lines_ref, weights_ref, out_ref, lines, *, angles):
-    lines[...] = lines_ref[...].astype(jnp.float32)
-    cut = lines_ref.shape[0] * LANES // SUB // angles
+class Routes:
+    UNITS = 4
+    AROUND = 16
+
+    def __init__(self, count):
+        step = count // self.AROUND
+        devices = lambda steps: [s * step + c for s in steps for c in range(step)]
+        link = lambda pairs: [p for src, dst in pairs for p in zip(devices([src]), devices([dst]))]
+        self.count, self.half = count, count // 2
+        self.near = devices((12, 13, 14, 15, 0, 1, 2, 3))
+        self.far = devices(range(4, 12))
+        self.relays = devices((12, 1, 2, 3))
+        first = link(((11, 12), (9, 3), (8, 2), (7, 1)))
+        self.enter = [first + [(dst, src) for src, dst in first], link(((10, 12), (4, 3), (5, 2), (6, 1)))]
+        self.leave = [link(((12, 11), (13, 9), (14, 7), (15, 5))), link(((12, 10), (13, 8), (14, 6), (15, 4)))]
+
+    def exchange_table(self):
+        table = np.zeros((3, self.half * self.UNITS * 2, 3 * self.count * 2), np.float32)
+
+        def put(kind, m, unit, source, region):
+            for i in range(2):
+                table[kind, (m * self.UNITS + unit) * 2 + i, (source * self.count + region) * 2 + i] = 1.0
+
+        for m, dest in enumerate(self.far):
+            put(0, m, 0, 0, dest)
+            put(0, m, 1, 1, dest)
+        for m, dest in enumerate(self.near):
+            put(1, m, 0, 0, dest)
+            put(2, m, 0, 0, dest)
+            for turn in range(2):
+                put(1, m, 1 + turn, 1 + turn, dest)
+                for src, final in self.leave[turn]:
+                    if src == dest:
+                        put(2, m, 1 + turn, 0, final)
+        return table.astype(jnp.bfloat16)
+
+    def arrival_table(self):
+        size = self.half * self.UNITS
+        table = np.zeros((3, self.count * 2, 3 * size * 2), np.float32)
+
+        def put(kind, angle, source, m, unit):
+            for i in range(2):
+                table[kind, angle * 2 + i, (source * size + m * self.UNITS + unit) * 2 + i] = 1.0
+
+        for m, angle in enumerate(self.near):
+            put(0, angle, 0, m, 0)
+            for turn in range(2):
+                for src, dst in self.enter[turn]:
+                    if dst == angle:
+                        put(0, src, 0, m, 1 + turn)
+                if angle not in self.relays:
+                    put(1 + turn, angle, 1 + turn, m, 1 + turn)
+        for m, angle in enumerate(self.far):
+            for turn in range(2):
+                put(1 + turn, angle, 0, m, 0)
+                for src, dst in self.enter[0]:
+                    if dst == angle:
+                        put(1 + turn, src, 0, m, 1)
+        return table.astype(jnp.bfloat16)
+
+    @classmethod
+    def kinds(cls, device, count):
+        step = device // (count // cls.AROUND)
+        turned = lax.rem(step + 4, cls.AROUND)
+        far = turned >= 8
+        other = (turned >= 1) & (turned <= 4)
+        return jnp.where(far, 0, jnp.where(other, 2, 1)), jnp.where(far, 2 - step % 2, 0)
+
+
+def repack_kernel(lines_ref, first_ref, second_ref, table_ref, out_ref):
+    kind, _ = Routes.kinds(lax.axis_index("ang"), lax.axis_size("ang"))
+    lines = jnp.concatenate((lines_ref[...], first_ref[...], second_ref[...]), axis=0)
+    out = jnp.dot(table_ref[kind], lines, preferred_element_type=jnp.float32)
+    out_ref[...] = out.astype(out_ref.dtype)
+
+
+def pixels_kernel(near_ref, first_ref, second_ref, table_ref, weights_ref, out_ref, lines, *, angles):
+    _, kind = Routes.kinds(lax.axis_index("ang"), lax.axis_size("ang"))
+    held = jnp.concatenate((near_ref[...], first_ref[...], second_ref[...]), axis=0)
+    lines[...] = jnp.dot(table_ref[kind], held, preferred_element_type=jnp.float32)
+    cut = lines.shape[0] * LANES // SUB // angles
     per = LANES // cut
     row = lax.broadcasted_iota(jnp.int32, (SUB, LANES), 0)
     lane = lax.broadcasted_iota(jnp.int32, (SUB, LANES), 1)
@@ -343,17 +421,28 @@
     )(own_spec, below, above, starts, turns, forward, inverse, gains)
 
 
-def make_pixels(lines, weights):
+def make_repack(lines, first, second, table):
+    return pl.pallas_call(
+        repack_kernel,
+        out_shape=jax.ShapeDtypeStruct((table.shape[1], LANES), lines.dtype),
+        in_specs=[VMEM] * 4,
+        out_specs=VMEM,
+        compiler_params=PARAMS,
+        name="repack",
+    )(lines, first, second, table)
+
+
+def make_pixels(near, first, second, table, weights):
     angles, cut, pixels = weights.shape
     return pl.pallas_call(
         partial(pixels_kernel, angles=angles),
         out_shape=jax.ShapeDtypeStruct((SUB, pixels), jnp.float32),
-        in_specs=[VMEM] * 2,
+        in_specs=[VMEM] * 5,
         out_specs=VMEM,
-        scratch_shapes=[pltpu.VMEM(lines.shape, jnp.float32)],
+        scratch_shapes=[pltpu.VMEM((table.shape[1], LANES), jnp.float32)],
         compiler_params=PARAMS,
         name="pixels",
-    )(lines, weights.reshape(angles * cut, pixels))
+    )(near, first, second, table, weights.reshape(angles * cut, pixels))
 
 
 def body(projections, flats, block_start, bp_weights):
@@ -369,8 +458,14 @@
     above = lax.ppermute(last, "row", up)
     own_spec, forward, inverse, gains, starts = make_own(own, turns, forward, inverse, gains, block_start)
     outgoing = make_tile(own_spec, below, above, starts, turns, forward, inverse, gains, cut)
-    incoming = lax.all_to_all(outgoing, "ang", split_axis=0, concat_axis=0, tiled=True)
-    return make_pixels(incoming, bp_weights)
+    routes = Routes(lax.axis_size("ang"))
+    entered = [lax.ppermute(outgoing, "ang", pairs) for pairs in routes.enter]
+    packed = make_repack(outgoing, *entered, jnp.asarray(routes.exchange_table()))
+    near = lax.all_to_all(
+        packed, "ang", split_axis=0, concat_axis=0, tiled=True, axis_index_groups=[routes.near, routes.far]
+    )
+    left = [lax.ppermute(near, "ang", pairs) for pairs in routes.leave]
+    return make_pixels(near, *left, jnp.asarray(routes.arrival_table()), bp_weights)
 
 
 def solution(mesh):

time: 68.4 us -> 69.2 us (1.012)
  the two profiles are of different devices: /device:TPU:88 before, /device:TPU:1112 now
where the time goes in v8:
time: 69.2 us; the launch traced here: 68.9 us
  blocking collectives  41 us (59%)
  waiting for transfers between devices  13.7 us (20%)
  starting transfers between devices  9.96 us (14%)
  Pallas kernels  4.2 us (6%)
    all_to_all x1, blocking collectives, body(): lax.all_to_all(packed, 'ang', split_axis=0, concat_axis=0, tiled=True, ax...  41 us
    ppermute x2, waiting for transfers between devices, body(): left = [lax.ppermute(near, 'ang', pairs) for pairs in routes.leave]  10.7 us
    ppermute x1, starting transfers between devices, body(): above = lax.ppermute(last, 'row', up)  3.57 us
    ppermute x1, starting transfers between devices, body(): below = lax.ppermute(first, 'row', down)  2.34 us
    ppermute x1, waiting for transfers between devices, body(): above = lax.ppermute(last, 'row', up)  2.2 us
    ppermute x2, starting transfers between devices, body(): entered = [lax.ppermute(outgoing, 'ang', pairs) for pairs in routes.enter]  2.1 us
    ppermute x2, starting transfers between devices, body(): left = [lax.ppermute(near, 'ang', pairs) for pairs in routes.leave]  1.96 us
  transfers between devices with their start and end apart: 6, of which 3 were waited for; matrix products, arithmetic and copies ran while one was open for 0% of the time, Pallas kernels for 2%

profile of v8, /device:TPU:1112, one launch (start us, length us, event | category | flops | bytes accessed | tf_op | source)
XLA Modules:
  0.0 68.9 jit_solution(11456788698582706552)
XLA Ops:
  0.0 0.0 copy-start.3
  0.0 0.0 copy-start.4
  0.0 1.0 %contrast.1 = (f32[8,2560]{1,0:T(8,128)S(1)}, f32[4,2560]{1,0:T(4,128)S(1)}, f32[4,2560]{1,0:T(4,128)S(1)}) custom-call(bf16[1,8,2560]{2,1,0:T(8,128)(2,1)} %proj_hbm.1, f32[8,2560]{1,0:T(8,128)} %flat_hbm.1), custom_call_target="tpu_custom_call" | custom-call | tf_op jit(solution)/shard_map/contrast/pallas_call | solution.py:375
  1.0 2.3 %collective-permute-start = (f32[4,2560]{1,0:T(4,128)S(1)}, f32[4,2560]{1,0:T(4,128)S(1)}, u32[]{:S(2)}, u32[]{:S(2)}) collective-permute-start(f32[4,2560]{1,0:T(4,128)S(1)} %get-tuple-element.15), channel_id=1, source_target_pairs={{1,0},{2,1},{3,2},{4,3},{5,4},{6,5},{7,6},{9,8},{10,9},{11,10},{12... | collective-permute-start | bytes 122888 | tf_op jit(solution)/shard_map/ppermute | solution.py:457
  3.3 3.6 %collective-permute-start.1 = (f32[4,2560]{1,0:T(4,128)S(1)}, f32[4,2560]{1,0:T(4,128)S(1)}, u32[]{:S(2)}, u32[]{:S(2)}) collective-permute-start(f32[4,2560]{1,0:T(4,128)S(1)} %get-tuple-element.16), channel_id=1, source_target_pairs={{0,1},{1,2},{2,3},{3,4},{4,5},{5,6},{6,7},{8,9},{9,10},{10,11},{11... | collective-permute-start | bytes 122888 | tf_op jit(solution)/shard_map/ppermute | solution.py:458
  6.9 0.0 copy-done.3
  6.9 0.0 copy-done.4
  6.9 1.3 %own_rows.1 = (f32[88,256]{1,0:T(8,128)S(1)}, bf16[2,256,256]{2,1,0:T(8,128)(2,1)S(1)}, bf16[2,256,256]{2,1,0:T(8,128)(2,1)S(1)}, f32[8,11,8,128]{3,2,1,0:T(8,128)S(1)}, s32[1,32]{1,0:T(1,128)S(4)}) custom-call(f32[8,2560]{1,0:T(8,128)S(1)} %get-tuple-element.13.own_ref, f32[2,11,128]{2,1,0:T(8,128)S(1)} %copy-done.4, f32[9,11,128]{2,1,0:T(8,128)S(1)} %copy-done.3, ...), custom_call_target="tpu_custom_call" | custom-call | tf_op jit(solution)/shard_map/own_rows/pallas_call | solution.py:392
  8.3 0.0 collective-permute-done.below_ref
  8.3 2.2 %collective-permute-done.1.above_ref = f32[4,2560]{1,0:T(4,128)S(1)} collective-permute-done((f32[4,2560]{1,0:T(4,128)S(1)}, f32[4,2560]{1,0:T(4,128)S(1)}, u32[]{:S(2)}, u32[]{:S(2)}) %collective-permute-start.1) | collective-permute-done | bytes 40992 | tf_op jit(solution)/shard_map/ppermute | solution.py:458
  10.5 0.0 copy-start.1
  10.5 0.0 copy-start
  10.5 0.8 %tile.1.lines_ref = bf16[64,128]{1,0:T(8,128)(2,1)S(1)} custom-call(f32[88,256]{1,0:T(8,128)S(1)} %get-tuple-element.14.own_ref, f32[4,2560]{1,0:T(4,128)S(1)} %collective-permute-done.below_ref, f32[4,2560]{1,0:T(4,128)S(1)} %collective-permute-done.1.above_ref, s32[1,32]{1,0:T(1,128)S(4)} %get-tuple-element.17.starts, f32[2,11,128]{2,1,0:T(8,128)S(1)} %copy-done.4, ...), custom_call_target="tpu_custom_call" | custom-call | tf_op jit(solution)/shard_map/tile/pallas_call | solution.py:411
  11.2 0.0 copy-start.2
  11.3 1.4 %collective-permute-start.3 = (bf16[64,128]{1,0:T(8,128)(2,1)S(1)}, bf16[64,128]{1,0:T(8,128)(2,1)S(1)}, u32[]{:S(2)}, u32[]{:S(2)}) collective-permute-start(bf16[64,128]{1,0:T(8,128)(2,1)S(1)} %tile.1.lines_ref), channel_id=1, source_target_pairs={{160,192},{168,200},{64,48},{72,56},{80,32},{88,40},{96,16},{104,2... | collective-permute-start | bytes 49160 | tf_op jit(solution)/shard_map/ppermute | solution.py:462
  12.7 0.7 collective-permute-start.2
  13.4 0.8 %collective-permute-done.3.second_ref = bf16[64,128]{1,0:T(8,128)(2,1)S(1)} collective-permute-done((bf16[64,128]{1,0:T(8,128)(2,1)S(1)}, bf16[64,128]{1,0:T(8,128)(2,1)S(1)}, u32[]{:S(2)}, u32[]{:S(2)}) %collective-permute-start.3) | collective-permute-done | bytes 16416 | tf_op jit(solution)/shard_map/ppermute | solution.py:462
  14.1 0.0 collective-permute-done.2.first_ref
  14.1 0.0 copy-done.1
  14.1 0.1 repack.1
  14.3 41.0 %all_to_all.11 = bf16[16,8,128]{2,1,0:T(8,128)(2,1)S(1)} all-to-all(bf16[16,8,128]{2,1,0:T(8,128)(2,1)S(1)} %bitcast.7), channel_id=1, replica_groups={{192,200,208,216,224,232,240,248,0,8,16,24,32,40,48,56},{64,72,80,88,96..., dimensions={0} | all-to-all | bytes 65536 | tf_op jit(solution)/shard_map/all_to_all | solution.py:464
  55.2 1.3 %collective-permute-start.5 = (bf16[128,128]{1,0:T(8,128)(2,1)S(1)}, bf16[128,128]{1,0:T(8,128)(2,1)S(1)}, u32[]{:S(2)}, u32[]{:S(2)}) collective-permute-start(bf16[128,128]{1,0:T(8,128)(2,1)S(1)} %bitcast.4), channel_id=1, source_target_pairs={{192,160},{200,168},{208,128},{216,136},{224,96},{232,104},{240,64... | collective-permute-start | bytes 98312 | tf_op jit(solution)/shard_map/ppermute | solution.py:467
  56.6 0.7 collective-permute-start.4
  57.2 10.7 %collective-permute-done.5.second_ref = bf16[128,128]{1,0:T(8,128)(2,1)S(1)} collective-permute-done((bf16[128,128]{1,0:T(8,128)(2,1)S(1)}, bf16[128,128]{1,0:T(8,128)(2,1)S(1)}, u32[]{:S(2)}, u32[]{:S(2)}) %collective-permute-start.5) | collective-permute-done | bytes 32800 | tf_op jit(solution)/shard_map/ppermute | solution.py:467
  67.9 0.0 collective-permute-done.4.first_ref
  67.9 0.0 copy-done
  67.9 0.0 copy-done.2
  67.9 1.0 %pixels.1 = f32[8,256]{1,0:T(8,128)} custom-call(bf16[128,128]{1,0:T(8,128)(2,1)S(1)} %bitcast.6, bf16[128,128]{1,0:T(8,128)(2,1)S(1)} %collective-permute-done.4.first_ref, bf16[128,128]{1,0:T(8,128)(2,1)S(1)} %collective-permute-done.5.second_ref, bf16[3,64,384]{2,1,0:T(8,128)(2,1)S(1)} %copy-done.2, bf16[1024,256]{1,0:T(8,128)(2,1)S(1)} %bitcast.3), custom_call_target="tpu_custom_call" | custom-call | tf_op jit(solution)/shard_map/pixels/pallas_call | solution.py:437
Async XLA Ops:
  0.0 6.9 %copy-start.3 = (f32[9,11,128]{2,1,0:T(8,128)S(1)}, f32[9,11,128]{2,1,0:T(8,128)}, u32[]{:S(2)}) copy-start(f32[9,11,128]{2,1,0:T(8,128)} %constant.15.clone.gains_ref) | copy-start | bytes 152068
  0.0 6.9 %copy-start.4 = (f32[2,11,128]{2,1,0:T(8,128)S(1)}, f32[2,11,128]{2,1,0:T(8,128)}, u32[]{:S(2)}) copy-start(f32[2,11,128]{2,1,0:T(8,128)} %constant.12.clone.turns_ref) | copy-start | bytes 33796
  1.0 7.3 %collective-permute-start = (f32[4,2560]{1,0:T(4,128)S(1)}, f32[4,2560]{1,0:T(4,128)S(1)}, u32[]{:S(2)}, u32[]{:S(2)}) collective-permute-start(f32[4,2560]{1,0:T(4,128)S(1)} %get-tuple-element.15), channel_id=1, source_target_pairs={{1,0},{2,1},{3,2},{4,3},{5,4},{6,5},{7,6},{9,8},{10,9},{11,10},{12... | collective-permute-start | bytes 122888 | tf_op jit(solution)/shard_map/ppermute | solution.py:457
  3.3 7.1 %collective-permute-start.1 = (f32[4,2560]{1,0:T(4,128)S(1)}, f32[4,2560]{1,0:T(4,128)S(1)}, u32[]{:S(2)}, u32[]{:S(2)}) collective-permute-start(f32[4,2560]{1,0:T(4,128)S(1)} %get-tuple-element.16), channel_id=1, source_target_pairs={{0,1},{1,2},{2,3},{3,4},{4,5},{5,6},{6,7},{8,9},{9,10},{10,11},{11... | collective-permute-start | bytes 122888 | tf_op jit(solution)/shard_map/ppermute | solution.py:458
  10.5 3.7 %copy-start.1 = (bf16[3,128,192]{2,1,0:T(8,128)(2,1)S(1)}, bf16[3,128,192]{2,1,0:T(8,128)(2,1)}, u32[]{:S(2)}) copy-start(bf16[3,128,192]{2,1,0:T(8,128)(2,1)} %constant.16.clone.table_ref) | copy-start | bytes 442372
  10.5 57.4 %copy-start = (bf16[32,32,256]{2,1,0:T(8,128)(2,1)S(1)}, bf16[32,32,256]{2,1,0:T(8,128)(2,1)}, u32[]{:S(2)}) copy-start(bf16[32,32,256]{2,1,0:T(8,128)(2,1)} %param.13) | copy-start | bytes 1572868
  11.2 56.7 %copy-start.2 = (bf16[3,64,384]{2,1,0:T(8,128)(2,1)S(1)}, bf16[3,64,384]{2,1,0:T(8,128)(2,1)}, u32[]{:S(2)}) copy-start(bf16[3,64,384]{2,1,0:T(8,128)(2,1)} %constant.17.clone.table_ref) | copy-start | bytes 442372
  11.3 2.9 %collective-permute-start.3 = (bf16[64,128]{1,0:T(8,128)(2,1)S(1)}, bf16[64,128]{1,0:T(8,128)(2,1)S(1)}, u32[]{:S(2)}, u32[]{:S(2)}) collective-permute-start(bf16[64,128]{1,0:T(8,128)(2,1)S(1)} %tile.1.lines_ref), channel_id=1, source_target_pairs={{160,192},{168,200},{64,48},{72,56},{80,32},{88,40},{96,16},{104,2... | collective-permute-start | bytes 49160 | tf_op jit(solution)/shard_map/ppermute | solution.py:462
  12.7 1.4 %collective-permute-start.2 = (bf16[64,128]{1,0:T(8,128)(2,1)S(1)}, bf16[64,128]{1,0:T(8,128)(2,1)S(1)}, u32[]{:S(2)}, u32[]{:S(2)}) collective-permute-start(bf16[64,128]{1,0:T(8,128)(2,1)S(1)} %tile.1.lines_ref), channel_id=1, source_target_pairs={{176,192},{184,200},{144,48},{152,56},{128,32},{136,40},{112,16},{... | collective-permute-start | bytes 49160 | tf_op jit(solution)/shard_map/ppermute | solution.py:462
  55.2 12.7 %collective-permute-start.5 = (bf16[128,128]{1,0:T(8,128)(2,1)S(1)}, bf16[128,128]{1,0:T(8,128)(2,1)S(1)}, u32[]{:S(2)}, u32[]{:S(2)}) collective-permute-start(bf16[128,128]{1,0:T(8,128)(2,1)S(1)} %bitcast.4), channel_id=1, source_target_pairs={{192,160},{200,168},{208,128},{216,136},{224,96},{232,104},{240,64... | collective-permute-start | bytes 98312 | tf_op jit(solution)/shard_map/ppermute | solution.py:467
  56.6 11.4 %collective-permute-start.4 = (bf16[128,128]{1,0:T(8,128)(2,1)S(1)}, bf16[128,128]{1,0:T(8,128)(2,1)S(1)}, u32[]{:S(2)}, u32[]{:S(2)}) collective-permute-start(bf16[128,128]{1,0:T(8,128)(2,1)S(1)} %bitcast.5), channel_id=1, source_target_pairs={{192,176},{200,184},{208,144},{216,152},{224,112},{232,120},{240,8... | collective-permute-start | bytes 98312 | tf_op jit(solution)/shard_map/ppermute | solution.py:467

commit v9 on v8

--- a/solution.py
+++ b/solution.py
@@ -274,7 +274,7 @@
         self.relays = devices((12, 1, 2, 3))
         first = link(((11, 12), (9, 3), (8, 2), (7, 1)))
         self.enter = [first + [(dst, src) for src, dst in first], link(((10, 12), (4, 3), (5, 2), (6, 1)))]
-        self.leave = [link(((12, 11), (13, 9), (14, 7), (15, 5))), link(((12, 10), (13, 8), (14, 6), (15, 4)))]
+        self.leave = [link(((12, 11), (13, 9), (2, 6), (3, 4))), link(((12, 10), (13, 8), (2, 7), (3, 5)))]
 
     def exchange_table(self):
         table = np.zeros((3, self.half * self.UNITS * 2, 3 * self.count * 2), np.float32)
@@ -326,7 +326,7 @@
         turned = lax.rem(step + 4, cls.AROUND)
         far = turned >= 8
         other = (turned >= 1) & (turned <= 4)
-        return jnp.where(far, 0, jnp.where(other, 2, 1)), jnp.where(far, 2 - step % 2, 0)
+        return jnp.where(far, 0, jnp.where(other, 2, 1)), jnp.where(far, 1 + (step + step // 8) % 2, 0)
 
 
 def repack_kernel(lines_ref, first_ref, second_ref, table_ref, out_ref):

time: 69.2 us -> 70 us (1.012)
  the two profiles are of different devices: /device:TPU:1112 before, /device:TPU:600 now
where the time goes in v9:
time: 70 us; the launch traced here: 69.7 us
  starting transfers between devices  42.4 us (61%)
  blocking collectives  17.4 us (25%)
  waiting for transfers between devices  5.48 us (8%)
  Pallas kernels  4.2 us (6%)
    ppermute x2, starting transfers between devices, body(): entered = [lax.ppermute(outgoing, 'ang', pairs) for pairs in routes.enter]  26.9 us
    all_to_all x1, blocking collectives, body(): lax.all_to_all(packed, 'ang', split_axis=0, concat_axis=0, tiled=True, ax...  17.4 us
    ppermute x2, starting transfers between devices, body(): left = [lax.ppermute(near, 'ang', pairs) for pairs in routes.leave]  9.62 us
    ppermute x1, starting transfers between devices, body(): above = lax.ppermute(last, 'row', up)  3.57 us
    ppermute x1, starting transfers between devices, body(): below = lax.ppermute(first, 'row', down)  2.34 us
    ppermute x1, waiting for transfers between devices, body(): above = lax.ppermute(last, 'row', up)  2.21 us
    ppermute x2, waiting for transfers between devices, body(): entered = [lax.ppermute(outgoing, 'ang', pairs) for pairs in routes.enter]  1.69 us
    ppermute x2, waiting for transfers between devices, body(): left = [lax.ppermute(near, 'ang', pairs) for pairs in routes.leave]  1.58 us
  transfers between devices with their start and end apart: 6, of which 4 were waited for; matrix products, arithmetic and copies ran while one was open for 0% of the time, Pallas kernels for 2%

profile of v9, /device:TPU:600, one launch (start us, length us, event | category | flops | bytes accessed | tf_op | source)
XLA Modules:
  0.0 69.7 jit_solution(10462933921589978674)
XLA Ops:
  0.0 0.0 copy-start.3
  0.0 0.0 copy-start.4
  0.0 1.0 %contrast.1 = (f32[8,2560]{1,0:T(8,128)S(1)}, f32[4,2560]{1,0:T(4,128)S(1)}, f32[4,2560]{1,0:T(4,128)S(1)}) custom-call(bf16[1,8,2560]{2,1,0:T(8,128)(2,1)} %proj_hbm.1, f32[8,2560]{1,0:T(8,128)} %flat_hbm.1), custom_call_target="tpu_custom_call" | custom-call | tf_op jit(solution)/shard_map/contrast/pallas_call | solution.py:375
  1.0 2.3 %collective-permute-start = (f32[4,2560]{1,0:T(4,128)S(1)}, f32[4,2560]{1,0:T(4,128)S(1)}, u32[]{:S(2)}, u32[]{:S(2)}) collective-permute-start(f32[4,2560]{1,0:T(4,128)S(1)} %get-tuple-element.15), channel_id=1, source_target_pairs={{1,0},{2,1},{3,2},{4,3},{5,4},{6,5},{7,6},{9,8},{10,9},{11,10},{12... | collective-permute-start | bytes 122888 | tf_op jit(solution)/shard_map/ppermute | solution.py:457
  3.3 3.6 %collective-permute-start.1 = (f32[4,2560]{1,0:T(4,128)S(1)}, f32[4,2560]{1,0:T(4,128)S(1)}, u32[]{:S(2)}, u32[]{:S(2)}) collective-permute-start(f32[4,2560]{1,0:T(4,128)S(1)} %get-tuple-element.16), channel_id=1, source_target_pairs={{0,1},{1,2},{2,3},{3,4},{4,5},{5,6},{6,7},{8,9},{9,10},{10,11},{11... | collective-permute-start | bytes 122888 | tf_op jit(solution)/shard_map/ppermute | solution.py:458
  6.9 0.0 copy-done.3
  6.9 0.0 copy-done.4
  6.9 1.3 %own_rows.1 = (f32[88,256]{1,0:T(8,128)S(1)}, bf16[2,256,256]{2,1,0:T(8,128)(2,1)S(1)}, bf16[2,256,256]{2,1,0:T(8,128)(2,1)S(1)}, f32[8,11,8,128]{3,2,1,0:T(8,128)S(1)}, s32[1,32]{1,0:T(1,128)S(4)}) custom-call(f32[8,2560]{1,0:T(8,128)S(1)} %get-tuple-element.13.own_ref, f32[2,11,128]{2,1,0:T(8,128)S(1)} %copy-done.4, f32[9,11,128]{2,1,0:T(8,128)S(1)} %copy-done.3, ...), custom_call_target="tpu_custom_call" | custom-call | tf_op jit(solution)/shard_map/own_rows/pallas_call | solution.py:392
  8.3 0.0 collective-permute-done.below_ref
  8.3 2.2 %collective-permute-done.1.above_ref = f32[4,2560]{1,0:T(4,128)S(1)} collective-permute-done((f32[4,2560]{1,0:T(4,128)S(1)}, f32[4,2560]{1,0:T(4,128)S(1)}, u32[]{:S(2)}, u32[]{:S(2)}) %collective-permute-start.1) | collective-permute-done | bytes 40992 | tf_op jit(solution)/shard_map/ppermute | solution.py:458
  10.5 0.0 copy-start.1
  10.5 0.0 copy-start
  10.5 0.8 %tile.1.lines_ref = bf16[64,128]{1,0:T(8,128)(2,1)S(1)} custom-call(f32[88,256]{1,0:T(8,128)S(1)} %get-tuple-element.14.own_ref, f32[4,2560]{1,0:T(4,128)S(1)} %collective-permute-done.below_ref, f32[4,2560]{1,0:T(4,128)S(1)} %collective-permute-done.1.above_ref, s32[1,32]{1,0:T(1,128)S(4)} %get-tuple-element.17.starts, f32[2,11,128]{2,1,0:T(8,128)S(1)} %copy-done.4, ...), custom_call_target="tpu_custom_call" | custom-call | tf_op jit(solution)/shard_map/tile/pallas_call | solution.py:411
  11.2 0.0 copy-start.2
  11.3 1.4 %collective-permute-start.3 = (bf16[64,128]{1,0:T(8,128)(2,1)S(1)}, bf16[64,128]{1,0:T(8,128)(2,1)S(1)}, u32[]{:S(2)}, u32[]{:S(2)}) collective-permute-start(bf16[64,128]{1,0:T(8,128)(2,1)S(1)} %tile.1.lines_ref), channel_id=1, source_target_pairs={{160,192},{168,200},{64,48},{72,56},{80,32},{88,40},{96,16},{104,2... | collective-permute-start | bytes 49160 | tf_op jit(solution)/shard_map/ppermute | solution.py:462
  12.7 25.4 %collective-permute-start.2 = (bf16[64,128]{1,0:T(8,128)(2,1)S(1)}, bf16[64,128]{1,0:T(8,128)(2,1)S(1)}, u32[]{:S(2)}, u32[]{:S(2)}) collective-permute-start(bf16[64,128]{1,0:T(8,128)(2,1)S(1)} %tile.1.lines_ref), channel_id=1, source_target_pairs={{176,192},{184,200},{144,48},{152,56},{128,32},{136,40},{112,16},{... | collective-permute-start | bytes 49160 | tf_op jit(solution)/shard_map/ppermute | solution.py:462
  38.2 0.0 collective-permute-done.3.second_ref
  38.2 1.7 %collective-permute-done.2.first_ref = bf16[64,128]{1,0:T(8,128)(2,1)S(1)} collective-permute-done((bf16[64,128]{1,0:T(8,128)(2,1)S(1)}, bf16[64,128]{1,0:T(8,128)(2,1)S(1)}, u32[]{:S(2)}, u32[]{:S(2)}) %collective-permute-start.2) | collective-permute-done | bytes 16416 | tf_op jit(solution)/shard_map/ppermute | solution.py:462
  39.9 0.0 copy-done.1
  39.9 0.1 repack.1
  40.0 17.4 %all_to_all.11 = bf16[16,8,128]{2,1,0:T(8,128)(2,1)S(1)} all-to-all(bf16[16,8,128]{2,1,0:T(8,128)(2,1)S(1)} %bitcast.7), channel_id=1, replica_groups={{192,200,208,216,224,232,240,248,0,8,16,24,32,40,48,56},{64,72,80,88,96..., dimensions={0} | all-to-all | bytes 65536 | tf_op jit(solution)/shard_map/all_to_all | solution.py:464
  57.4 8.3 %collective-permute-start.5 = (bf16[128,128]{1,0:T(8,128)(2,1)S(1)}, bf16[128,128]{1,0:T(8,128)(2,1)S(1)}, u32[]{:S(2)}, u32[]{:S(2)}) collective-permute-start(bf16[128,128]{1,0:T(8,128)(2,1)S(1)} %bitcast.4), channel_id=1, source_target_pairs={{192,160},{200,168},{208,128},{216,136},{32,112},{40,120},{48,80},... | collective-permute-start | bytes 98312 | tf_op jit(solution)/shard_map/ppermute | solution.py:467
  65.8 1.3 %collective-permute-start.4 = (bf16[128,128]{1,0:T(8,128)(2,1)S(1)}, bf16[128,128]{1,0:T(8,128)(2,1)S(1)}, u32[]{:S(2)}, u32[]{:S(2)}) collective-permute-start(bf16[128,128]{1,0:T(8,128)(2,1)S(1)} %bitcast.5), channel_id=1, source_target_pairs={{192,176},{200,184},{208,144},{216,152},{32,96},{40,104},{48,64},{... | collective-permute-start | bytes 98312 | tf_op jit(solution)/shard_map/ppermute | solution.py:467
  67.1 0.3 collective-permute-done.5.second_ref
  67.3 1.3 %collective-permute-done.4.first_ref = bf16[128,128]{1,0:T(8,128)(2,1)S(1)} collective-permute-done((bf16[128,128]{1,0:T(8,128)(2,1)S(1)}, bf16[128,128]{1,0:T(8,128)(2,1)S(1)}, u32[]{:S(2)}, u32[]{:S(2)}) %collective-permute-start.4) | collective-permute-done | bytes 32800 | tf_op jit(solution)/shard_map/ppermute | solution.py:467
  68.7 0.0 copy-done
  68.7 0.0 copy-done.2
  68.7 1.0 %pixels.1 = f32[8,256]{1,0:T(8,128)} custom-call(bf16[128,128]{1,0:T(8,128)(2,1)S(1)} %bitcast.6, bf16[128,128]{1,0:T(8,128)(2,1)S(1)} %collective-permute-done.4.first_ref, bf16[128,128]{1,0:T(8,128)(2,1)S(1)} %collective-permute-done.5.second_ref, bf16[3,64,384]{2,1,0:T(8,128)(2,1)S(1)} %copy-done.2, bf16[1024,256]{1,0:T(8,128)(2,1)S(1)} %bitcast.3), custom_call_target="tpu_custom_call" | custom-call | tf_op jit(solution)/shard_map/pixels/pallas_call | solution.py:437
Async XLA Ops:
  0.0 6.9 %copy-start.3 = (f32[9,11,128]{2,1,0:T(8,128)S(1)}, f32[9,11,128]{2,1,0:T(8,128)}, u32[]{:S(2)}) copy-start(f32[9,11,128]{2,1,0:T(8,128)} %constant.15.clone.gains_ref) | copy-start | bytes 152068
  0.0 6.9 %copy-start.4 = (f32[2,11,128]{2,1,0:T(8,128)S(1)}, f32[2,11,128]{2,1,0:T(8,128)}, u32[]{:S(2)}) copy-start(f32[2,11,128]{2,1,0:T(8,128)} %constant.12.clone.turns_ref) | copy-start | bytes 33796
  1.0 7.3 %collective-permute-start = (f32[4,2560]{1,0:T(4,128)S(1)}, f32[4,2560]{1,0:T(4,128)S(1)}, u32[]{:S(2)}, u32[]{:S(2)}) collective-permute-start(f32[4,2560]{1,0:T(4,128)S(1)} %get-tuple-element.15), channel_id=1, source_target_pairs={{1,0},{2,1},{3,2},{4,3},{5,4},{6,5},{7,6},{9,8},{10,9},{11,10},{12... | collective-permute-start | bytes 122888 | tf_op jit(solution)/shard_map/ppermute | solution.py:457
  3.3 7.1 %collective-permute-start.1 = (f32[4,2560]{1,0:T(4,128)S(1)}, f32[4,2560]{1,0:T(4,128)S(1)}, u32[]{:S(2)}, u32[]{:S(2)}) collective-permute-start(f32[4,2560]{1,0:T(4,128)S(1)} %get-tuple-element.16), channel_id=1, source_target_pairs={{0,1},{1,2},{2,3},{3,4},{4,5},{5,6},{6,7},{8,9},{9,10},{10,11},{11... | collective-permute-start | bytes 122888 | tf_op jit(solution)/shard_map/ppermute | solution.py:458
  10.5 29.4 %copy-start.1 = (bf16[3,128,192]{2,1,0:T(8,128)(2,1)S(1)}, bf16[3,128,192]{2,1,0:T(8,128)(2,1)}, u32[]{:S(2)}) copy-start(bf16[3,128,192]{2,1,0:T(8,128)(2,1)} %constant.16.clone.table_ref) | copy-start | bytes 442372
  10.5 58.2 %copy-start = (bf16[32,32,256]{2,1,0:T(8,128)(2,1)S(1)}, bf16[32,32,256]{2,1,0:T(8,128)(2,1)}, u32[]{:S(2)}) copy-start(bf16[32,32,256]{2,1,0:T(8,128)(2,1)} %param.13) | copy-start | bytes 1572868
  11.2 57.4 %copy-start.2 = (bf16[3,64,384]{2,1,0:T(8,128)(2,1)S(1)}, bf16[3,64,384]{2,1,0:T(8,128)(2,1)}, u32[]{:S(2)}) copy-start(bf16[3,64,384]{2,1,0:T(8,128)(2,1)} %constant.17.clone.table_ref) | copy-start | bytes 442372
  11.3 26.9 %collective-permute-start.3 = (bf16[64,128]{1,0:T(8,128)(2,1)S(1)}, bf16[64,128]{1,0:T(8,128)(2,1)S(1)}, u32[]{:S(2)}, u32[]{:S(2)}) collective-permute-start(bf16[64,128]{1,0:T(8,128)(2,1)S(1)} %tile.1.lines_ref), channel_id=1, source_target_pairs={{160,192},{168,200},{64,48},{72,56},{80,32},{88,40},{96,16},{104,2... | collective-permute-start | bytes 49160 | tf_op jit(solution)/shard_map/ppermute | solution.py:462
  12.7 27.1 %collective-permute-start.2 = (bf16[64,128]{1,0:T(8,128)(2,1)S(1)}, bf16[64,128]{1,0:T(8,128)(2,1)S(1)}, u32[]{:S(2)}, u32[]{:S(2)}) collective-permute-start(bf16[64,128]{1,0:T(8,128)(2,1)S(1)} %tile.1.lines_ref), channel_id=1, source_target_pairs={{176,192},{184,200},{144,48},{152,56},{128,32},{136,40},{112,16},{... | collective-permute-start | bytes 49160 | tf_op jit(solution)/shard_map/ppermute | solution.py:462
  57.4 9.9 %collective-permute-start.5 = (bf16[128,128]{1,0:T(8,128)(2,1)S(1)}, bf16[128,128]{1,0:T(8,128)(2,1)S(1)}, u32[]{:S(2)}, u32[]{:S(2)}) collective-permute-start(bf16[128,128]{1,0:T(8,128)(2,1)S(1)} %bitcast.4), channel_id=1, source_target_pairs={{192,160},{200,168},{208,128},{216,136},{32,112},{40,120},{48,80},... | collective-permute-start | bytes 98312 | tf_op jit(solution)/shard_map/ppermute | solution.py:467
  65.8 2.9 %collective-permute-start.4 = (bf16[128,128]{1,0:T(8,128)(2,1)S(1)}, bf16[128,128]{1,0:T(8,128)(2,1)S(1)}, u32[]{:S(2)}, u32[]{:S(2)}) collective-permute-start(bf16[128,128]{1,0:T(8,128)(2,1)S(1)} %bitcast.5), channel_id=1, source_target_pairs={{192,176},{200,184},{208,144},{216,152},{32,96},{40,104},{48,64},{... | collective-permute-start | bytes 98312 | tf_op jit(solution)/shard_map/ppermute | solution.py:467

commit v10 on v9

--- a/solution.py
+++ b/solution.py
@@ -272,9 +272,9 @@
         self.near = devices((12, 13, 14, 15, 0, 1, 2, 3))
         self.far = devices(range(4, 12))
         self.relays = devices((12, 1, 2, 3))
-        first = link(((11, 12), (9, 3), (8, 2), (7, 1)))
-        self.enter = [first + [(dst, src) for src, dst in first], link(((10, 12), (4, 3), (5, 2), (6, 1)))]
-        self.leave = [link(((12, 11), (13, 9), (2, 6), (3, 4))), link(((12, 10), (13, 8), (2, 7), (3, 5)))]
+        first = link(((11, 12), (4, 3), (5, 2), (6, 1)))
+        self.enter = [first + [(dst, src) for src, dst in first], link(((10, 12), (9, 3), (8, 2), (7, 1)))]
+        self.leave = [link(((12, 11), (13, 9), (14, 7), (3, 4))), link(((12, 10), (13, 8), (14, 6), (3, 5)))]
 
     def exchange_table(self):
         table = np.zeros((3, self.half * self.UNITS * 2, 3 * self.count * 2), np.float32)
@@ -326,7 +326,8 @@
         turned = lax.rem(step + 4, cls.AROUND)
         far = turned >= 8
         other = (turned >= 1) & (turned <= 4)
-        return jnp.where(far, 0, jnp.where(other, 2, 1)), jnp.where(far, 1 + (step + step // 8) % 2, 0)
+        early = (step == 4) | ((step > 6) & (step % 2 == 1))
+        return jnp.where(far, 0, jnp.where(other, 2, 1)), jnp.where(far, jnp.where(early, 1, 2), 0)
 
 
 def repack_kernel(lines_ref, first_ref, second_ref, table_ref, out_ref):

time: 70 us -> 67.3 us (0.961)
  the two profiles are of different devices: /device:TPU:600 before, /device:TPU:88 now
where the time goes in v10:
time: 67.3 us; the launch traced here: 66.8 us
  blocking collectives  51.5 us (77%)
  starting transfers between devices  8.67 us (13%)
  Pallas kernels  4.21 us (6%)
  waiting for transfers between devices  2.21 us (3%)
    all_to_all x1, blocking collectives, body(): lax.all_to_all(packed, 'ang', split_axis=0, concat_axis=0, tiled=True, ax...  51.5 us
    ppermute x1, starting transfers between devices, body(): above = lax.ppermute(last, 'row', up)  3.57 us
    ppermute x1, starting transfers between devices, body(): below = lax.ppermute(first, 'row', down)  2.34 us
    ppermute x1, waiting for transfers between devices, body(): above = lax.ppermute(last, 'row', up)  2.2 us
    ppermute x2, starting transfers between devices, body(): entered = [lax.ppermute(outgoing, 'ang', pairs) for pairs in routes.enter]  1.46 us
  transfers between devices with their start and end apart: 6, of which 1 were waited for; matrix products, arithmetic and copies ran while one was open for 0% of the time, Pallas kernels for 2%

profile of v10, /device:TPU:88, one launch (start us, length us, event | category | flops | bytes accessed | tf_op | source)
XLA Modules:
  0.0 66.8 jit_solution(5174535653379969696)
XLA Ops:
  0.0 0.0 copy-start.3
  0.0 0.0 copy-start.4
  0.0 1.0 %contrast.1 = (f32[8,2560]{1,0:T(8,128)S(1)}, f32[4,2560]{1,0:T(4,128)S(1)}, f32[4,2560]{1,0:T(4,128)S(1)}) custom-call(bf16[1,8,2560]{2,1,0:T(8,128)(2,1)} %proj_hbm.1, f32[8,2560]{1,0:T(8,128)} %flat_hbm.1), custom_call_target="tpu_custom_call" | custom-call | tf_op jit(solution)/shard_map/contrast/pallas_call | solution.py:376
  1.0 2.3 %collective-permute-start = (f32[4,2560]{1,0:T(4,128)S(1)}, f32[4,2560]{1,0:T(4,128)S(1)}, u32[]{:S(2)}, u32[]{:S(2)}) collective-permute-start(f32[4,2560]{1,0:T(4,128)S(1)} %get-tuple-element.15), channel_id=1, source_target_pairs={{1,0},{2,1},{3,2},{4,3},{5,4},{6,5},{7,6},{9,8},{10,9},{11,10},{12... | collective-permute-start | bytes 122888 | tf_op jit(solution)/shard_map/ppermute | solution.py:458
  3.3 3.6 %collective-permute-start.1 = (f32[4,2560]{1,0:T(4,128)S(1)}, f32[4,2560]{1,0:T(4,128)S(1)}, u32[]{:S(2)}, u32[]{:S(2)}) collective-permute-start(f32[4,2560]{1,0:T(4,128)S(1)} %get-tuple-element.16), channel_id=1, source_target_pairs={{0,1},{1,2},{2,3},{3,4},{4,5},{5,6},{6,7},{8,9},{9,10},{10,11},{11... | collective-permute-start | bytes 122888 | tf_op jit(solution)/shard_map/ppermute | solution.py:459
  6.9 0.0 copy-done.3
  6.9 0.0 copy-done.4
  6.9 1.3 %own_rows.1 = (f32[88,256]{1,0:T(8,128)S(1)}, bf16[2,256,256]{2,1,0:T(8,128)(2,1)S(1)}, bf16[2,256,256]{2,1,0:T(8,128)(2,1)S(1)}, f32[8,11,8,128]{3,2,1,0:T(8,128)S(1)}, s32[1,32]{1,0:T(1,128)S(4)}) custom-call(f32[8,2560]{1,0:T(8,128)S(1)} %get-tuple-element.13.own_ref, f32[2,11,128]{2,1,0:T(8,128)S(1)} %copy-done.4, f32[9,11,128]{2,1,0:T(8,128)S(1)} %copy-done.3, ...), custom_call_target="tpu_custom_call" | custom-call | tf_op jit(solution)/shard_map/own_rows/pallas_call | solution.py:393
  8.3 0.0 collective-permute-done.below_ref
  8.3 2.2 %collective-permute-done.1.above_ref = f32[4,2560]{1,0:T(4,128)S(1)} collective-permute-done((f32[4,2560]{1,0:T(4,128)S(1)}, f32[4,2560]{1,0:T(4,128)S(1)}, u32[]{:S(2)}, u32[]{:S(2)}) %collective-permute-start.1) | collective-permute-done | bytes 40992 | tf_op jit(solution)/shard_map/ppermute | solution.py:459
  10.5 0.0 copy-start.1
  10.5 0.0 copy-start
  10.5 0.8 %tile.1.lines_ref = bf16[64,128]{1,0:T(8,128)(2,1)S(1)} custom-call(f32[88,256]{1,0:T(8,128)S(1)} %get-tuple-element.14.own_ref, f32[4,2560]{1,0:T(4,128)S(1)} %collective-permute-done.below_ref, f32[4,2560]{1,0:T(4,128)S(1)} %collective-permute-done.1.above_ref, s32[1,32]{1,0:T(1,128)S(4)} %get-tuple-element.17.starts, f32[2,11,128]{2,1,0:T(8,128)S(1)} %copy-done.4, ...), custom_call_target="tpu_custom_call" | custom-call | tf_op jit(solution)/shard_map/tile/pallas_call | solution.py:412
  11.2 0.0 copy-start.2
  11.3 0.8 %collective-permute-start.3 = (bf16[64,128]{1,0:T(8,128)(2,1)S(1)}, bf16[64,128]{1,0:T(8,128)(2,1)S(1)}, u32[]{:S(2)}, u32[]{:S(2)}) collective-permute-start(bf16[64,128]{1,0:T(8,128)(2,1)S(1)} %tile.1.lines_ref), channel_id=1, source_target_pairs={{160,192},{168,200},{144,48},{152,56},{128,32},{136,40},{112,16},{... | collective-permute-start | bytes 49160 | tf_op jit(solution)/shard_map/ppermute | solution.py:463
  12.1 0.7 collective-permute-start.2
  12.7 0.0 collective-permute-done.3.second_ref
  12.7 0.0 collective-permute-done.2.first_ref
  12.8 0.0 copy-done.1
  12.8 0.1 repack.1
  12.9 51.5 %all_to_all.11 = bf16[16,8,128]{2,1,0:T(8,128)(2,1)S(1)} all-to-all(bf16[16,8,128]{2,1,0:T(8,128)(2,1)S(1)} %bitcast.7), channel_id=1, replica_groups={{192,200,208,216,224,232,240,248,0,8,16,24,32,40,48,56},{64,72,80,88,96..., dimensions={0} | all-to-all | bytes 65536 | tf_op jit(solution)/shard_map/all_to_all | solution.py:465
  64.5 0.7 collective-permute-start.5
  65.1 0.7 collective-permute-start.4
  65.8 0.0 collective-permute-done.5.second_ref
  65.8 0.0 collective-permute-done.4.first_ref
  65.8 0.0 copy-done
  65.8 0.0 copy-done.2
  65.8 1.0 %pixels.1 = f32[8,256]{1,0:T(8,128)} custom-call(bf16[128,128]{1,0:T(8,128)(2,1)S(1)} %bitcast.6, bf16[128,128]{1,0:T(8,128)(2,1)S(1)} %collective-permute-done.4.first_ref, bf16[128,128]{1,0:T(8,128)(2,1)S(1)} %collective-permute-done.5.second_ref, bf16[3,64,384]{2,1,0:T(8,128)(2,1)S(1)} %copy-done.2, bf16[1024,256]{1,0:T(8,128)(2,1)S(1)} %bitcast.3), custom_call_target="tpu_custom_call" | custom-call | tf_op jit(solution)/shard_map/pixels/pallas_call | solution.py:438
Async XLA Ops:
  0.0 6.9 %copy-start.3 = (f32[9,11,128]{2,1,0:T(8,128)S(1)}, f32[9,11,128]{2,1,0:T(8,128)}, u32[]{:S(2)}) copy-start(f32[9,11,128]{2,1,0:T(8,128)} %constant.15.clone.gains_ref) | copy-start | bytes 152068
  0.0 6.9 %copy-start.4 = (f32[2,11,128]{2,1,0:T(8,128)S(1)}, f32[2,11,128]{2,1,0:T(8,128)}, u32[]{:S(2)}) copy-start(f32[2,11,128]{2,1,0:T(8,128)} %constant.12.clone.turns_ref) | copy-start | bytes 33796
  1.0 7.3 %collective-permute-start = (f32[4,2560]{1,0:T(4,128)S(1)}, f32[4,2560]{1,0:T(4,128)S(1)}, u32[]{:S(2)}, u32[]{:S(2)}) collective-permute-start(f32[4,2560]{1,0:T(4,128)S(1)} %get-tuple-element.15), channel_id=1, source_target_pairs={{1,0},{2,1},{3,2},{4,3},{5,4},{6,5},{7,6},{9,8},{10,9},{11,10},{12... | collective-permute-start | bytes 122888 | tf_op jit(solution)/shard_map/ppermute | solution.py:458
  3.3 7.1 %collective-permute-start.1 = (f32[4,2560]{1,0:T(4,128)S(1)}, f32[4,2560]{1,0:T(4,128)S(1)}, u32[]{:S(2)}, u32[]{:S(2)}) collective-permute-start(f32[4,2560]{1,0:T(4,128)S(1)} %get-tuple-element.16), channel_id=1, source_target_pairs={{0,1},{1,2},{2,3},{3,4},{4,5},{5,6},{6,7},{8,9},{9,10},{10,11},{11... | collective-permute-start | bytes 122888 | tf_op jit(solution)/shard_map/ppermute | solution.py:459
  10.5 2.3 %copy-start.1 = (bf16[3,128,192]{2,1,0:T(8,128)(2,1)S(1)}, bf16[3,128,192]{2,1,0:T(8,128)(2,1)}, u32[]{:S(2)}) copy-start(bf16[3,128,192]{2,1,0:T(8,128)(2,1)} %constant.16.clone.table_ref) | copy-start | bytes 442372
  10.5 55.3 %copy-start = (bf16[32,32,256]{2,1,0:T(8,128)(2,1)S(1)}, bf16[32,32,256]{2,1,0:T(8,128)(2,1)}, u32[]{:S(2)}) copy-start(bf16[32,32,256]{2,1,0:T(8,128)(2,1)} %param.13) | copy-start | bytes 1572868
  11.2 54.6 %copy-start.2 = (bf16[3,64,384]{2,1,0:T(8,128)(2,1)S(1)}, bf16[3,64,384]{2,1,0:T(8,128)(2,1)}, u32[]{:S(2)}) copy-start(bf16[3,64,384]{2,1,0:T(8,128)(2,1)} %constant.17.clone.table_ref) | copy-start | bytes 442372
  11.3 1.5 %collective-permute-start.3 = (bf16[64,128]{1,0:T(8,128)(2,1)S(1)}, bf16[64,128]{1,0:T(8,128)(2,1)S(1)}, u32[]{:S(2)}, u32[]{:S(2)}) collective-permute-start(bf16[64,128]{1,0:T(8,128)(2,1)S(1)} %tile.1.lines_ref), channel_id=1, source_target_pairs={{160,192},{168,200},{144,48},{152,56},{128,32},{136,40},{112,16},{... | collective-permute-start | bytes 49160 | tf_op jit(solution)/shard_map/ppermute | solution.py:463
  12.1 0.7 %collective-permute-start.2 = (bf16[64,128]{1,0:T(8,128)(2,1)S(1)}, bf16[64,128]{1,0:T(8,128)(2,1)S(1)}, u32[]{:S(2)}, u32[]{:S(2)}) collective-permute-start(bf16[64,128]{1,0:T(8,128)(2,1)S(1)} %tile.1.lines_ref), channel_id=1, source_target_pairs={{176,192},{184,200},{64,48},{72,56},{80,32},{88,40},{96,16},{104,2... | collective-permute-start | bytes 49160 | tf_op jit(solution)/shard_map/ppermute | solution.py:463
  64.5 1.3 %collective-permute-start.5 = (bf16[128,128]{1,0:T(8,128)(2,1)S(1)}, bf16[128,128]{1,0:T(8,128)(2,1)S(1)}, u32[]{:S(2)}, u32[]{:S(2)}) collective-permute-start(bf16[128,128]{1,0:T(8,128)(2,1)S(1)} %bitcast.4), channel_id=1, source_target_pairs={{192,160},{200,168},{208,128},{216,136},{224,96},{232,104},{48,80}... | collective-permute-start | bytes 98312 | tf_op jit(solution)/shard_map/ppermute | solution.py:468
  65.1 0.7 %collective-permute-start.4 = (bf16[128,128]{1,0:T(8,128)(2,1)S(1)}, bf16[128,128]{1,0:T(8,128)(2,1)S(1)}, u32[]{:S(2)}, u32[]{:S(2)}) collective-permute-start(bf16[128,128]{1,0:T(8,128)(2,1)S(1)} %bitcast.5), channel_id=1, source_target_pairs={{192,176},{200,184},{208,144},{216,152},{224,112},{232,120},{48,64... | collective-permute-start | bytes 98312 | tf_op jit(solution)/shard_map/ppermute | solution.py:468

commit v11 on v10

--- a/solution.py
+++ b/solution.py
@@ -261,7 +261,7 @@
 
 
 class Routes:
-    UNITS = 4
+    UNITS = 3
     AROUND = 16
 
     def __init__(self, count):
@@ -463,8 +463,9 @@
     entered = [lax.ppermute(outgoing, "ang", pairs) for pairs in routes.enter]
     packed = make_repack(outgoing, *entered, jnp.asarray(routes.exchange_table()))
     near = lax.all_to_all(
-        packed, "ang", split_axis=0, concat_axis=0, tiled=True, axis_index_groups=[routes.near, routes.far]
-    )
+        packed.reshape(-1, 2, LANES), "ang", split_axis=0, concat_axis=0, tiled=True,
+        axis_index_groups=[routes.near, routes.far],
+    ).reshape(packed.shape)
     left = [lax.ppermute(near, "ang", pairs) for pairs in routes.leave]
     return make_pixels(near, *left, jnp.asarray(routes.arrival_table()), bp_weights)
 

time: 67.3 us -> 67.3 us (level)
  the two profiles are of different devices: /device:TPU:88 before, /device:TPU:73 now
where the time goes in v11:
time: 67.3 us; the launch traced here: 67 us
  blocking collectives  53.2 us (79%)
  starting transfers between devices  8.11 us (12%)
  Pallas kernels  4.21 us (6%)
  waiting for transfers between devices  1.35 us (2%)
    all_to_all x1, blocking collectives, body(): lax.all_to_all(packed.reshape(-1, 2, LANES), 'ang', split_axis=0, concat_...  53.2 us
    ppermute x1, starting transfers between devices, body(): above = lax.ppermute(last, 'row', up)  3.29 us
    ppermute x1, starting transfers between devices, body(): below = lax.ppermute(first, 'row', down)  2.06 us
    ppermute x2, starting transfers between devices, body(): entered = [lax.ppermute(outgoing, 'ang', pairs) for pairs in routes.enter]  1.46 us
  transfers between devices with their start and end apart: 6, of which 1 were waited for; matrix products, arithmetic and copies ran while one was open for 0% of the time, Pallas kernels for 2%

profile of v11, /device:TPU:73, one launch (start us, length us, event | category | flops | bytes accessed | tf_op | source)
XLA Modules:
  0.0 67.0 jit_solution(9930517114990248881)
XLA Ops:
  0.0 0.0 copy-start.3
  0.0 0.0 copy-start.4
  0.0 1.0 %contrast.1 = (f32[8,2560]{1,0:T(8,128)S(1)}, f32[4,2560]{1,0:T(4,128)S(1)}, f32[4,2560]{1,0:T(4,128)S(1)}) custom-call(bf16[1,8,2560]{2,1,0:T(8,128)(2,1)} %proj_hbm.1, f32[8,2560]{1,0:T(8,128)} %flat_hbm.1), custom_call_target="tpu_custom_call" | custom-call | tf_op jit(solution)/shard_map/contrast/pallas_call | solution.py:376
  1.0 2.1 %collective-permute-start = (f32[4,2560]{1,0:T(4,128)S(1)}, f32[4,2560]{1,0:T(4,128)S(1)}, u32[]{:S(2)}, u32[]{:S(2)}) collective-permute-start(f32[4,2560]{1,0:T(4,128)S(1)} %get-tuple-element.15), channel_id=1, source_target_pairs={{1,0},{2,1},{3,2},{4,3},{5,4},{6,5},{7,6},{9,8},{10,9},{11,10},{12... | collective-permute-start | bytes 122888 | tf_op jit(solution)/shard_map/ppermute | solution.py:458
  3.1 3.3 %collective-permute-start.1 = (f32[4,2560]{1,0:T(4,128)S(1)}, f32[4,2560]{1,0:T(4,128)S(1)}, u32[]{:S(2)}, u32[]{:S(2)}) collective-permute-start(f32[4,2560]{1,0:T(4,128)S(1)} %get-tuple-element.16), channel_id=1, source_target_pairs={{0,1},{1,2},{2,3},{3,4},{4,5},{5,6},{6,7},{8,9},{9,10},{10,11},{11... | collective-permute-start | bytes 122888 | tf_op jit(solution)/shard_map/ppermute | solution.py:459
  6.4 0.0 copy-done.3
  6.4 0.0 copy-done.4
  6.4 1.3 %own_rows.1 = (f32[88,256]{1,0:T(8,128)S(1)}, bf16[2,256,256]{2,1,0:T(8,128)(2,1)S(1)}, bf16[2,256,256]{2,1,0:T(8,128)(2,1)S(1)}, f32[8,11,8,128]{3,2,1,0:T(8,128)S(1)}, s32[1,32]{1,0:T(1,128)S(4)}) custom-call(f32[8,2560]{1,0:T(8,128)S(1)} %get-tuple-element.13.own_ref, f32[2,11,128]{2,1,0:T(8,128)S(1)} %copy-done.4, f32[9,11,128]{2,1,0:T(8,128)S(1)} %copy-done.3, ...), custom_call_target="tpu_custom_call" | custom-call | tf_op jit(solution)/shard_map/own_rows/pallas_call | solution.py:393
  7.7 0.0 collective-permute-done.below_ref
  7.7 1.3 %collective-permute-done.1.above_ref = f32[4,2560]{1,0:T(4,128)S(1)} collective-permute-done((f32[4,2560]{1,0:T(4,128)S(1)}, f32[4,2560]{1,0:T(4,128)S(1)}, u32[]{:S(2)}, u32[]{:S(2)}) %collective-permute-start.1) | collective-permute-done | bytes 40992 | tf_op jit(solution)/shard_map/ppermute | solution.py:459
  9.0 0.0 copy-start.1
  9.0 0.0 copy-start
  9.1 0.8 %tile.1.lines_ref = bf16[64,128]{1,0:T(8,128)(2,1)S(1)} custom-call(f32[88,256]{1,0:T(8,128)S(1)} %get-tuple-element.14.own_ref, f32[4,2560]{1,0:T(4,128)S(1)} %collective-permute-done.below_ref, f32[4,2560]{1,0:T(4,128)S(1)} %collective-permute-done.1.above_ref, s32[1,32]{1,0:T(1,128)S(4)} %get-tuple-element.17.starts, f32[2,11,128]{2,1,0:T(8,128)S(1)} %copy-done.4, ...), custom_call_target="tpu_custom_call" | custom-call | tf_op jit(solution)/shard_map/tile/pallas_call | solution.py:412
  9.8 0.0 copy-start.2
  9.8 0.8 %collective-permute-start.3 = (bf16[64,128]{1,0:T(8,128)(2,1)S(1)}, bf16[64,128]{1,0:T(8,128)(2,1)S(1)}, u32[]{:S(2)}, u32[]{:S(2)}) collective-permute-start(bf16[64,128]{1,0:T(8,128)(2,1)S(1)} %tile.1.lines_ref), channel_id=1, source_target_pairs={{160,192},{168,200},{144,48},{152,56},{128,32},{136,40},{112,16},{... | collective-permute-start | bytes 49160 | tf_op jit(solution)/shard_map/ppermute | solution.py:463
  10.6 0.7 collective-permute-start.2
  11.3 0.0 collective-permute-done.3.second_ref
  11.3 0.0 collective-permute-done.2.first_ref
  11.3 0.0 copy-done.1
  11.3 0.1 repack.1
  11.5 53.2 %all_to_all.5 = bf16[48,2,128]{2,1,0:T(2,128)(2,1)S(1)} all-to-all(bf16[48,2,128]{2,1,0:T(2,128)(2,1)S(1)} %bitcast.7), channel_id=1, replica_groups={{192,200,208,216,224,232,240,248,0,8,16,24,32,40,48,56},{64,72,80,88,96..., dimensions={0} | all-to-all | bytes 49152 | tf_op jit(solution)/shard_map/all_to_all | solution.py:465
  64.6 0.7 collective-permute-start.5
  65.3 0.7 collective-permute-start.4
  66.0 0.0 collective-permute-done.5.second_ref
  66.0 0.0 collective-permute-done.4.first_ref
  66.0 0.0 copy-done
  66.0 0.0 copy-done.2
  66.0 1.0 %pixels.1 = f32[8,256]{1,0:T(8,128)} custom-call(bf16[96,128]{1,0:T(8,128)(2,1)S(1)} %bitcast.6, bf16[96,128]{1,0:T(8,128)(2,1)S(1)} %collective-permute-done.4.first_ref, bf16[96,128]{1,0:T(8,128)(2,1)S(1)} %collective-permute-done.5.second_ref, bf16[3,64,288]{2,1,0:T(8,128)(2,1)S(1)} %copy-done.2, bf16[1024,256]{1,0:T(8,128)(2,1)S(1)} %bitcast.3), custom_call_target="tpu_custom_call" | custom-call | tf_op jit(solution)/shard_map/pixels/pallas_call | solution.py:438
Async XLA Ops:
  0.0 6.4 %copy-start.3 = (f32[9,11,128]{2,1,0:T(8,128)S(1)}, f32[9,11,128]{2,1,0:T(8,128)}, u32[]{:S(2)}) copy-start(f32[9,11,128]{2,1,0:T(8,128)} %constant.15.clone.gains_ref) | copy-start | bytes 152068
  0.0 6.4 %copy-start.4 = (f32[2,11,128]{2,1,0:T(8,128)S(1)}, f32[2,11,128]{2,1,0:T(8,128)}, u32[]{:S(2)}) copy-start(f32[2,11,128]{2,1,0:T(8,128)} %constant.12.clone.turns_ref) | copy-start | bytes 33796
  1.0 6.7 %collective-permute-start = (f32[4,2560]{1,0:T(4,128)S(1)}, f32[4,2560]{1,0:T(4,128)S(1)}, u32[]{:S(2)}, u32[]{:S(2)}) collective-permute-start(f32[4,2560]{1,0:T(4,128)S(1)} %get-tuple-element.15), channel_id=1, source_target_pairs={{1,0},{2,1},{3,2},{4,3},{5,4},{6,5},{7,6},{9,8},{10,9},{11,10},{12... | collective-permute-start | bytes 122888 | tf_op jit(solution)/shard_map/ppermute | solution.py:458
  3.1 6.0 %collective-permute-start.1 = (f32[4,2560]{1,0:T(4,128)S(1)}, f32[4,2560]{1,0:T(4,128)S(1)}, u32[]{:S(2)}, u32[]{:S(2)}) collective-permute-start(f32[4,2560]{1,0:T(4,128)S(1)} %get-tuple-element.16), channel_id=1, source_target_pairs={{0,1},{1,2},{2,3},{3,4},{4,5},{5,6},{6,7},{8,9},{9,10},{10,11},{11... | collective-permute-start | bytes 122888 | tf_op jit(solution)/shard_map/ppermute | solution.py:459
  9.0 2.3 %copy-start.1 = (bf16[3,96,192]{2,1,0:T(8,128)(2,1)S(1)}, bf16[3,96,192]{2,1,0:T(8,128)(2,1)}, u32[]{:S(2)}) copy-start(bf16[3,96,192]{2,1,0:T(8,128)(2,1)} %constant.16.clone.table_ref) | copy-start | bytes 331780
  9.0 56.9 %copy-start = (bf16[32,32,256]{2,1,0:T(8,128)(2,1)S(1)}, bf16[32,32,256]{2,1,0:T(8,128)(2,1)}, u32[]{:S(2)}) copy-start(bf16[32,32,256]{2,1,0:T(8,128)(2,1)} %param.13) | copy-start | bytes 1572868
  9.8 56.2 %copy-start.2 = (bf16[3,64,288]{2,1,0:T(8,128)(2,1)S(1)}, bf16[3,64,288]{2,1,0:T(8,128)(2,1)}, u32[]{:S(2)}) copy-start(bf16[3,64,288]{2,1,0:T(8,128)(2,1)} %constant.17.clone.table_ref) | copy-start | bytes 331780
  9.8 1.5 %collective-permute-start.3 = (bf16[64,128]{1,0:T(8,128)(2,1)S(1)}, bf16[64,128]{1,0:T(8,128)(2,1)S(1)}, u32[]{:S(2)}, u32[]{:S(2)}) collective-permute-start(bf16[64,128]{1,0:T(8,128)(2,1)S(1)} %tile.1.lines_ref), channel_id=1, source_target_pairs={{160,192},{168,200},{144,48},{152,56},{128,32},{136,40},{112,16},{... | collective-permute-start | bytes 49160 | tf_op jit(solution)/shard_map/ppermute | solution.py:463
  10.6 0.7 %collective-permute-start.2 = (bf16[64,128]{1,0:T(8,128)(2,1)S(1)}, bf16[64,128]{1,0:T(8,128)(2,1)S(1)}, u32[]{:S(2)}, u32[]{:S(2)}) collective-permute-start(bf16[64,128]{1,0:T(8,128)(2,1)S(1)} %tile.1.lines_ref), channel_id=1, source_target_pairs={{176,192},{184,200},{64,48},{72,56},{80,32},{88,40},{96,16},{104,2... | collective-permute-start | bytes 49160 | tf_op jit(solution)/shard_map/ppermute | solution.py:463
  64.6 1.3 %collective-permute-start.5 = (bf16[96,128]{1,0:T(8,128)(2,1)S(1)}, bf16[96,128]{1,0:T(8,128)(2,1)S(1)}, u32[]{:S(2)}, u32[]{:S(2)}) collective-permute-start(bf16[96,128]{1,0:T(8,128)(2,1)S(1)} %bitcast.4), channel_id=1, source_target_pairs={{192,160},{200,168},{208,128},{216,136},{224,96},{232,104},{48,80}... | collective-permute-start | bytes 73736 | tf_op jit(solution)/shard_map/ppermute | solution.py:469
  65.3 0.7 %collective-permute-start.4 = (bf16[96,128]{1,0:T(8,128)(2,1)S(1)}, bf16[96,128]{1,0:T(8,128)(2,1)S(1)}, u32[]{:S(2)}, u32[]{:S(2)}) collective-permute-start(bf16[96,128]{1,0:T(8,128)(2,1)S(1)} %bitcast.5), channel_id=1, source_target_pairs={{192,176},{200,184},{208,144},{216,152},{224,112},{232,120},{48,64... | collective-permute-start | bytes 73736 | tf_op jit(solution)/shard_map/ppermute | solution.py:469

commit v12 on v11

--- a/solution.py
+++ b/solution.py
@@ -261,7 +261,7 @@
 
 
 class Routes:
-    UNITS = 3
+    UNITS = 4
     AROUND = 16
 
     def __init__(self, count):
@@ -271,13 +271,16 @@
         self.count, self.half = count, count // 2
         self.near = devices((12, 13, 14, 15, 0, 1, 2, 3))
         self.far = devices(range(4, 12))
-        self.relays = devices((12, 1, 2, 3))
-        first = link(((11, 12), (4, 3), (5, 2), (6, 1)))
-        self.enter = [first + [(dst, src) for src, dst in first], link(((10, 12), (9, 3), (8, 2), (7, 1)))]
+        self.relays = devices((1, 2, 3))
+        self.enter = [
+            link(((11, 1), (9, 2), (7, 3))),
+            link(((10, 1), (8, 2), (6, 3))),
+            link(((5, 2), (4, 3), (1, 6), (2, 5), (3, 4))),
+        ]
         self.leave = [link(((12, 11), (13, 9), (14, 7), (3, 4))), link(((12, 10), (13, 8), (14, 6), (3, 5)))]
 
     def exchange_table(self):
-        table = np.zeros((3, self.half * self.UNITS * 2, 3 * self.count * 2), np.float32)
+        table = np.zeros((3, self.half * self.UNITS * 2, (1 + len(self.enter)) * self.count * 2), np.float32)
 
         def put(kind, m, unit, source, region):
             for i in range(2):
@@ -285,12 +288,13 @@
 
         for m, dest in enumerate(self.far):
             put(0, m, 0, 0, dest)
-            put(0, m, 1, 1, dest)
+            put(0, m, 1, len(self.enter), dest)
         for m, dest in enumerate(self.near):
             put(1, m, 0, 0, dest)
             put(2, m, 0, 0, dest)
-            for turn in range(2):
+            for turn in range(len(self.enter)):
                 put(1, m, 1 + turn, 1 + turn, dest)
+            for turn in range(len(self.leave)):
                 for src, final in self.leave[turn]:
                     if src == dest:
                         put(2, m, 1 + turn, 0, final)
@@ -306,16 +310,17 @@
 
         for m, angle in enumerate(self.near):
             put(0, angle, 0, m, 0)
-            for turn in range(2):
+            for turn in range(len(self.enter)):
                 for src, dst in self.enter[turn]:
                     if dst == angle:
                         put(0, src, 0, m, 1 + turn)
+            for turn in range(len(self.leave)):
                 if angle not in self.relays:
                     put(1 + turn, angle, 1 + turn, m, 1 + turn)
         for m, angle in enumerate(self.far):
-            for turn in range(2):
+            for turn in range(len(self.leave)):
                 put(1 + turn, angle, 0, m, 0)
-                for src, dst in self.enter[0]:
+                for src, dst in self.enter[-1]:
                     if dst == angle:
                         put(1 + turn, src, 0, m, 1)
         return table.astype(jnp.bfloat16)
@@ -325,14 +330,14 @@
         step = device // (count // cls.AROUND)
         turned = lax.rem(step + 4, cls.AROUND)
         far = turned >= 8
-        other = (turned >= 1) & (turned <= 4)
+        other = turned <= 4
         early = (step == 4) | ((step > 6) & (step % 2 == 1))
         return jnp.where(far, 0, jnp.where(other, 2, 1)), jnp.where(far, jnp.where(early, 1, 2), 0)
 
 
-def repack_kernel(lines_ref, first_ref, second_ref, table_ref, out_ref):
+def repack_kernel(lines_ref, first_ref, second_ref, third_ref, table_ref, out_ref):
     kind, _ = Routes.kinds(lax.axis_index("ang"), lax.axis_size("ang"))
-    lines = jnp.concatenate((lines_ref[...], first_ref[...], second_ref[...]), axis=0)
+    lines = jnp.concatenate((lines_ref[...], first_ref[...], second_ref[...], third_ref[...]), axis=0)
     out = jnp.dot(table_ref[kind], lines, preferred_element_type=jnp.float32)
     out_ref[...] = out.astype(out_ref.dtype)
 
@@ -422,15 +427,15 @@
     )(own_spec, below, above, starts, turns, forward, inverse, gains)
 
 
-def make_repack(lines, first, second, table):
+def make_repack(lines, first, second, third, table):
     return pl.pallas_call(
         repack_kernel,
         out_shape=jax.ShapeDtypeStruct((table.shape[1], LANES), lines.dtype),
-        in_specs=[VMEM] * 4,
+        in_specs=[VMEM] * 5,
         out_specs=VMEM,
         compiler_params=PARAMS,
         name="repack",
-    )(lines, first, second, table)
+    )(lines, first, second, third, table)
 
 
 def make_pixels(near, first, second, table, weights):

time: 67.3 us -> 68.2 us (1.013)
  the two profiles are of different devices: /device:TPU:73 before, /device:TPU:88 now
where the time goes in v12:
time: 68.2 us; the launch traced here: 67.7 us
  blocking collectives  51.7 us (76%)
  starting transfers between devices  9.34 us (14%)
  Pallas kernels  4.22 us (6%)
  waiting for transfers between devices  2.22 us (3%)
    all_to_all x1, blocking collectives, body(): lax.all_to_all(packed.reshape(-1, 2, LANES), 'ang', split_axis=0, concat_...  51.7 us
    ppermute x1, starting transfers between devices, body(): above = lax.ppermute(last, 'row', up)  3.57 us
    ppermute x1, starting transfers between devices, body(): below = lax.ppermute(first, 'row', down)  2.34 us
    ppermute x1, waiting for transfers between devices, body(): above = lax.ppermute(last, 'row', up)  2.2 us
    ppermute x3, starting transfers between devices, body(): entered = [lax.ppermute(outgoing, 'ang', pairs) for pairs in routes.enter]  2.12 us
  transfers between devices with their start and end apart: 7, of which 1 were waited for; matrix products, arithmetic and copies ran while one was open for 0% of the time, Pallas kernels for 2%

profile of v12, /device:TPU:88, one launch (start us, length us, event | category | flops | bytes accessed | tf_op | source)
XLA Modules:
  0.0 67.7 jit_solution(15755704504604437732)
XLA Ops:
  0.0 0.0 copy-start.3
  0.0 0.0 copy-start.4
  0.0 1.0 %contrast.1 = (f32[8,2560]{1,0:T(8,128)S(1)}, f32[4,2560]{1,0:T(4,128)S(1)}, f32[4,2560]{1,0:T(4,128)S(1)}) custom-call(bf16[1,8,2560]{2,1,0:T(8,128)(2,1)} %proj_hbm.1, f32[8,2560]{1,0:T(8,128)} %flat_hbm.1), custom_call_target="tpu_custom_call" | custom-call | tf_op jit(solution)/shard_map/contrast/pallas_call | solution.py:381
  1.0 2.3 %collective-permute-start = (f32[4,2560]{1,0:T(4,128)S(1)}, f32[4,2560]{1,0:T(4,128)S(1)}, u32[]{:S(2)}, u32[]{:S(2)}) collective-permute-start(f32[4,2560]{1,0:T(4,128)S(1)} %get-tuple-element.15), channel_id=1, source_target_pairs={{1,0},{2,1},{3,2},{4,3},{5,4},{6,5},{7,6},{9,8},{10,9},{11,10},{12... | collective-permute-start | bytes 122888 | tf_op jit(solution)/shard_map/ppermute | solution.py:463
  3.3 3.6 %collective-permute-start.1 = (f32[4,2560]{1,0:T(4,128)S(1)}, f32[4,2560]{1,0:T(4,128)S(1)}, u32[]{:S(2)}, u32[]{:S(2)}) collective-permute-start(f32[4,2560]{1,0:T(4,128)S(1)} %get-tuple-element.16), channel_id=1, source_target_pairs={{0,1},{1,2},{2,3},{3,4},{4,5},{5,6},{6,7},{8,9},{9,10},{10,11},{11... | collective-permute-start | bytes 122888 | tf_op jit(solution)/shard_map/ppermute | solution.py:464
  6.9 0.0 copy-done.3
  6.9 0.0 copy-done.4
  6.9 1.3 %own_rows.1 = (f32[88,256]{1,0:T(8,128)S(1)}, bf16[2,256,256]{2,1,0:T(8,128)(2,1)S(1)}, bf16[2,256,256]{2,1,0:T(8,128)(2,1)S(1)}, f32[8,11,8,128]{3,2,1,0:T(8,128)S(1)}, s32[1,32]{1,0:T(1,128)S(4)}) custom-call(f32[8,2560]{1,0:T(8,128)S(1)} %get-tuple-element.13.own_ref, f32[2,11,128]{2,1,0:T(8,128)S(1)} %copy-done.4, f32[9,11,128]{2,1,0:T(8,128)S(1)} %copy-done.3, ...), custom_call_target="tpu_custom_call" | custom-call | tf_op jit(solution)/shard_map/own_rows/pallas_call | solution.py:398
  8.3 0.0 collective-permute-done.below_ref
  8.3 2.2 %collective-permute-done.1.above_ref = f32[4,2560]{1,0:T(4,128)S(1)} collective-permute-done((f32[4,2560]{1,0:T(4,128)S(1)}, f32[4,2560]{1,0:T(4,128)S(1)}, u32[]{:S(2)}, u32[]{:S(2)}) %collective-permute-start.1) | collective-permute-done | bytes 40992 | tf_op jit(solution)/shard_map/ppermute | solution.py:464
  10.5 0.0 copy-start.1
  10.5 0.0 copy-start
  10.5 0.8 %tile.1.lines_ref = bf16[64,128]{1,0:T(8,128)(2,1)S(1)} custom-call(f32[88,256]{1,0:T(8,128)S(1)} %get-tuple-element.14.own_ref, f32[4,2560]{1,0:T(4,128)S(1)} %collective-permute-done.below_ref, f32[4,2560]{1,0:T(4,128)S(1)} %collective-permute-done.1.above_ref, s32[1,32]{1,0:T(1,128)S(4)} %get-tuple-element.17.starts, f32[2,11,128]{2,1,0:T(8,128)S(1)} %copy-done.4, ...), custom_call_target="tpu_custom_call" | custom-call | tf_op jit(solution)/shard_map/tile/pallas_call | solution.py:417
  11.2 0.0 copy-start.2
  11.3 0.8 %collective-permute-start.4 = (bf16[64,128]{1,0:T(8,128)(2,1)S(1)}, bf16[64,128]{1,0:T(8,128)(2,1)S(1)}, u32[]{:S(2)}, u32[]{:S(2)}) collective-permute-start(bf16[64,128]{1,0:T(8,128)(2,1)S(1)} %tile.1.lines_ref), channel_id=1, source_target_pairs={{80,32},{88,40},{64,48},{72,56},{16,96},{24,104},{32,80},{40,88},{... | collective-permute-start | bytes 49160 | tf_op jit(solution)/shard_map/ppermute | solution.py:468
  12.1 0.7 collective-permute-start.3
  12.7 0.7 collective-permute-start.2
  13.4 0.0 collective-permute-done.4.third_ref
  13.4 0.0 collective-permute-done.3.second_ref
  13.4 0.0 collective-permute-done.2.first_ref
  13.4 0.0 copy-done.1
  13.4 0.2 repack.1
  13.6 51.7 %all_to_all.5 = bf16[64,2,128]{2,1,0:T(2,128)(2,1)S(1)} all-to-all(bf16[64,2,128]{2,1,0:T(2,128)(2,1)S(1)} %bitcast.7), channel_id=1, replica_groups={{192,200,208,216,224,232,240,248,0,8,16,24,32,40,48,56},{64,72,80,88,96..., dimensions={0} | all-to-all | bytes 65536 | tf_op jit(solution)/shard_map/all_to_all | solution.py:470
  65.3 0.7 collective-permute-start.6
  66.0 0.7 collective-permute-start.5
  66.6 0.0 collective-permute-done.6.second_ref
  66.6 0.0 collective-permute-done.5.first_ref
  66.7 0.0 copy-done
  66.7 0.0 copy-done.2
  66.7 1.0 %pixels.1 = f32[8,256]{1,0:T(8,128)} custom-call(bf16[128,128]{1,0:T(8,128)(2,1)S(1)} %bitcast.6, bf16[128,128]{1,0:T(8,128)(2,1)S(1)} %collective-permute-done.5.first_ref, bf16[128,128]{1,0:T(8,128)(2,1)S(1)} %collective-permute-done.6.second_ref, bf16[3,64,384]{2,1,0:T(8,128)(2,1)S(1)} %copy-done.2, bf16[1024,256]{1,0:T(8,128)(2,1)S(1)} %bitcast.3), custom_call_target="tpu_custom_call" | custom-call | tf_op jit(solution)/shard_map/pixels/pallas_call | solution.py:443
Async XLA Ops:
  0.0 6.9 %copy-start.3 = (f32[9,11,128]{2,1,0:T(8,128)S(1)}, f32[9,11,128]{2,1,0:T(8,128)}, u32[]{:S(2)}) copy-start(f32[9,11,128]{2,1,0:T(8,128)} %constant.15.clone.gains_ref) | copy-start | bytes 152068
  0.0 6.9 %copy-start.4 = (f32[2,11,128]{2,1,0:T(8,128)S(1)}, f32[2,11,128]{2,1,0:T(8,128)}, u32[]{:S(2)}) copy-start(f32[2,11,128]{2,1,0:T(8,128)} %constant.12.clone.turns_ref) | copy-start | bytes 33796
  1.0 7.3 %collective-permute-start = (f32[4,2560]{1,0:T(4,128)S(1)}, f32[4,2560]{1,0:T(4,128)S(1)}, u32[]{:S(2)}, u32[]{:S(2)}) collective-permute-start(f32[4,2560]{1,0:T(4,128)S(1)} %get-tuple-element.15), channel_id=1, source_target_pairs={{1,0},{2,1},{3,2},{4,3},{5,4},{6,5},{7,6},{9,8},{10,9},{11,10},{12... | collective-permute-start | bytes 122888 | tf_op jit(solution)/shard_map/ppermute | solution.py:463
  3.3 7.1 %collective-permute-start.1 = (f32[4,2560]{1,0:T(4,128)S(1)}, f32[4,2560]{1,0:T(4,128)S(1)}, u32[]{:S(2)}, u32[]{:S(2)}) collective-permute-start(f32[4,2560]{1,0:T(4,128)S(1)} %get-tuple-element.16), channel_id=1, source_target_pairs={{0,1},{1,2},{2,3},{3,4},{4,5},{5,6},{6,7},{8,9},{9,10},{10,11},{11... | collective-permute-start | bytes 122888 | tf_op jit(solution)/shard_map/ppermute | solution.py:464
  10.5 3.0 %copy-start.1 = (bf16[3,128,256]{2,1,0:T(8,128)(2,1)S(1)}, bf16[3,128,256]{2,1,0:T(8,128)(2,1)}, u32[]{:S(2)}) copy-start(bf16[3,128,256]{2,1,0:T(8,128)(2,1)} %constant.16.clone.table_ref) | copy-start | bytes 589828
  10.5 56.2 %copy-start = (bf16[32,32,256]{2,1,0:T(8,128)(2,1)S(1)}, bf16[32,32,256]{2,1,0:T(8,128)(2,1)}, u32[]{:S(2)}) copy-start(bf16[32,32,256]{2,1,0:T(8,128)(2,1)} %param.13) | copy-start | bytes 1572868
  11.2 55.4 %copy-start.2 = (bf16[3,64,384]{2,1,0:T(8,128)(2,1)S(1)}, bf16[3,64,384]{2,1,0:T(8,128)(2,1)}, u32[]{:S(2)}) copy-start(bf16[3,64,384]{2,1,0:T(8,128)(2,1)} %constant.17.clone.table_ref) | copy-start | bytes 442372
  11.3 2.1 %collective-permute-start.4 = (bf16[64,128]{1,0:T(8,128)(2,1)S(1)}, bf16[64,128]{1,0:T(8,128)(2,1)S(1)}, u32[]{:S(2)}, u32[]{:S(2)}) collective-permute-start(bf16[64,128]{1,0:T(8,128)(2,1)S(1)} %tile.1.lines_ref), channel_id=1, source_target_pairs={{80,32},{88,40},{64,48},{72,56},{16,96},{24,104},{32,80},{40,88},{... | collective-permute-start | bytes 49160 | tf_op jit(solution)/shard_map/ppermute | solution.py:468
  12.1 1.4 %collective-permute-start.3 = (bf16[64,128]{1,0:T(8,128)(2,1)S(1)}, bf16[64,128]{1,0:T(8,128)(2,1)S(1)}, u32[]{:S(2)}, u32[]{:S(2)}) collective-permute-start(bf16[64,128]{1,0:T(8,128)(2,1)S(1)} %tile.1.lines_ref), channel_id=1, source_target_pairs={{160,16},{168,24},{128,32},{136,40},{96,48},{104,56},{161,17},{169... | collective-permute-start | bytes 49160 | tf_op jit(solution)/shard_map/ppermute | solution.py:468
  12.7 0.7 %collective-permute-start.2 = (bf16[64,128]{1,0:T(8,128)(2,1)S(1)}, bf16[64,128]{1,0:T(8,128)(2,1)S(1)}, u32[]{:S(2)}, u32[]{:S(2)}) collective-permute-start(bf16[64,128]{1,0:T(8,128)(2,1)S(1)} %tile.1.lines_ref), channel_id=1, source_target_pairs={{176,16},{184,24},{144,32},{152,40},{112,48},{120,56},{177,17},{18... | collective-permute-start | bytes 49160 | tf_op jit(solution)/shard_map/ppermute | solution.py:468
  65.3 1.3 %collective-permute-start.6 = (bf16[128,128]{1,0:T(8,128)(2,1)S(1)}, bf16[128,128]{1,0:T(8,128)(2,1)S(1)}, u32[]{:S(2)}, u32[]{:S(2)}) collective-permute-start(bf16[128,128]{1,0:T(8,128)(2,1)S(1)} %bitcast.4), channel_id=1, source_target_pairs={{192,160},{200,168},{208,128},{216,136},{224,96},{232,104},{48,80}... | collective-permute-start | bytes 98312 | tf_op jit(solution)/shard_map/ppermute | solution.py:474
  66.0 0.7 %collective-permute-start.5 = (bf16[128,128]{1,0:T(8,128)(2,1)S(1)}, bf16[128,128]{1,0:T(8,128)(2,1)S(1)}, u32[]{:S(2)}, u32[]{:S(2)}) collective-permute-start(bf16[128,128]{1,0:T(8,128)(2,1)S(1)} %bitcast.5), channel_id=1, source_target_pairs={{192,176},{200,184},{208,144},{216,152},{224,112},{232,120},{48,64... | collective-permute-start | bytes 98312 | tf_op jit(solution)/shard_map/ppermute | solution.py:474

commit v13 on v11

--- a/solution.py
+++ b/solution.py
@@ -269,8 +269,8 @@
         devices = lambda steps: [s * step + c for s in steps for c in range(step)]
         link = lambda pairs: [p for src, dst in pairs for p in zip(devices([src]), devices([dst]))]
         self.count, self.half = count, count // 2
-        self.near = devices((12, 13, 14, 15, 0, 1, 2, 3))
-        self.far = devices(range(4, 12))
+        self.near = devices((12, 13, 14, 15, 3, 2, 1, 0))
+        self.far = devices((11, 10, 9, 8, 7, 6, 5, 4))
         self.relays = devices((12, 1, 2, 3))
         first = link(((11, 12), (4, 3), (5, 2), (6, 1)))
         self.enter = [first + [(dst, src) for src, dst in first], link(((10, 12), (9, 3), (8, 2), (7, 1)))]

time: 67.3 us -> 67.3 us (level)
  the two profiles are of different devices: /device:TPU:73 before, /device:TPU:88 now
where the time goes in v13:
time: 67.3 us; the launch traced here: 66.8 us
  blocking collectives  51.5 us (77%)
  starting transfers between devices  8.67 us (13%)
  Pallas kernels  4.21 us (6%)
  waiting for transfers between devices  2.21 us (3%)
    all_to_all x1, blocking collectives, body(): lax.all_to_all(packed.reshape(-1, 2, LANES), 'ang', split_axis=0, concat_...  51.5 us
    ppermute x1, starting transfers between devices, body(): above = lax.ppermute(last, 'row', up)  3.57 us
    ppermute x1, starting transfers between devices, body(): below = lax.ppermute(first, 'row', down)  2.34 us
    ppermute x1, waiting for transfers between devices, body(): above = lax.ppermute(last, 'row', up)  2.2 us
    ppermute x2, starting transfers between devices, body(): entered = [lax.ppermute(outgoing, 'ang', pairs) for pairs in routes.enter]  1.46 us
  transfers between devices with their start and end apart: 6, of which 1 were waited for; matrix products, arithmetic and copies ran while one was open for 0% of the time, Pallas kernels for 2%

profile of v13, /device:TPU:88, one launch (start us, length us, event | category | flops | bytes accessed | tf_op | source)
XLA Modules:
  0.0 66.8 jit_solution(11553132455962463238)
XLA Ops:
  0.0 0.0 copy-start.3
  0.0 0.0 copy-start.4
  0.0 1.0 %contrast.1 = (f32[8,2560]{1,0:T(8,128)S(1)}, f32[4,2560]{1,0:T(4,128)S(1)}, f32[4,2560]{1,0:T(4,128)S(1)}) custom-call(bf16[1,8,2560]{2,1,0:T(8,128)(2,1)} %proj_hbm.1, f32[8,2560]{1,0:T(8,128)} %flat_hbm.1), custom_call_target="tpu_custom_call" | custom-call | tf_op jit(solution)/shard_map/contrast/pallas_call | solution.py:376
  1.0 2.3 %collective-permute-start = (f32[4,2560]{1,0:T(4,128)S(1)}, f32[4,2560]{1,0:T(4,128)S(1)}, u32[]{:S(2)}, u32[]{:S(2)}) collective-permute-start(f32[4,2560]{1,0:T(4,128)S(1)} %get-tuple-element.15), channel_id=1, source_target_pairs={{1,0},{2,1},{3,2},{4,3},{5,4},{6,5},{7,6},{9,8},{10,9},{11,10},{12... | collective-permute-start | bytes 122888 | tf_op jit(solution)/shard_map/ppermute | solution.py:458
  3.3 3.6 %collective-permute-start.1 = (f32[4,2560]{1,0:T(4,128)S(1)}, f32[4,2560]{1,0:T(4,128)S(1)}, u32[]{:S(2)}, u32[]{:S(2)}) collective-permute-start(f32[4,2560]{1,0:T(4,128)S(1)} %get-tuple-element.16), channel_id=1, source_target_pairs={{0,1},{1,2},{2,3},{3,4},{4,5},{5,6},{6,7},{8,9},{9,10},{10,11},{11... | collective-permute-start | bytes 122888 | tf_op jit(solution)/shard_map/ppermute | solution.py:459
  6.9 0.0 copy-done.3
  6.9 0.0 copy-done.4
  6.9 1.3 %own_rows.1 = (f32[88,256]{1,0:T(8,128)S(1)}, bf16[2,256,256]{2,1,0:T(8,128)(2,1)S(1)}, bf16[2,256,256]{2,1,0:T(8,128)(2,1)S(1)}, f32[8,11,8,128]{3,2,1,0:T(8,128)S(1)}, s32[1,32]{1,0:T(1,128)S(4)}) custom-call(f32[8,2560]{1,0:T(8,128)S(1)} %get-tuple-element.13.own_ref, f32[2,11,128]{2,1,0:T(8,128)S(1)} %copy-done.4, f32[9,11,128]{2,1,0:T(8,128)S(1)} %copy-done.3, ...), custom_call_target="tpu_custom_call" | custom-call | tf_op jit(solution)/shard_map/own_rows/pallas_call | solution.py:393
  8.3 0.0 collective-permute-done.below_ref
  8.3 2.2 %collective-permute-done.1.above_ref = f32[4,2560]{1,0:T(4,128)S(1)} collective-permute-done((f32[4,2560]{1,0:T(4,128)S(1)}, f32[4,2560]{1,0:T(4,128)S(1)}, u32[]{:S(2)}, u32[]{:S(2)}) %collective-permute-start.1) | collective-permute-done | bytes 40992 | tf_op jit(solution)/shard_map/ppermute | solution.py:459
  10.5 0.0 copy-start.1
  10.5 0.0 copy-start
  10.5 0.8 %tile.1.lines_ref = bf16[64,128]{1,0:T(8,128)(2,1)S(1)} custom-call(f32[88,256]{1,0:T(8,128)S(1)} %get-tuple-element.14.own_ref, f32[4,2560]{1,0:T(4,128)S(1)} %collective-permute-done.below_ref, f32[4,2560]{1,0:T(4,128)S(1)} %collective-permute-done.1.above_ref, s32[1,32]{1,0:T(1,128)S(4)} %get-tuple-element.17.starts, f32[2,11,128]{2,1,0:T(8,128)S(1)} %copy-done.4, ...), custom_call_target="tpu_custom_call" | custom-call | tf_op jit(solution)/shard_map/tile/pallas_call | solution.py:412
  11.2 0.0 copy-start.2
  11.3 0.8 %collective-permute-start.3 = (bf16[64,128]{1,0:T(8,128)(2,1)S(1)}, bf16[64,128]{1,0:T(8,128)(2,1)S(1)}, u32[]{:S(2)}, u32[]{:S(2)}) collective-permute-start(bf16[64,128]{1,0:T(8,128)(2,1)S(1)} %tile.1.lines_ref), channel_id=1, source_target_pairs={{160,192},{168,200},{144,48},{152,56},{128,32},{136,40},{112,16},{... | collective-permute-start | bytes 49160 | tf_op jit(solution)/shard_map/ppermute | solution.py:463
  12.1 0.7 collective-permute-start.2
  12.7 0.0 collective-permute-done.3.second_ref
  12.7 0.0 collective-permute-done.2.first_ref
  12.8 0.0 copy-done.1
  12.8 0.1 repack.1
  12.9 51.5 %all_to_all.5 = bf16[48,2,128]{2,1,0:T(2,128)(2,1)S(1)} all-to-all(bf16[48,2,128]{2,1,0:T(2,128)(2,1)S(1)} %bitcast.7), channel_id=1, replica_groups={{192,200,208,216,224,232,240,248,48,56,32,40,16,24,0,8},{176,184,160,16..., dimensions={0} | all-to-all | bytes 49152 | tf_op jit(solution)/shard_map/all_to_all | solution.py:465
  64.4 0.7 collective-permute-start.5
  65.0 0.7 collective-permute-start.4
  65.7 0.0 collective-permute-done.5.second_ref
  65.7 0.0 collective-permute-done.4.first_ref
  65.7 0.0 copy-done
  65.7 0.0 copy-done.2
  65.8 1.0 %pixels.1 = f32[8,256]{1,0:T(8,128)} custom-call(bf16[96,128]{1,0:T(8,128)(2,1)S(1)} %bitcast.6, bf16[96,128]{1,0:T(8,128)(2,1)S(1)} %collective-permute-done.4.first_ref, bf16[96,128]{1,0:T(8,128)(2,1)S(1)} %collective-permute-done.5.second_ref, bf16[3,64,288]{2,1,0:T(8,128)(2,1)S(1)} %copy-done.2, bf16[1024,256]{1,0:T(8,128)(2,1)S(1)} %bitcast.3), custom_call_target="tpu_custom_call" | custom-call | tf_op jit(solution)/shard_map/pixels/pallas_call | solution.py:438
Async XLA Ops:
  0.0 6.9 %copy-start.3 = (f32[9,11,128]{2,1,0:T(8,128)S(1)}, f32[9,11,128]{2,1,0:T(8,128)}, u32[]{:S(2)}) copy-start(f32[9,11,128]{2,1,0:T(8,128)} %constant.15.clone.gains_ref) | copy-start | bytes 152068
  0.0 6.9 %copy-start.4 = (f32[2,11,128]{2,1,0:T(8,128)S(1)}, f32[2,11,128]{2,1,0:T(8,128)}, u32[]{:S(2)}) copy-start(f32[2,11,128]{2,1,0:T(8,128)} %constant.12.clone.turns_ref) | copy-start | bytes 33796
  1.0 7.3 %collective-permute-start = (f32[4,2560]{1,0:T(4,128)S(1)}, f32[4,2560]{1,0:T(4,128)S(1)}, u32[]{:S(2)}, u32[]{:S(2)}) collective-permute-start(f32[4,2560]{1,0:T(4,128)S(1)} %get-tuple-element.15), channel_id=1, source_target_pairs={{1,0},{2,1},{3,2},{4,3},{5,4},{6,5},{7,6},{9,8},{10,9},{11,10},{12... | collective-permute-start | bytes 122888 | tf_op jit(solution)/shard_map/ppermute | solution.py:458
  3.3 7.1 %collective-permute-start.1 = (f32[4,2560]{1,0:T(4,128)S(1)}, f32[4,2560]{1,0:T(4,128)S(1)}, u32[]{:S(2)}, u32[]{:S(2)}) collective-permute-start(f32[4,2560]{1,0:T(4,128)S(1)} %get-tuple-element.16), channel_id=1, source_target_pairs={{0,1},{1,2},{2,3},{3,4},{4,5},{5,6},{6,7},{8,9},{9,10},{10,11},{11... | collective-permute-start | bytes 122888 | tf_op jit(solution)/shard_map/ppermute | solution.py:459
  10.5 2.3 %copy-start.1 = (bf16[3,96,192]{2,1,0:T(8,128)(2,1)S(1)}, bf16[3,96,192]{2,1,0:T(8,128)(2,1)}, u32[]{:S(2)}) copy-start(bf16[3,96,192]{2,1,0:T(8,128)(2,1)} %constant.16.clone.table_ref) | copy-start | bytes 331780
  10.5 55.3 %copy-start = (bf16[32,32,256]{2,1,0:T(8,128)(2,1)S(1)}, bf16[32,32,256]{2,1,0:T(8,128)(2,1)}, u32[]{:S(2)}) copy-start(bf16[32,32,256]{2,1,0:T(8,128)(2,1)} %param.13) | copy-start | bytes 1572868
  11.2 54.5 %copy-start.2 = (bf16[3,64,288]{2,1,0:T(8,128)(2,1)S(1)}, bf16[3,64,288]{2,1,0:T(8,128)(2,1)}, u32[]{:S(2)}) copy-start(bf16[3,64,288]{2,1,0:T(8,128)(2,1)} %constant.17.clone.table_ref) | copy-start | bytes 331780
  11.3 1.5 %collective-permute-start.3 = (bf16[64,128]{1,0:T(8,128)(2,1)S(1)}, bf16[64,128]{1,0:T(8,128)(2,1)S(1)}, u32[]{:S(2)}, u32[]{:S(2)}) collective-permute-start(bf16[64,128]{1,0:T(8,128)(2,1)S(1)} %tile.1.lines_ref), channel_id=1, source_target_pairs={{160,192},{168,200},{144,48},{152,56},{128,32},{136,40},{112,16},{... | collective-permute-start | bytes 49160 | tf_op jit(solution)/shard_map/ppermute | solution.py:463
  12.1 0.7 %collective-permute-start.2 = (bf16[64,128]{1,0:T(8,128)(2,1)S(1)}, bf16[64,128]{1,0:T(8,128)(2,1)S(1)}, u32[]{:S(2)}, u32[]{:S(2)}) collective-permute-start(bf16[64,128]{1,0:T(8,128)(2,1)S(1)} %tile.1.lines_ref), channel_id=1, source_target_pairs={{176,192},{184,200},{64,48},{72,56},{80,32},{88,40},{96,16},{104,2... | collective-permute-start | bytes 49160 | tf_op jit(solution)/shard_map/ppermute | solution.py:463
  64.4 1.3 %collective-permute-start.5 = (bf16[96,128]{1,0:T(8,128)(2,1)S(1)}, bf16[96,128]{1,0:T(8,128)(2,1)S(1)}, u32[]{:S(2)}, u32[]{:S(2)}) collective-permute-start(bf16[96,128]{1,0:T(8,128)(2,1)S(1)} %bitcast.4), channel_id=1, source_target_pairs={{192,160},{200,168},{208,128},{216,136},{224,96},{232,104},{48,80}... | collective-permute-start | bytes 73736 | tf_op jit(solution)/shard_map/ppermute | solution.py:469
  65.0 0.7 %collective-permute-start.4 = (bf16[96,128]{1,0:T(8,128)(2,1)S(1)}, bf16[96,128]{1,0:T(8,128)(2,1)S(1)}, u32[]{:S(2)}, u32[]{:S(2)}) collective-permute-start(bf16[96,128]{1,0:T(8,128)(2,1)S(1)} %bitcast.5), channel_id=1, source_target_pairs={{192,176},{200,184},{208,144},{216,152},{224,112},{232,120},{48,64... | collective-permute-start | bytes 73736 | tf_op jit(solution)/shard_map/ppermute | solution.py:469

commit v14 on v11

--- a/solution.py
+++ b/solution.py
@@ -329,6 +329,11 @@
         early = (step == 4) | ((step > 6) & (step % 2 == 1))
         return jnp.where(far, 0, jnp.where(other, 2, 1)), jnp.where(far, jnp.where(early, 1, 2), 0)
 
+    @classmethod
+    def taking_part(cls, device, count):
+        step = device // (count // cls.AROUND)
+        return (step > 0) & (step < cls.AROUND - 1)
+
 
 def repack_kernel(lines_ref, first_ref, second_ref, table_ref, out_ref):
     kind, _ = Routes.kinds(lax.axis_index("ang"), lax.axis_size("ang"))
@@ -460,14 +465,21 @@
     own_spec, forward, inverse, gains, starts = make_own(own, turns, forward, inverse, gains, block_start)
     outgoing = make_tile(own_spec, below, above, starts, turns, forward, inverse, gains, cut)
     routes = Routes(lax.axis_size("ang"))
-    entered = [lax.ppermute(outgoing, "ang", pairs) for pairs in routes.enter]
-    packed = make_repack(outgoing, *entered, jnp.asarray(routes.exchange_table()))
+    relayed = routes.taking_part(lax.axis_index("ang"), routes.count)
+    exchange, arrival = jnp.asarray(routes.exchange_table()), jnp.asarray(routes.arrival_table())
+
+    def enter(lines):
+        return make_repack(lines, *(lax.ppermute(lines, "ang", pairs) for pairs in routes.enter), exchange)
+
+    def leave(lines):
+        return make_pixels(lines, *(lax.ppermute(lines, "ang", pairs) for pairs in routes.leave), arrival, bp_weights)
+
+    packed = lax.cond(relayed, enter, lambda lines: make_repack(lines, lines, lines, exchange), outgoing)
     near = lax.all_to_all(
         packed.reshape(-1, 2, LANES), "ang", split_axis=0, concat_axis=0, tiled=True,
         axis_index_groups=[routes.near, routes.far],
     ).reshape(packed.shape)
-    left = [lax.ppermute(near, "ang", pairs) for pairs in routes.leave]
-    return make_pixels(near, *left, jnp.asarray(routes.arrival_table()), bp_weights)
+    return lax.cond(relayed, leave, lambda lines: make_pixels(lines, lines, lines, arrival, bp_weights), near)
 
 
 def solution(mesh):

time: 67.3 us -> 66.5 us (0.988)
  the two profiles are of different devices: /device:TPU:73 before, /device:TPU:856 now
where the time goes in v14:
time: 66.5 us; the launch traced here: 66.1 us
  starting transfers between devices  23.6 us (35%)
  waiting for transfers between devices  21.3 us (32%)
  blocking collectives  16.1 us (24%)
  Pallas kernels  3.57 us (5%)
  local copies, waits for them, and re-layouts  1.45 us (2%)
    ppermute x2, waiting for transfers between devices, enter(): lax.ppermute(lines, 'ang', pairs)  18.3 us
    all_to_all x1, blocking collectives, body(): lax.all_to_all(packed.reshape(-1, 2, LANES), 'ang', split_axis=0, concat_...  16.1 us
    ppermute x2, starting transfers between devices, leave(): lax.ppermute(lines, 'ang', pairs)  9.63 us
    ppermute x2, starting transfers between devices, enter(): lax.ppermute(lines, 'ang', pairs)  8.02 us
    ppermute x1, starting transfers between devices, body(): above = lax.ppermute(last, 'row', up)  3.57 us
    ppermute x1, starting transfers between devices, body(): below = lax.ppermute(first, 'row', down)  2.34 us
    ppermute x1, waiting for transfers between devices, body(): above = lax.ppermute(last, 'row', up)  1.5 us
    ppermute x2, waiting for transfers between devices, leave(): lax.ppermute(lines, 'ang', pairs)  1.5 us
  transfers between devices with their start and end apart: 6, of which 4 were waited for; matrix products, arithmetic and copies ran while one was open for 0% of the time, Pallas kernels for 2%

profile of v14, /device:TPU:856, one launch (start us, length us, event | category | flops | bytes accessed | tf_op | source)
XLA Modules:
  0.0 66.1 jit_solution(11816438757050191219)
XLA Ops:
  0.0 0.0 copy-start
  0.0 1.0 %contrast.1 = (f32[8,2560]{1,0:T(8,128)S(1)}, f32[4,2560]{1,0:T(4,128)S(1)}, f32[4,2560]{1,0:T(4,128)S(1)}) custom-call(bf16[1,8,2560]{2,1,0:T(8,128)(2,1)} %proj_hbm.1, f32[8,2560]{1,0:T(8,128)} %flat_hbm.1), custom_call_target="tpu_custom_call" | custom-call | tf_op jit(solution)/shard_map/contrast/pallas_call | solution.py:381
  1.0 2.3 %collective-permute-start.4 = (f32[4,2560]{1,0:T(4,128)S(1)}, f32[4,2560]{1,0:T(4,128)S(1)}, u32[]{:S(2)}, u32[]{:S(2)}) collective-permute-start(f32[4,2560]{1,0:T(4,128)S(1)} %get-tuple-element.51), channel_id=1, source_target_pairs={{1,0},{2,1},{3,2},{4,3},{5,4},{6,5},{7,6},{9,8},{10,9},{11,10},{12... | collective-permute-start | bytes 122888 | tf_op jit(solution)/shard_map/ppermute | solution.py:463
  3.3 3.6 %collective-permute-start.5 = (f32[4,2560]{1,0:T(4,128)S(1)}, f32[4,2560]{1,0:T(4,128)S(1)}, u32[]{:S(2)}, u32[]{:S(2)}) collective-permute-start(f32[4,2560]{1,0:T(4,128)S(1)} %get-tuple-element.52), channel_id=1, source_target_pairs={{0,1},{1,2},{2,3},{3,4},{4,5},{5,6},{6,7},{8,9},{9,10},{10,11},{11... | collective-permute-start | bytes 122888 | tf_op jit(solution)/shard_map/ppermute | solution.py:464
  6.9 0.0 copy-start.1
  6.9 0.0 copy-done
  7.0 0.7 %copy-done.1 = f32[2,11,128]{2,1,0:T(8,128)S(1)} copy-done((f32[2,11,128]{2,1,0:T(8,128)S(1)}, f32[2,11,128]{2,1,0:T(8,128)}, u32[]{:S(2)}) %copy-start.1) | copy-done | bytes 11288
  7.6 1.3 %own_rows.1 = (f32[88,256]{1,0:T(8,128)S(1)}, bf16[2,256,256]{2,1,0:T(8,128)(2,1)S(1)}, bf16[2,256,256]{2,1,0:T(8,128)(2,1)S(1)}, f32[8,11,8,128]{3,2,1,0:T(8,128)S(1)}, s32[1,32]{1,0:T(1,128)S(4)}) custom-call(f32[8,2560]{1,0:T(8,128)S(1)} %get-tuple-element.49.own_ref, f32[2,11,128]{2,1,0:T(8,128)S(1)} %copy-done.1, f32[9,11,128]{2,1,0:T(8,128)S(1)} %copy-done, ...), custom_call_target="tpu_custom_call" | custom-call | tf_op jit(solution)/shard_map/own_rows/pallas_call | solution.py:398
  9.0 0.0 collective-permute-done.4.below_ref
  9.0 1.5 %collective-permute-done.5.above_ref = f32[4,2560]{1,0:T(4,128)S(1)} collective-permute-done((f32[4,2560]{1,0:T(4,128)S(1)}, f32[4,2560]{1,0:T(4,128)S(1)}, u32[]{:S(2)}, u32[]{:S(2)}) %collective-permute-start.5) | collective-permute-done | bytes 40992 | tf_op jit(solution)/shard_map/ppermute | solution.py:464
  10.5 0.0 copy-start.3
  10.5 0.0 copy-start.2
  10.5 0.8 %tile.1 = bf16[64,128]{1,0:T(8,128)(2,1)S(1)} custom-call(f32[88,256]{1,0:T(8,128)S(1)} %get-tuple-element.50.own_ref, f32[4,2560]{1,0:T(4,128)S(1)} %collective-permute-done.4.below_ref, f32[4,2560]{1,0:T(4,128)S(1)} %collective-permute-done.5.above_ref, s32[1,32]{1,0:T(1,128)S(4)} %get-tuple-element.53.starts, f32[2,11,128]{2,1,0:T(8,128)S(1)} %copy-done.1, ...), custom_call_target="tpu_custom_call" | custom-call | tf_op jit(solution)/shard_map/tile/pallas_call | solution.py:417
  11.2 0.1 copy-done.3
  11.4 0.0 copy-start.4
  11.4 26.5 %conditional.2 = (bf16[96,128]{1,0:T(8,128)(2,1)S(1)}) conditional(s32[]{:T(128)} %convert_element_type.4, (bf16[64,128]{1,0:T(8,128)(2,1)S(1)}, bf16[3,96,192]{2,1,0:T(8,128)(2,1)S(1)}) %tuple.30, (bf16[64,128]{1,0:T(8,128)(2,1)S(1)}, bf16[3,96,192]{2,1,0:T(8,128)(2,1)S(1)}) %tuple.31), branch_computations={%region_0.1_spmd, %region_1.2_spmd} | conditional | bytes 131160 | solution.py:477
  11.4 1.4 %collective-permute-start.1 = (bf16[64,128]{1,0:T(8,128)(2,1)S(1)}, bf16[64,128]{1,0:T(8,128)(2,1)S(1)}, u32[]{:S(2)}, u32[]{:S(2)}) collective-permute-start(bf16[64,128]{1,0:T(8,128)(2,1)S(1)} %get-tuple-element.33.lines_ref), channel_id=1, source_target_pairs={{160,192},{168,200},{144,48},{152,56},{128,32},{136,40},{112,16},{... | collective-permute-start | bytes 49160 | tf_op jit(solution)/shard_map/cond/branch_1_fun/ppermute | solution.py:472
  12.8 6.6 %collective-permute-start = (bf16[64,128]{1,0:T(8,128)(2,1)S(1)}, bf16[64,128]{1,0:T(8,128)(2,1)S(1)}, u32[]{:S(2)}, u32[]{:S(2)}) collective-permute-start(bf16[64,128]{1,0:T(8,128)(2,1)S(1)} %get-tuple-element.33.lines_ref), channel_id=1, source_target_pairs={{176,192},{184,200},{64,48},{72,56},{80,32},{88,40},{96,16},{104,2... | collective-permute-start | bytes 49160 | tf_op jit(solution)/shard_map/cond/branch_1_fun/ppermute | solution.py:472
  19.4 18.3 %collective-permute-done.1.second_ref = bf16[64,128]{1,0:T(8,128)(2,1)S(1)} collective-permute-done((bf16[64,128]{1,0:T(8,128)(2,1)S(1)}, bf16[64,128]{1,0:T(8,128)(2,1)S(1)}, u32[]{:S(2)}, u32[]{:S(2)}) %collective-permute-start.1) | collective-permute-done | bytes 16416 | tf_op jit(solution)/shard_map/cond/branch_1_fun/ppermute | solution.py:472
  37.8 0.0 collective-permute-done.first_ref
  37.8 0.1 repack.3
  37.9 16.1 %all_to_all.5 = bf16[48,2,128]{2,1,0:T(2,128)(2,1)S(1)} all-to-all(bf16[48,2,128]{2,1,0:T(2,128)(2,1)S(1)} %bitcast.8), channel_id=1, replica_groups={{192,200,208,216,224,232,240,248,0,8,16,24,32,40,48,56},{64,72,80,88,96..., dimensions={0} | all-to-all | bytes 49152 | tf_op jit(solution)/shard_map/all_to_all | solution.py:478
  54.0 0.0 copy-done.2
  54.0 0.0 copy-done.4
  54.0 11.5 %conditional.3 = (f32[8,256]{1,0:T(8,128)S(1)}) conditional(s32[]{:T(128)} %convert_element_type.4, (bf16[32,32,256]{2,1,0:T(8,128)(2,1)S(1)}, bf16[96,128]{1,0:T(8,128)(2,1)S(1)}, bf16[3,64,288]{2,1,0:T(8,128)(2,1)S(1)}) %tuple.32, (bf16[96,128]{1,0:T(8,128)(2,1)S(1)}, bf16[32,32,256]{2,1,0:T(8,128)(2,1)S(1)}, ...), branch_computations={%region_2.3_spmd, %region_3.4_spmd} | conditional | bytes 196696 | solution.py:482
  54.0 8.3 %collective-permute-start.3 = (bf16[96,128]{1,0:T(8,128)(2,1)S(1)}, bf16[96,128]{1,0:T(8,128)(2,1)S(1)}, u32[]{:S(2)}, u32[]{:S(2)}) collective-permute-start(bf16[96,128]{1,0:T(8,128)(2,1)S(1)} %get-tuple-element.38.near_ref), channel_id=1, source_target_pairs={{192,160},{200,168},{208,128},{216,136},{224,96},{232,104},{48,80}... | collective-permute-start | bytes 73736 | tf_op jit(solution)/shard_map/cond/branch_1_fun/ppermute | solution.py:475
  62.3 1.3 %collective-permute-start.2 = (bf16[96,128]{1,0:T(8,128)(2,1)S(1)}, bf16[96,128]{1,0:T(8,128)(2,1)S(1)}, u32[]{:S(2)}, u32[]{:S(2)}) collective-permute-start(bf16[96,128]{1,0:T(8,128)(2,1)S(1)} %get-tuple-element.38.near_ref), channel_id=1, source_target_pairs={{192,176},{200,184},{208,144},{216,152},{224,112},{232,120},{48,64... | collective-permute-start | bytes 73736 | tf_op jit(solution)/shard_map/cond/branch_1_fun/ppermute | solution.py:475
  63.6 0.2 collective-permute-done.3.second_ref
  63.8 1.3 %collective-permute-done.2.first_ref = bf16[96,128]{1,0:T(8,128)(2,1)S(1)} collective-permute-done((bf16[96,128]{1,0:T(8,128)(2,1)S(1)}, bf16[96,128]{1,0:T(8,128)(2,1)S(1)}, u32[]{:S(2)}, u32[]{:S(2)}) %collective-permute-start.2) | collective-permute-done | bytes 24608 | tf_op jit(solution)/shard_map/cond/branch_1_fun/ppermute | solution.py:475
  65.1 0.4 pixels.3
  65.5 0.0 copy-start.5
  65.5 0.6 copy-done.5
Async XLA Ops:
  0.0 6.9 %copy-start = (f32[9,11,128]{2,1,0:T(8,128)S(1)}, f32[9,11,128]{2,1,0:T(8,128)}, u32[]{:S(2)}) copy-start(f32[9,11,128]{2,1,0:T(8,128)} %constant.38.clone.gains_ref) | copy-start | bytes 152068
  1.0 8.0 %collective-permute-start.4 = (f32[4,2560]{1,0:T(4,128)S(1)}, f32[4,2560]{1,0:T(4,128)S(1)}, u32[]{:S(2)}, u32[]{:S(2)}) collective-permute-start(f32[4,2560]{1,0:T(4,128)S(1)} %get-tuple-element.51), channel_id=1, source_target_pairs={{1,0},{2,1},{3,2},{4,3},{5,4},{6,5},{7,6},{9,8},{10,9},{11,10},{12... | collective-permute-start | bytes 122888 | tf_op jit(solution)/shard_map/ppermute | solution.py:463
  3.3 7.1 %collective-permute-start.5 = (f32[4,2560]{1,0:T(4,128)S(1)}, f32[4,2560]{1,0:T(4,128)S(1)}, u32[]{:S(2)}, u32[]{:S(2)}) collective-permute-start(f32[4,2560]{1,0:T(4,128)S(1)} %get-tuple-element.52), channel_id=1, source_target_pairs={{0,1},{1,2},{2,3},{3,4},{4,5},{5,6},{6,7},{8,9},{9,10},{10,11},{11... | collective-permute-start | bytes 122888 | tf_op jit(solution)/shard_map/ppermute | solution.py:464
  6.9 0.7 %copy-start.1 = (f32[2,11,128]{2,1,0:T(8,128)S(1)}, f32[2,11,128]{2,1,0:T(8,128)}, u32[]{:S(2)}) copy-start(f32[2,11,128]{2,1,0:T(8,128)} %constant.35.clone.turns_ref) | copy-start | bytes 33796
  10.5 0.9 %copy-start.3 = (bf16[3,96,192]{2,1,0:T(8,128)(2,1)S(1)}, bf16[3,96,192]{2,1,0:T(8,128)(2,1)}, u32[]{:S(2)}) copy-start(bf16[3,96,192]{2,1,0:T(8,128)(2,1)} %constant.39.clone) | copy-start | bytes 331780
  10.5 43.5 %copy-start.2 = (bf16[32,32,256]{2,1,0:T(8,128)(2,1)S(1)}, bf16[32,32,256]{2,1,0:T(8,128)(2,1)}, u32[]{:S(2)}) copy-start(bf16[32,32,256]{2,1,0:T(8,128)(2,1)} %param.17) | copy-start | bytes 1572868
  11.4 42.6 %copy-start.4 = (bf16[3,64,288]{2,1,0:T(8,128)(2,1)S(1)}, bf16[3,64,288]{2,1,0:T(8,128)(2,1)}, u32[]{:S(2)}) copy-start(bf16[3,64,288]{2,1,0:T(8,128)(2,1)} %constant.40.clone) | copy-start | bytes 331780
  11.4 26.4 %collective-permute-start.1 = (bf16[64,128]{1,0:T(8,128)(2,1)S(1)}, bf16[64,128]{1,0:T(8,128)(2,1)S(1)}, u32[]{:S(2)}, u32[]{:S(2)}) collective-permute-start(bf16[64,128]{1,0:T(8,128)(2,1)S(1)} %get-tuple-element.33.lines_ref), channel_id=1, source_target_pairs={{160,192},{168,200},{144,48},{152,56},{128,32},{136,40},{112,16},{... | collective-permute-start | bytes 49160 | tf_op jit(solution)/shard_map/cond/branch_1_fun/ppermute | solution.py:472
  12.8 24.9 %collective-permute-start = (bf16[64,128]{1,0:T(8,128)(2,1)S(1)}, bf16[64,128]{1,0:T(8,128)(2,1)S(1)}, u32[]{:S(2)}, u32[]{:S(2)}) collective-permute-start(bf16[64,128]{1,0:T(8,128)(2,1)S(1)} %get-tuple-element.33.lines_ref), channel_id=1, source_target_pairs={{176,192},{184,200},{64,48},{72,56},{80,32},{88,40},{96,16},{104,2... | collective-permute-start | bytes 49160 | tf_op jit(solution)/shard_map/cond/branch_1_fun/ppermute | solution.py:472
  54.0 9.8 %collective-permute-start.3 = (bf16[96,128]{1,0:T(8,128)(2,1)S(1)}, bf16[96,128]{1,0:T(8,128)(2,1)S(1)}, u32[]{:S(2)}, u32[]{:S(2)}) collective-permute-start(bf16[96,128]{1,0:T(8,128)(2,1)S(1)} %get-tuple-element.38.near_ref), channel_id=1, source_target_pairs={{192,160},{200,168},{208,128},{216,136},{224,96},{232,104},{48,80}... | collective-permute-start | bytes 73736 | tf_op jit(solution)/shard_map/cond/branch_1_fun/ppermute | solution.py:475
  62.3 2.8 %collective-permute-start.2 = (bf16[96,128]{1,0:T(8,128)(2,1)S(1)}, bf16[96,128]{1,0:T(8,128)(2,1)S(1)}, u32[]{:S(2)}, u32[]{:S(2)}) collective-permute-start(bf16[96,128]{1,0:T(8,128)(2,1)S(1)} %get-tuple-element.38.near_ref), channel_id=1, source_target_pairs={{192,176},{200,184},{208,144},{216,152},{224,112},{232,120},{48,64... | collective-permute-start | bytes 73736 | tf_op jit(solution)/shard_map/cond/branch_1_fun/ppermute | solution.py:475
  65.5 0.6 copy-start.5

commit v15 on v12

--- a/solution.py
+++ b/solution.py
@@ -272,10 +272,11 @@
         self.near = devices((12, 13, 14, 15, 0, 1, 2, 3))
         self.far = devices(range(4, 12))
         self.relays = devices((1, 2, 3))
+        self.swaps = 0
         self.enter = [
+            link(((5, 2), (4, 3), (1, 6), (2, 5), (3, 4))),
+            link(((10, 1), (8, 2), (6, 3))),
             link(((11, 1), (9, 2), (7, 3))),
-            link(((10, 1), (8, 2), (6, 3))),
-            link(((5, 2), (4, 3), (1, 6), (2, 5), (3, 4))),
         ]
         self.leave = [link(((12, 11), (13, 9), (14, 7), (3, 4))), link(((12, 10), (13, 8), (14, 6), (3, 5)))]
 
@@ -288,7 +289,7 @@
 
         for m, dest in enumerate(self.far):
             put(0, m, 0, 0, dest)
-            put(0, m, 1, len(self.enter), dest)
+            put(0, m, 1, 1 + self.swaps, dest)
         for m, dest in enumerate(self.near):
             put(1, m, 0, 0, dest)
             put(2, m, 0, 0, dest)
@@ -320,7 +321,7 @@
         for m, angle in enumerate(self.far):
             for turn in range(len(self.leave)):
                 put(1 + turn, angle, 0, m, 0)
-                for src, dst in self.enter[-1]:
+                for src, dst in self.enter[self.swaps]:
                     if dst == angle:
                         put(1 + turn, src, 0, m, 1)
         return table.astype(jnp.bfloat16)
@@ -333,6 +334,11 @@
         other = turned <= 4
         early = (step == 4) | ((step > 6) & (step % 2 == 1))
         return jnp.where(far, 0, jnp.where(other, 2, 1)), jnp.where(far, jnp.where(early, 1, 2), 0)
+
+    @classmethod
+    def taking_part(cls, device, count):
+        step = device // (count // cls.AROUND)
+        return (step > 0) & (step < cls.AROUND - 1)
 
 
 def repack_kernel(lines_ref, first_ref, second_ref, third_ref, table_ref, out_ref):
@@ -465,14 +471,21 @@
     own_spec, forward, inverse, gains, starts = make_own(own, turns, forward, inverse, gains, block_start)
     outgoing = make_tile(own_spec, below, above, starts, turns, forward, inverse, gains, cut)
     routes = Routes(lax.axis_size("ang"))
-    entered = [lax.ppermute(outgoing, "ang", pairs) for pairs in routes.enter]
-    packed = make_repack(outgoing, *entered, jnp.asarray(routes.exchange_table()))
+    relayed = routes.taking_part(lax.axis_index("ang"), routes.count)
+    exchange, arrival = jnp.asarray(routes.exchange_table()), jnp.asarray(routes.arrival_table())
+
+    def enter(lines):
+        return make_repack(lines, *(lax.ppermute(lines, "ang", pairs) for pairs in routes.enter), exchange)
+
+    def leave(lines):
+        return make_pixels(lines, *(lax.ppermute(lines, "ang", pairs) for pairs in routes.leave), arrival, bp_weights)
+
+    packed = lax.cond(relayed, enter, lambda lines: make_repack(lines, lines, lines, lines, exchange), outgoing)
     near = lax.all_to_all(
         packed.reshape(-1, 2, LANES), "ang", split_axis=0, concat_axis=0, tiled=True,
         axis_index_groups=[routes.near, routes.far],
     ).reshape(packed.shape)
-    left = [lax.ppermute(near, "ang", pairs) for pairs in routes.leave]
-    return make_pixels(near, *left, jnp.asarray(routes.arrival_table()), bp_weights)
+    return lax.cond(relayed, leave, lambda lines: make_pixels(lines, lines, lines, arrival, bp_weights), near)
 
 
 def solution(mesh):

time: 68.2 us -> 65.7 us (0.963)
  starting transfers between devices: 9.34 us -> 5.9 us
  local copies, waits for them, and re-layouts: 0.02 us -> 1.47 us
  blocking collectives: 51.7 us -> 52.5 us
  waiting for transfers between devices: 2.22 us -> 1.51 us
    ppermute x5 -> x0, starting transfers between devices: 3.43 us -> none  [the longest x3 2.12 us: body(): entered = [lax.ppermute(outgoing, 'ang', pairs) for pairs in routes.enter]]
    unnamed x10 -> x12, local copies, waits for them, and re-layouts: 0.02 us -> 1.47 us
    all_to_all x1, blocking collectives: 51.7 us -> 52.5 us  [body(): lax.all_to_all(packed.reshape(-1, 2, LANES), 'ang', split_axis=0, concat_...]
    ppermute x1, waiting for transfers between devices: 2.2 us -> 1.51 us  [body(): above = lax.ppermute(last, 'row', up)]
  transfers between devices with their start and end apart: 7 -> 2, of which waited for: 1 -> 1; matrix products, arithmetic and copies ran while one was open for 0% -> 0% of each run, Pallas kernels for 2% -> 2%
where the time goes in v15:
time: 65.7 us; the launch traced here: 65.1 us
  blocking collectives  52.5 us (80%)
  starting transfers between devices  5.9 us (9%)
  Pallas kernels  3.58 us (5%)
  waiting for transfers between devices  1.51 us (2%)
  local copies, waits for them, and re-layouts  1.47 us (2%)
    all_to_all x1, blocking collectives, body(): lax.all_to_all(packed.reshape(-1, 2, LANES), 'ang', split_axis=0, concat_...  52.5 us
    ppermute x1, starting transfers between devices, body(): above = lax.ppermute(last, 'row', up)  3.57 us
    ppermute x1, starting transfers between devices, body(): below = lax.ppermute(first, 'row', down)  2.34 us
    ppermute x1, waiting for transfers between devices, body(): above = lax.ppermute(last, 'row', up)  1.51 us
    unnamed x12, local copies, waits for them, and re-layouts  1.47 us
  transfers between devices with their start and end apart: 2, of which 1 were waited for; matrix products, arithmetic and copies ran while one was open for 0% of the time, Pallas kernels for 2%

profile of v15, /device:TPU:88, one launch (start us, length us, event | category | flops | bytes accessed | tf_op | source)
XLA Modules:
  0.0 65.1 jit_solution(2966358170246807857)
XLA Ops:
  0.0 0.0 copy-start
  0.0 1.0 %contrast.1 = (f32[8,2560]{1,0:T(8,128)S(1)}, f32[4,2560]{1,0:T(4,128)S(1)}, f32[4,2560]{1,0:T(4,128)S(1)}) custom-call(bf16[1,8,2560]{2,1,0:T(8,128)(2,1)} %proj_hbm.1, f32[8,2560]{1,0:T(8,128)} %flat_hbm.1), custom_call_target="tpu_custom_call" | custom-call | tf_op jit(solution)/shard_map/contrast/pallas_call | solution.py:387
  1.0 2.3 %collective-permute-start.5 = (f32[4,2560]{1,0:T(4,128)S(1)}, f32[4,2560]{1,0:T(4,128)S(1)}, u32[]{:S(2)}, u32[]{:S(2)}) collective-permute-start(f32[4,2560]{1,0:T(4,128)S(1)} %get-tuple-element.51), channel_id=1, source_target_pairs={{1,0},{2,1},{3,2},{4,3},{5,4},{6,5},{7,6},{9,8},{10,9},{11,10},{12... | collective-permute-start | bytes 122888 | tf_op jit(solution)/shard_map/ppermute | solution.py:469
  3.3 3.6 %collective-permute-start.6 = (f32[4,2560]{1,0:T(4,128)S(1)}, f32[4,2560]{1,0:T(4,128)S(1)}, u32[]{:S(2)}, u32[]{:S(2)}) collective-permute-start(f32[4,2560]{1,0:T(4,128)S(1)} %get-tuple-element.52), channel_id=1, source_target_pairs={{0,1},{1,2},{2,3},{3,4},{4,5},{5,6},{6,7},{8,9},{9,10},{10,11},{11... | collective-permute-start | bytes 122888 | tf_op jit(solution)/shard_map/ppermute | solution.py:470
  6.9 0.0 copy-start.1
  6.9 0.0 copy-done
  7.0 0.7 %copy-done.1 = f32[2,11,128]{2,1,0:T(8,128)S(1)} copy-done((f32[2,11,128]{2,1,0:T(8,128)S(1)}, f32[2,11,128]{2,1,0:T(8,128)}, u32[]{:S(2)}) %copy-start.1) | copy-done | bytes 11288
  7.6 1.3 %own_rows.1 = (f32[88,256]{1,0:T(8,128)S(1)}, bf16[2,256,256]{2,1,0:T(8,128)(2,1)S(1)}, bf16[2,256,256]{2,1,0:T(8,128)(2,1)S(1)}, f32[8,11,8,128]{3,2,1,0:T(8,128)S(1)}, s32[1,32]{1,0:T(1,128)S(4)}) custom-call(f32[8,2560]{1,0:T(8,128)S(1)} %get-tuple-element.49.own_ref, f32[2,11,128]{2,1,0:T(8,128)S(1)} %copy-done.1, f32[9,11,128]{2,1,0:T(8,128)S(1)} %copy-done, ...), custom_call_target="tpu_custom_call" | custom-call | tf_op jit(solution)/shard_map/own_rows/pallas_call | solution.py:404
  9.0 0.0 collective-permute-done.5.below_ref
  9.0 1.5 %collective-permute-done.6.above_ref = f32[4,2560]{1,0:T(4,128)S(1)} collective-permute-done((f32[4,2560]{1,0:T(4,128)S(1)}, f32[4,2560]{1,0:T(4,128)S(1)}, u32[]{:S(2)}, u32[]{:S(2)}) %collective-permute-start.6) | collective-permute-done | bytes 40992 | tf_op jit(solution)/shard_map/ppermute | solution.py:470
  10.5 0.0 copy-start.3
  10.5 0.8 %tile.1 = bf16[64,128]{1,0:T(8,128)(2,1)S(1)} custom-call(f32[88,256]{1,0:T(8,128)S(1)} %get-tuple-element.50.own_ref, f32[4,2560]{1,0:T(4,128)S(1)} %collective-permute-done.5.below_ref, f32[4,2560]{1,0:T(4,128)S(1)} %collective-permute-done.6.above_ref, s32[1,32]{1,0:T(1,128)S(4)} %get-tuple-element.53.starts, f32[2,11,128]{2,1,0:T(8,128)S(1)} %copy-done.1, ...), custom_call_target="tpu_custom_call" | custom-call | tf_op jit(solution)/shard_map/tile/pallas_call | solution.py:423
  11.2 0.2 copy-done.3
  11.4 0.0 copy-start.2
  11.4 0.0 copy-start.4
  11.4 0.2 conditional.2
  11.4 0.2 repack.2
  11.6 52.5 %all_to_all.5 = bf16[64,2,128]{2,1,0:T(2,128)(2,1)S(1)} all-to-all(bf16[64,2,128]{2,1,0:T(2,128)(2,1)S(1)} %bitcast.8), channel_id=1, replica_groups={{192,200,208,216,224,232,240,248,0,8,16,24,32,40,48,56},{64,72,80,88,96..., dimensions={0} | all-to-all | bytes 65536 | tf_op jit(solution)/shard_map/all_to_all | solution.py:484
  64.1 0.0 copy-done.2
  64.1 0.0 copy-done.4
  64.1 0.4 conditional.3
  64.1 0.4 pixels.2
  64.5 0.0 copy-start.5
  64.5 0.6 copy-done.5
Async XLA Ops:
  0.0 6.9 %copy-start = (f32[9,11,128]{2,1,0:T(8,128)S(1)}, f32[9,11,128]{2,1,0:T(8,128)}, u32[]{:S(2)}) copy-start(f32[9,11,128]{2,1,0:T(8,128)} %constant.38.clone.gains_ref) | copy-start | bytes 152068
  1.0 8.0 %collective-permute-start.5 = (f32[4,2560]{1,0:T(4,128)S(1)}, f32[4,2560]{1,0:T(4,128)S(1)}, u32[]{:S(2)}, u32[]{:S(2)}) collective-permute-start(f32[4,2560]{1,0:T(4,128)S(1)} %get-tuple-element.51), channel_id=1, source_target_pairs={{1,0},{2,1},{3,2},{4,3},{5,4},{6,5},{7,6},{9,8},{10,9},{11,10},{12... | collective-permute-start | bytes 122888 | tf_op jit(solution)/shard_map/ppermute | solution.py:469
  3.3 7.1 %collective-permute-start.6 = (f32[4,2560]{1,0:T(4,128)S(1)}, f32[4,2560]{1,0:T(4,128)S(1)}, u32[]{:S(2)}, u32[]{:S(2)}) collective-permute-start(f32[4,2560]{1,0:T(4,128)S(1)} %get-tuple-element.52), channel_id=1, source_target_pairs={{0,1},{1,2},{2,3},{3,4},{4,5},{5,6},{6,7},{8,9},{9,10},{10,11},{11... | collective-permute-start | bytes 122888 | tf_op jit(solution)/shard_map/ppermute | solution.py:470
  6.9 0.7 %copy-start.1 = (f32[2,11,128]{2,1,0:T(8,128)S(1)}, f32[2,11,128]{2,1,0:T(8,128)}, u32[]{:S(2)}) copy-start(f32[2,11,128]{2,1,0:T(8,128)} %constant.35.clone.turns_ref) | copy-start | bytes 33796
  10.5 0.9 %copy-start.3 = (bf16[3,128,256]{2,1,0:T(8,128)(2,1)S(1)}, bf16[3,128,256]{2,1,0:T(8,128)(2,1)}, u32[]{:S(2)}) copy-start(bf16[3,128,256]{2,1,0:T(8,128)(2,1)} %constant.39.clone) | copy-start | bytes 589828
  11.4 52.7 %copy-start.2 = (bf16[32,32,256]{2,1,0:T(8,128)(2,1)S(1)}, bf16[32,32,256]{2,1,0:T(8,128)(2,1)}, u32[]{:S(2)}) copy-start(bf16[32,32,256]{2,1,0:T(8,128)(2,1)} %param.17) | copy-start | bytes 1572868
  11.4 52.7 %copy-start.4 = (bf16[3,64,384]{2,1,0:T(8,128)(2,1)S(1)}, bf16[3,64,384]{2,1,0:T(8,128)(2,1)}, u32[]{:S(2)}) copy-start(bf16[3,64,384]{2,1,0:T(8,128)(2,1)} %constant.40.clone) | copy-start | bytes 442372
  64.5 0.6 copy-start.5

commit v16 on v15

--- a/solution.py
+++ b/solution.py
@@ -177,8 +177,8 @@
 
 
 def own_kernel(
-    own_ref, turns_ref, gains_ref, forward_hbm, inverse_hbm, starts_hbm,
-    out_ref, forward_ref, inverse_ref, halo_ref, starts_ref, sems
+    own_ref, turns_ref, gains_ref, forward_hbm, inverse_hbm, starts_hbm, exchange_hbm,
+    out_ref, forward_ref, inverse_ref, halo_ref, starts_ref, exchange_ref, sems
 ):
     forward_copy = pltpu.make_async_copy(forward_hbm, forward_ref, sems.at[0])
     inverse_copy = pltpu.make_async_copy(inverse_hbm, inverse_ref, sems.at[1])
@@ -186,6 +186,8 @@
     forward_copy.start()
     inverse_copy.start()
     starts_copy.start()
+    exchange_copy = pltpu.make_async_copy(exchange_hbm, exchange_ref, sems.at[3])
+    exchange_copy.start()
     row = lax.broadcasted_iota(jnp.int32, (SUB, LANES), 0)
     for k in range(gains_ref.shape[1]):
         for s, gain in halo_gains(gains_ref, k, row):
@@ -205,6 +207,7 @@
             out_ref[rows, side] = total
     inverse_copy.wait()
     starts_copy.wait()
+    exchange_copy.wait()
 
 
 def tile_kernel(
@@ -348,10 +351,12 @@
     out_ref[...] = out.astype(out_ref.dtype)
 
 
-def pixels_kernel(near_ref, first_ref, second_ref, table_ref, weights_ref, out_ref, lines, *, angles):
+def pixels_kernel(*refs, angles):
     _, kind = Routes.kinds(lax.axis_index("ang"), lax.axis_size("ang"))
-    held = jnp.concatenate((near_ref[...], first_ref[...], second_ref[...]), axis=0)
-    lines[...] = jnp.dot(table_ref[kind], held, preferred_element_type=jnp.float32)
+    *held_refs, table_ref, weights_ref, out_ref, lines = refs
+    held = jnp.concatenate([ref[...] for ref in held_refs], axis=0)
+    table = table_ref[kind if len(held_refs) > 1 else 0, :, : held.shape[0]]
+    lines[...] = jnp.dot(table, held, preferred_element_type=jnp.float32)
     cut = lines.shape[0] * LANES // SUB // angles
     per = LANES // cut
     row = lax.broadcasted_iota(jnp.int32, (SUB, LANES), 0)
@@ -399,7 +404,7 @@
     )(in_hbm(projections), in_hbm(flats))
 
 
-def make_own(own, turns, forward, inverse, gains, starts):
+def make_own(own, turns, forward, inverse, gains, starts, exchange):
     groups = turns.shape[1]
     return pl.pallas_call(
         own_kernel,
@@ -409,13 +414,14 @@
             jax.ShapeDtypeStruct(inverse.shape, inverse.dtype),
             jax.ShapeDtypeStruct((SUB, groups, SUB, LANES), jnp.float32),
             pltpu.SMEM((1, starts.shape[1]), jnp.int32),
+            jax.ShapeDtypeStruct(exchange.shape, exchange.dtype),
         ),
-        in_specs=[VMEM] * 3 + [HBM] * 3,
-        out_specs=(VMEM,) * 4 + (SMEM,),
-        scratch_shapes=[pltpu.SemaphoreType.DMA((3,))],
+        in_specs=[VMEM] * 3 + [HBM] * 4,
+        out_specs=(VMEM,) * 4 + (SMEM, VMEM),
+        scratch_shapes=[pltpu.SemaphoreType.DMA((4,))],
         compiler_params=PARAMS,
         name="own_rows",
-    )(own, turns, gains, in_hbm(forward), in_hbm(inverse), in_hbm(starts))
+    )(own, turns, gains, in_hbm(forward), in_hbm(inverse), in_hbm(starts), in_hbm(exchange))
 
 
 def make_tile(own_spec, below, above, starts, turns, forward, inverse, gains, cut):
@@ -444,17 +450,17 @@
     )(lines, first, second, third, table)
 
 
-def make_pixels(near, first, second, table, weights):
+def make_pixels(held, table, weights):
     angles, cut, pixels = weights.shape
     return pl.pallas_call(
         partial(pixels_kernel, angles=angles),
         out_shape=jax.ShapeDtypeStruct((SUB, pixels), jnp.float32),
-        in_specs=[VMEM] * 5,
+        in_specs=[VMEM] * (len(held) + 2),
         out_specs=VMEM,
         scratch_shapes=[pltpu.VMEM((table.shape[1], LANES), jnp.float32)],
         compiler_params=PARAMS,
         name="pixels",
-    )(near, first, second, table, weights.reshape(angles * cut, pixels))
+    )(*held, table, weights.reshape(angles * cut, pixels))
 
 
 def body(projections, flats, block_start, bp_weights):
@@ -468,24 +474,26 @@
     own, first, last = make_contrast(projections, flats)
     below = lax.ppermute(first, "row", down)
     above = lax.ppermute(last, "row", up)
-    own_spec, forward, inverse, gains, starts = make_own(own, turns, forward, inverse, gains, block_start)
+    routes = Routes(lax.axis_size("ang"))
+    exchange, arrival = jnp.asarray(routes.exchange_table()), jnp.asarray(routes.arrival_table())
+    own_spec, forward, inverse, gains, starts, exchange = make_own(
+        own, turns, forward, inverse, gains, block_start, exchange
+    )
     outgoing = make_tile(own_spec, below, above, starts, turns, forward, inverse, gains, cut)
-    routes = Routes(lax.axis_size("ang"))
     relayed = routes.taking_part(lax.axis_index("ang"), routes.count)
-    exchange, arrival = jnp.asarray(routes.exchange_table()), jnp.asarray(routes.arrival_table())
 
     def enter(lines):
         return make_repack(lines, *(lax.ppermute(lines, "ang", pairs) for pairs in routes.enter), exchange)
 
     def leave(lines):
-        return make_pixels(lines, *(lax.ppermute(lines, "ang", pairs) for pairs in routes.leave), arrival, bp_weights)
+        return make_pixels([lines, *(lax.ppermute(lines, "ang", pairs) for pairs in routes.leave)], arrival, bp_weights)
 
     packed = lax.cond(relayed, enter, lambda lines: make_repack(lines, lines, lines, lines, exchange), outgoing)
     near = lax.all_to_all(
         packed.reshape(-1, 2, LANES), "ang", split_axis=0, concat_axis=0, tiled=True,
         axis_index_groups=[routes.near, routes.far],
     ).reshape(packed.shape)
-    return lax.cond(relayed, leave, lambda lines: make_pixels(lines, lines, lines, arrival, bp_weights), near)
+    return lax.cond(relayed, leave, lambda lines: make_pixels([lines], arrival, bp_weights), near)
 
 
 def solution(mesh):

time: 65.7 us -> 65.6 us (level)
    unnamed x12 -> x10, local copies, waits for them, and re-layouts: 1.47 us -> 1.32 us
where the time goes in v16:
time: 65.6 us; the launch traced here: 65 us
  blocking collectives  52.5 us (80%)
  starting transfers between devices  5.9 us (9%)
  Pallas kernels  3.58 us (5%)
  waiting for transfers between devices  1.5 us (2%)
  local copies, waits for them, and re-layouts  1.32 us (2%)
    all_to_all x1, blocking collectives, body(): lax.all_to_all(packed.reshape(-1, 2, LANES), 'ang', split_axis=0, concat_...  52.5 us
    ppermute x1, starting transfers between devices, body(): above = lax.ppermute(last, 'row', up)  3.57 us
    ppermute x1, starting transfers between devices, body(): below = lax.ppermute(first, 'row', down)  2.34 us
    ppermute x1, waiting for transfers between devices, body(): above = lax.ppermute(last, 'row', up)  1.5 us
    pallas_call x1, Pallas kernels, make_own(): pl.pallas_call(own_kernel, out_shape=(jax.ShapeDtypeStruct((groups * SUB,...  1.32 us
    unnamed x10, local copies, waits for them, and re-layouts  1.32 us
  transfers between devices with their start and end apart: 2, of which 1 were waited for; matrix products, arithmetic and copies ran while one was open for 0% of the time, Pallas kernels for 2%

profile of v16, /device:TPU:88, one launch (start us, length us, event | category | flops | bytes accessed | tf_op | source)
XLA Modules:
  0.0 65.0 jit_solution(7251081328733234928)
XLA Ops:
  0.0 0.0 copy-start
  0.0 1.0 %contrast.1 = (f32[8,2560]{1,0:T(8,128)S(1)}, f32[4,2560]{1,0:T(4,128)S(1)}, f32[4,2560]{1,0:T(4,128)S(1)}) custom-call(bf16[1,8,2560]{2,1,0:T(8,128)(2,1)} %proj_hbm.1, f32[8,2560]{1,0:T(8,128)} %flat_hbm.1), custom_call_target="tpu_custom_call" | custom-call | tf_op jit(solution)/shard_map/contrast/pallas_call | solution.py:392
  1.0 2.3 %collective-permute-start.5 = (f32[4,2560]{1,0:T(4,128)S(1)}, f32[4,2560]{1,0:T(4,128)S(1)}, u32[]{:S(2)}, u32[]{:S(2)}) collective-permute-start(f32[4,2560]{1,0:T(4,128)S(1)} %get-tuple-element.52), channel_id=1, source_target_pairs={{1,0},{2,1},{3,2},{4,3},{5,4},{6,5},{7,6},{9,8},{10,9},{11,10},{12... | collective-permute-start | bytes 122888 | tf_op jit(solution)/shard_map/ppermute | solution.py:475
  3.3 3.6 %collective-permute-start.6 = (f32[4,2560]{1,0:T(4,128)S(1)}, f32[4,2560]{1,0:T(4,128)S(1)}, u32[]{:S(2)}, u32[]{:S(2)}) collective-permute-start(f32[4,2560]{1,0:T(4,128)S(1)} %get-tuple-element.53), channel_id=1, source_target_pairs={{0,1},{1,2},{2,3},{3,4},{4,5},{5,6},{6,7},{8,9},{9,10},{10,11},{11... | collective-permute-start | bytes 122888 | tf_op jit(solution)/shard_map/ppermute | solution.py:476
  6.9 0.0 copy-start.1
  6.9 0.0 copy-done
  7.0 0.7 %copy-done.1 = f32[2,11,128]{2,1,0:T(8,128)S(1)} copy-done((f32[2,11,128]{2,1,0:T(8,128)S(1)}, f32[2,11,128]{2,1,0:T(8,128)}, u32[]{:S(2)}) %copy-start.1) | copy-done | bytes 11288
  7.6 1.3 %own_rows.1 = (f32[88,256]{1,0:T(8,128)S(1)}, bf16[2,256,256]{2,1,0:T(8,128)(2,1)S(1)}, bf16[2,256,256]{2,1,0:T(8,128)(2,1)S(1)}, f32[8,11,8,128]{3,2,1,0:T(8,12...) custom-call(f32[8,2560]{1,0:T(8,128)S(1)} %get-tuple-element.50.own_ref, f32[2,11,128]{2,1,0:T(8,128)S(1)} %copy-done.1, ...), custom_call_target="tpu_custom_call" | custom-call | tf_op jit(solution)/shard_map/own_rows/pallas_call | solution.py:409
  9.0 0.0 collective-permute-done.5.below_ref
  9.0 1.5 %collective-permute-done.6.above_ref = f32[4,2560]{1,0:T(4,128)S(1)} collective-permute-done((f32[4,2560]{1,0:T(4,128)S(1)}, f32[4,2560]{1,0:T(4,128)S(1)}, u32[]{:S(2)}, u32[]{:S(2)}) %collective-permute-start.6) | collective-permute-done | bytes 40992 | tf_op jit(solution)/shard_map/ppermute | solution.py:476
  10.5 0.8 %tile.1 = bf16[64,128]{1,0:T(8,128)(2,1)S(1)} custom-call(f32[88,256]{1,0:T(8,128)S(1)} %get-tuple-element.51.own_ref, f32[4,2560]{1,0:T(4,128)S(1)} %collective-permute-done.5.below_ref, f32[4,2560]{1,0:T(4,128)S(1)} %collective-permute-done.6.above_ref, s32[1,32]{1,0:T(1,128)S(4)} %get-tuple-element.54.starts, f32[2,11,128]{2,1,0:T(8,128)S(1)} %copy-done.1, ...), custom_call_target="tpu_custom_call" | custom-call | tf_op jit(solution)/shard_map/tile/pallas_call | solution.py:429
  11.2 0.0 copy-start.2
  11.3 0.0 copy-start.3
  11.3 0.2 conditional.2
  11.3 0.2 repack.2
  11.4 52.5 %all_to_all.5 = bf16[64,2,128]{2,1,0:T(2,128)(2,1)S(1)} all-to-all(bf16[64,2,128]{2,1,0:T(2,128)(2,1)S(1)} %bitcast.8), channel_id=1, replica_groups={{192,200,208,216,224,232,240,248,0,8,16,24,32,40,48,56},{64,72,80,88,96..., dimensions={0} | all-to-all | bytes 65536 | tf_op jit(solution)/shard_map/all_to_all | solution.py:492
  64.0 0.0 copy-done.2
  64.0 0.0 copy-done.3
  64.0 0.4 conditional.3
  64.0 0.4 pixels.2
  64.4 0.0 copy-start.4
  64.4 0.6 copy-done.4
Async XLA Ops:
  0.0 6.9 %copy-start = (f32[9,11,128]{2,1,0:T(8,128)S(1)}, f32[9,11,128]{2,1,0:T(8,128)}, u32[]{:S(2)}) copy-start(f32[9,11,128]{2,1,0:T(8,128)} %constant.38.clone.gains_ref) | copy-start | bytes 152068
  1.0 8.0 %collective-permute-start.5 = (f32[4,2560]{1,0:T(4,128)S(1)}, f32[4,2560]{1,0:T(4,128)S(1)}, u32[]{:S(2)}, u32[]{:S(2)}) collective-permute-start(f32[4,2560]{1,0:T(4,128)S(1)} %get-tuple-element.52), channel_id=1, source_target_pairs={{1,0},{2,1},{3,2},{4,3},{5,4},{6,5},{7,6},{9,8},{10,9},{11,10},{12... | collective-permute-start | bytes 122888 | tf_op jit(solution)/shard_map/ppermute | solution.py:475
  3.3 7.1 %collective-permute-start.6 = (f32[4,2560]{1,0:T(4,128)S(1)}, f32[4,2560]{1,0:T(4,128)S(1)}, u32[]{:S(2)}, u32[]{:S(2)}) collective-permute-start(f32[4,2560]{1,0:T(4,128)S(1)} %get-tuple-element.53), channel_id=1, source_target_pairs={{0,1},{1,2},{2,3},{3,4},{4,5},{5,6},{6,7},{8,9},{9,10},{10,11},{11... | collective-permute-start | bytes 122888 | tf_op jit(solution)/shard_map/ppermute | solution.py:476
  6.9 0.7 %copy-start.1 = (f32[2,11,128]{2,1,0:T(8,128)S(1)}, f32[2,11,128]{2,1,0:T(8,128)}, u32[]{:S(2)}) copy-start(f32[2,11,128]{2,1,0:T(8,128)} %constant.35.clone.turns_ref) | copy-start | bytes 33796
  11.2 52.8 %copy-start.2 = (bf16[32,32,256]{2,1,0:T(8,128)(2,1)S(1)}, bf16[32,32,256]{2,1,0:T(8,128)(2,1)}, u32[]{:S(2)}) copy-start(bf16[32,32,256]{2,1,0:T(8,128)(2,1)} %param.17) | copy-start | bytes 1572868
  11.3 52.7 %copy-start.3 = (bf16[3,64,384]{2,1,0:T(8,128)(2,1)S(1)}, bf16[3,64,384]{2,1,0:T(8,128)(2,1)}, u32[]{:S(2)}) copy-start(bf16[3,64,384]{2,1,0:T(8,128)(2,1)} %constant.40.clone) | copy-start | bytes 442372
  64.4 0.6 copy-start.4

commit v17 on v16

--- a/solution.py
+++ b/solution.py
@@ -281,7 +281,7 @@
             link(((10, 1), (8, 2), (6, 3))),
             link(((11, 1), (9, 2), (7, 3))),
         ]
-        self.leave = [link(((12, 11), (13, 9), (14, 7), (3, 4))), link(((12, 10), (13, 8), (14, 6), (3, 5)))]
+        self.leave = [link(((12, 11), (13, 9), (2, 7), (3, 4))), link(((12, 10), (13, 8), (2, 6), (3, 5)))]
 
     def exchange_table(self):
         table = np.zeros((3, self.half * self.UNITS * 2, (1 + len(self.enter)) * self.count * 2), np.float32)
@@ -341,7 +341,7 @@
     @classmethod
     def taking_part(cls, device, count):
         step = device // (count // cls.AROUND)
-        return (step > 0) & (step < cls.AROUND - 1)
+        return (step > 0) & (step < cls.AROUND - 2)
 
 
 def repack_kernel(lines_ref, first_ref, second_ref, third_ref, table_ref, out_ref):

time: 65.6 us -> 65.6 us (level)
  no operation moved by 1% of the time
where the time goes in v17:
time: 65.6 us; the launch traced here: 65 us
  blocking collectives  52.5 us (80%)
  starting transfers between devices  5.9 us (9%)
  Pallas kernels  3.58 us (5%)
  waiting for transfers between devices  1.5 us (2%)
  local copies, waits for them, and re-layouts  1.32 us (2%)
    all_to_all x1, blocking collectives, body(): lax.all_to_all(packed.reshape(-1, 2, LANES), 'ang', split_axis=0, concat_...  52.5 us
    ppermute x1, starting transfers between devices, body(): above = lax.ppermute(last, 'row', up)  3.57 us
    ppermute x1, starting transfers between devices, body(): below = lax.ppermute(first, 'row', down)  2.34 us
    ppermute x1, waiting for transfers between devices, body(): above = lax.ppermute(last, 'row', up)  1.5 us
    pallas_call x1, Pallas kernels, make_own(): pl.pallas_call(own_kernel, out_shape=(jax.ShapeDtypeStruct((groups * SUB,...  1.32 us
    unnamed x10, local copies, waits for them, and re-layouts  1.32 us
  transfers between devices with their start and end apart: 2, of which 1 were waited for; matrix products, arithmetic and copies ran while one was open for 0% of the time, Pallas kernels for 2%

profile of v17, /device:TPU:88, one launch (start us, length us, event | category | flops | bytes accessed | tf_op | source)
XLA Modules:
  0.0 65.0 jit_solution(3655979000607027009)
XLA Ops:
  0.0 0.0 copy-start
  0.0 1.0 %contrast.1 = (f32[8,2560]{1,0:T(8,128)S(1)}, f32[4,2560]{1,0:T(4,128)S(1)}, f32[4,2560]{1,0:T(4,128)S(1)}) custom-call(bf16[1,8,2560]{2,1,0:T(8,128)(2,1)} %proj_hbm.1, f32[8,2560]{1,0:T(8,128)} %flat_hbm.1), custom_call_target="tpu_custom_call" | custom-call | tf_op jit(solution)/shard_map/contrast/pallas_call | solution.py:392
  1.0 2.3 %collective-permute-start.5 = (f32[4,2560]{1,0:T(4,128)S(1)}, f32[4,2560]{1,0:T(4,128)S(1)}, u32[]{:S(2)}, u32[]{:S(2)}) collective-permute-start(f32[4,2560]{1,0:T(4,128)S(1)} %get-tuple-element.52), channel_id=1, source_target_pairs={{1,0},{2,1},{3,2},{4,3},{5,4},{6,5},{7,6},{9,8},{10,9},{11,10},{12... | collective-permute-start | bytes 122888 | tf_op jit(solution)/shard_map/ppermute | solution.py:475
  3.3 3.6 %collective-permute-start.6 = (f32[4,2560]{1,0:T(4,128)S(1)}, f32[4,2560]{1,0:T(4,128)S(1)}, u32[]{:S(2)}, u32[]{:S(2)}) collective-permute-start(f32[4,2560]{1,0:T(4,128)S(1)} %get-tuple-element.53), channel_id=1, source_target_pairs={{0,1},{1,2},{2,3},{3,4},{4,5},{5,6},{6,7},{8,9},{9,10},{10,11},{11... | collective-permute-start | bytes 122888 | tf_op jit(solution)/shard_map/ppermute | solution.py:476
  6.9 0.0 copy-start.1
  6.9 0.0 copy-done
  7.0 0.7 %copy-done.1 = f32[2,11,128]{2,1,0:T(8,128)S(1)} copy-done((f32[2,11,128]{2,1,0:T(8,128)S(1)}, f32[2,11,128]{2,1,0:T(8,128)}, u32[]{:S(2)}) %copy-start.1) | copy-done | bytes 11288
  7.6 1.3 %own_rows.1 = (f32[88,256]{1,0:T(8,128)S(1)}, bf16[2,256,256]{2,1,0:T(8,128)(2,1)S(1)}, bf16[2,256,256]{2,1,0:T(8,128)(2,1)S(1)}, f32[8,11,8,128]{3,2,1,0:T(8,12...) custom-call(f32[8,2560]{1,0:T(8,128)S(1)} %get-tuple-element.50.own_ref, f32[2,11,128]{2,1,0:T(8,128)S(1)} %copy-done.1, ...), custom_call_target="tpu_custom_call" | custom-call | tf_op jit(solution)/shard_map/own_rows/pallas_call | solution.py:409
  9.0 0.0 collective-permute-done.5.below_ref
  9.0 1.5 %collective-permute-done.6.above_ref = f32[4,2560]{1,0:T(4,128)S(1)} collective-permute-done((f32[4,2560]{1,0:T(4,128)S(1)}, f32[4,2560]{1,0:T(4,128)S(1)}, u32[]{:S(2)}, u32[]{:S(2)}) %collective-permute-start.6) | collective-permute-done | bytes 40992 | tf_op jit(solution)/shard_map/ppermute | solution.py:476
  10.5 0.8 %tile.1 = bf16[64,128]{1,0:T(8,128)(2,1)S(1)} custom-call(f32[88,256]{1,0:T(8,128)S(1)} %get-tuple-element.51.own_ref, f32[4,2560]{1,0:T(4,128)S(1)} %collective-permute-done.5.below_ref, f32[4,2560]{1,0:T(4,128)S(1)} %collective-permute-done.6.above_ref, s32[1,32]{1,0:T(1,128)S(4)} %get-tuple-element.54.starts, f32[2,11,128]{2,1,0:T(8,128)S(1)} %copy-done.1, ...), custom_call_target="tpu_custom_call" | custom-call | tf_op jit(solution)/shard_map/tile/pallas_call | solution.py:429
  11.2 0.0 copy-start.2
  11.3 0.0 copy-start.3
  11.3 0.2 conditional.2
  11.3 0.2 repack.2
  11.4 52.5 %all_to_all.5 = bf16[64,2,128]{2,1,0:T(2,128)(2,1)S(1)} all-to-all(bf16[64,2,128]{2,1,0:T(2,128)(2,1)S(1)} %bitcast.8), channel_id=1, replica_groups={{192,200,208,216,224,232,240,248,0,8,16,24,32,40,48,56},{64,72,80,88,96..., dimensions={0} | all-to-all | bytes 65536 | tf_op jit(solution)/shard_map/all_to_all | solution.py:492
  64.0 0.0 copy-done.2
  64.0 0.0 copy-done.3
  64.0 0.4 conditional.3
  64.0 0.4 pixels.2
  64.4 0.0 copy-start.4
  64.4 0.6 copy-done.4
Async XLA Ops:
  0.0 6.9 %copy-start = (f32[9,11,128]{2,1,0:T(8,128)S(1)}, f32[9,11,128]{2,1,0:T(8,128)}, u32[]{:S(2)}) copy-start(f32[9,11,128]{2,1,0:T(8,128)} %constant.38.clone.gains_ref) | copy-start | bytes 152068
  1.0 8.0 %collective-permute-start.5 = (f32[4,2560]{1,0:T(4,128)S(1)}, f32[4,2560]{1,0:T(4,128)S(1)}, u32[]{:S(2)}, u32[]{:S(2)}) collective-permute-start(f32[4,2560]{1,0:T(4,128)S(1)} %get-tuple-element.52), channel_id=1, source_target_pairs={{1,0},{2,1},{3,2},{4,3},{5,4},{6,5},{7,6},{9,8},{10,9},{11,10},{12... | collective-permute-start | bytes 122888 | tf_op jit(solution)/shard_map/ppermute | solution.py:475
  3.3 7.1 %collective-permute-start.6 = (f32[4,2560]{1,0:T(4,128)S(1)}, f32[4,2560]{1,0:T(4,128)S(1)}, u32[]{:S(2)}, u32[]{:S(2)}) collective-permute-start(f32[4,2560]{1,0:T(4,128)S(1)} %get-tuple-element.53), channel_id=1, source_target_pairs={{0,1},{1,2},{2,3},{3,4},{4,5},{5,6},{6,7},{8,9},{9,10},{10,11},{11... | collective-permute-start | bytes 122888 | tf_op jit(solution)/shard_map/ppermute | solution.py:476
  6.9 0.7 %copy-start.1 = (f32[2,11,128]{2,1,0:T(8,128)S(1)}, f32[2,11,128]{2,1,0:T(8,128)}, u32[]{:S(2)}) copy-start(f32[2,11,128]{2,1,0:T(8,128)} %constant.35.clone.turns_ref) | copy-start | bytes 33796
  11.2 52.8 %copy-start.2 = (bf16[32,32,256]{2,1,0:T(8,128)(2,1)S(1)}, bf16[32,32,256]{2,1,0:T(8,128)(2,1)}, u32[]{:S(2)}) copy-start(bf16[32,32,256]{2,1,0:T(8,128)(2,1)} %param.17) | copy-start | bytes 1572868
  11.3 52.7 %copy-start.3 = (bf16[3,64,384]{2,1,0:T(8,128)(2,1)S(1)}, bf16[3,64,384]{2,1,0:T(8,128)(2,1)}, u32[]{:S(2)}) copy-start(bf16[3,64,384]{2,1,0:T(8,128)(2,1)} %constant.40.clone) | copy-start | bytes 442372
  64.4 0.6 copy-start.4

commit v18 on v16

--- a/solution.py
+++ b/solution.py
@@ -353,7 +353,7 @@
 
 def pixels_kernel(*refs, angles):
     _, kind = Routes.kinds(lax.axis_index("ang"), lax.axis_size("ang"))
-    *held_refs, table_ref, weights_ref, out_ref, lines = refs
+    *held_refs, table_ref, weights_ref, out_hbm, lines, out_ref, sem = refs
     held = jnp.concatenate([ref[...] for ref in held_refs], axis=0)
     table = table_ref[kind if len(held_refs) > 1 else 0, :, : held.shape[0]]
     lines[...] = jnp.dot(table, held, preferred_element_type=jnp.float32)
@@ -380,6 +380,9 @@
             part = mixed if shift == 0 else jnp.where(turn == shift, mixed, part)
         parts.append(part.astype(jnp.bfloat16))
     out_ref[...] = jnp.dot(jnp.concatenate(parts, axis=1), weights_ref[...], preferred_element_type=jnp.float32)
+    copy = pltpu.make_async_copy(out_ref, out_hbm, sem)
+    copy.start()
+    copy.wait()
 
 
 def in_hbm(array):
@@ -454,10 +457,14 @@
     angles, cut, pixels = weights.shape
     return pl.pallas_call(
         partial(pixels_kernel, angles=angles),
-        out_shape=jax.ShapeDtypeStruct((SUB, pixels), jnp.float32),
+        out_shape=pltpu.HBM((SUB, pixels), jnp.float32),
         in_specs=[VMEM] * (len(held) + 2),
-        out_specs=VMEM,
-        scratch_shapes=[pltpu.VMEM((table.shape[1], LANES), jnp.float32)],
+        out_specs=HBM,
+        scratch_shapes=[
+            pltpu.VMEM((table.shape[1], LANES), jnp.float32),
+            pltpu.VMEM((SUB, pixels), jnp.float32),
+            pltpu.SemaphoreType.DMA,
+        ],
         compiler_params=PARAMS,
         name="pixels",
     )(*held, table, weights.reshape(angles * cut, pixels))

time: 65.6 us -> 65.6 us (level)
    unnamed x10 -> x8, local copies, waits for them, and re-layouts: 1.32 us -> 0.71 us
where the time goes in v18:
time: 65.6 us; the launch traced here: 65 us
  blocking collectives  52.5 us (80%)
  starting transfers between devices  5.9 us (9%)
  Pallas kernels  4.2 us (6%)
  waiting for transfers between devices  1.49 us (2%)
  local copies, waits for them, and re-layouts  0.71 us (1%)
    all_to_all x1, blocking collectives, body(): lax.all_to_all(packed.reshape(-1, 2, LANES), 'ang', split_axis=0, concat_...  52.5 us
    ppermute x1, starting transfers between devices, body(): above = lax.ppermute(last, 'row', up)  3.57 us
    ppermute x1, starting transfers between devices, body(): below = lax.ppermute(first, 'row', down)  2.34 us
    ppermute x1, waiting for transfers between devices, body(): above = lax.ppermute(last, 'row', up)  1.49 us
    pallas_call x1, Pallas kernels, make_own(): pl.pallas_call(own_kernel, out_shape=(jax.ShapeDtypeStruct((groups * SUB,...  1.33 us
  transfers between devices with their start and end apart: 2, of which 1 were waited for; matrix products, arithmetic and copies ran while one was open for 0% of the time, Pallas kernels for 2%

profile of v18, /device:TPU:88, one launch (start us, length us, event | category | flops | bytes accessed | tf_op | source)
XLA Modules:
  0.0 65.0 jit_solution(5516809739260088518)
XLA Ops:
  0.0 0.0 copy-start
  0.0 1.0 %contrast.1 = (f32[8,2560]{1,0:T(8,128)S(1)}, f32[4,2560]{1,0:T(4,128)S(1)}, f32[4,2560]{1,0:T(4,128)S(1)}) custom-call(bf16[1,8,2560]{2,1,0:T(8,128)(2,1)} %proj_hbm.1, f32[8,2560]{1,0:T(8,128)} %flat_hbm.1), custom_call_target="tpu_custom_call" | custom-call | tf_op jit(solution)/shard_map/contrast/pallas_call | solution.py:395
  1.0 2.3 %collective-permute-start.5 = (f32[4,2560]{1,0:T(4,128)S(1)}, f32[4,2560]{1,0:T(4,128)S(1)}, u32[]{:S(2)}, u32[]{:S(2)}) collective-permute-start(f32[4,2560]{1,0:T(4,128)S(1)} %get-tuple-element.52), channel_id=1, source_target_pairs={{1,0},{2,1},{3,2},{4,3},{5,4},{6,5},{7,6},{9,8},{10,9},{11,10},{12... | collective-permute-start | bytes 122888 | tf_op jit(solution)/shard_map/ppermute | solution.py:482
  3.3 3.6 %collective-permute-start.6 = (f32[4,2560]{1,0:T(4,128)S(1)}, f32[4,2560]{1,0:T(4,128)S(1)}, u32[]{:S(2)}, u32[]{:S(2)}) collective-permute-start(f32[4,2560]{1,0:T(4,128)S(1)} %get-tuple-element.53), channel_id=1, source_target_pairs={{0,1},{1,2},{2,3},{3,4},{4,5},{5,6},{6,7},{8,9},{9,10},{10,11},{11... | collective-permute-start | bytes 122888 | tf_op jit(solution)/shard_map/ppermute | solution.py:483
  6.9 0.0 copy-start.1
  6.9 0.0 copy-done
  7.0 0.7 %copy-done.1 = f32[2,11,128]{2,1,0:T(8,128)S(1)} copy-done((f32[2,11,128]{2,1,0:T(8,128)S(1)}, f32[2,11,128]{2,1,0:T(8,128)}, u32[]{:S(2)}) %copy-start.1) | copy-done | bytes 11288
  7.6 1.3 %own_rows.1 = (f32[88,256]{1,0:T(8,128)S(1)}, bf16[2,256,256]{2,1,0:T(8,128)(2,1)S(1)}, bf16[2,256,256]{2,1,0:T(8,128)(2,1)S(1)}, f32[8,11,8,128]{3,2,1,0:T(8,12...) custom-call(f32[8,2560]{1,0:T(8,128)S(1)} %get-tuple-element.50.own_ref, f32[2,11,128]{2,1,0:T(8,128)S(1)} %copy-done.1, ...), custom_call_target="tpu_custom_call" | custom-call | tf_op jit(solution)/shard_map/own_rows/pallas_call | solution.py:412
  9.0 0.0 collective-permute-done.5.below_ref
  9.0 1.5 %collective-permute-done.6.above_ref = f32[4,2560]{1,0:T(4,128)S(1)} collective-permute-done((f32[4,2560]{1,0:T(4,128)S(1)}, f32[4,2560]{1,0:T(4,128)S(1)}, u32[]{:S(2)}, u32[]{:S(2)}) %collective-permute-start.6) | collective-permute-done | bytes 40992 | tf_op jit(solution)/shard_map/ppermute | solution.py:483
  10.5 0.8 %tile.1 = bf16[64,128]{1,0:T(8,128)(2,1)S(1)} custom-call(f32[88,256]{1,0:T(8,128)S(1)} %get-tuple-element.51.own_ref, f32[4,2560]{1,0:T(4,128)S(1)} %collective-permute-done.5.below_ref, f32[4,2560]{1,0:T(4,128)S(1)} %collective-permute-done.6.above_ref, s32[1,32]{1,0:T(1,128)S(4)} %get-tuple-element.54.starts, f32[2,11,128]{2,1,0:T(8,128)S(1)} %copy-done.1, ...), custom_call_target="tpu_custom_call" | custom-call | tf_op jit(solution)/shard_map/tile/pallas_call | solution.py:432
  11.2 0.0 copy-start.2
  11.2 0.0 copy-start.3
  11.3 0.2 conditional.2
  11.3 0.2 repack.2
  11.4 52.5 %all_to_all.5 = bf16[64,2,128]{2,1,0:T(2,128)(2,1)S(1)} all-to-all(bf16[64,2,128]{2,1,0:T(2,128)(2,1)S(1)} %bitcast.8), channel_id=1, replica_groups={{192,200,208,216,224,232,240,248,0,8,16,24,32,40,48,56},{64,72,80,88,96..., dimensions={0} | all-to-all | bytes 65536 | tf_op jit(solution)/shard_map/all_to_all | solution.py:499
  64.0 0.0 copy-done.2
  64.0 0.0 copy-done.3
  64.0 1.0 %conditional.3 = (f32[8,256]{1,0:T(8,128)}) conditional(s32[]{:T(128)} %convert_element_type.4, (bf16[32,32,256]{2,1,0:T(8,128)(2,1)S(1)}, bf16[128,128]{1,0:T(8,128)(2,1)S(1)}, bf16[3,64,384]{2,1,0:T(8,128)(2,1)S(1)}) %tuple.30, (bf16[128,128]{1,0:T(8,128)(2,1)S(1)}, bf16[32,32,256]{2,1,0:T(8,128)(2,1)S(1)}, bf16[3,64,384]{2,1,0:T(8,128)(2,1)S(1)}) %tuple.31), branch_computations={%region_2.3_spmd, %region_3.4_spmd} | conditional | bytes 262232 | solution.py:503
  64.0 1.0 %pixels.2 = f32[8,256]{1,0:T(8,128)} custom-call(bf16[128,128]{1,0:T(8,128)(2,1)S(1)} %get-tuple-element.35.refs_0_, bf16[3,64,384]{2,1,0:T(8,128)(2,1)S(1)} %get-tuple-element.36.refs_1_, bf16[1024,256]{1,0:T(8,128)(2,1)S(1)} %bitcast.4), custom_call_target="tpu_custom_call" | custom-call | tf_op jit(solution)/shard_map/cond/branch_0_fun/pixels/pallas_call | solution.py:458
Async XLA Ops:
  0.0 6.9 %copy-start = (f32[9,11,128]{2,1,0:T(8,128)S(1)}, f32[9,11,128]{2,1,0:T(8,128)}, u32[]{:S(2)}) copy-start(f32[9,11,128]{2,1,0:T(8,128)} %constant.38.clone.gains_ref) | copy-start | bytes 152068
  1.0 8.0 %collective-permute-start.5 = (f32[4,2560]{1,0:T(4,128)S(1)}, f32[4,2560]{1,0:T(4,128)S(1)}, u32[]{:S(2)}, u32[]{:S(2)}) collective-permute-start(f32[4,2560]{1,0:T(4,128)S(1)} %get-tuple-element.52), channel_id=1, source_target_pairs={{1,0},{2,1},{3,2},{4,3},{5,4},{6,5},{7,6},{9,8},{10,9},{11,10},{12... | collective-permute-start | bytes 122888 | tf_op jit(solution)/shard_map/ppermute | solution.py:482
  3.3 7.1 %collective-permute-start.6 = (f32[4,2560]{1,0:T(4,128)S(1)}, f32[4,2560]{1,0:T(4,128)S(1)}, u32[]{:S(2)}, u32[]{:S(2)}) collective-permute-start(f32[4,2560]{1,0:T(4,128)S(1)} %get-tuple-element.53), channel_id=1, source_target_pairs={{0,1},{1,2},{2,3},{3,4},{4,5},{5,6},{6,7},{8,9},{9,10},{10,11},{11... | collective-permute-start | bytes 122888 | tf_op jit(solution)/shard_map/ppermute | solution.py:483
  6.9 0.7 %copy-start.1 = (f32[2,11,128]{2,1,0:T(8,128)S(1)}, f32[2,11,128]{2,1,0:T(8,128)}, u32[]{:S(2)}) copy-start(f32[2,11,128]{2,1,0:T(8,128)} %constant.35.clone.turns_ref) | copy-start | bytes 33796
  11.2 52.8 %copy-start.2 = (bf16[32,32,256]{2,1,0:T(8,128)(2,1)S(1)}, bf16[32,32,256]{2,1,0:T(8,128)(2,1)}, u32[]{:S(2)}) copy-start(bf16[32,32,256]{2,1,0:T(8,128)(2,1)} %param.17) | copy-start | bytes 1572868
  11.2 52.7 %copy-start.3 = (bf16[3,64,384]{2,1,0:T(8,128)(2,1)S(1)}, bf16[3,64,384]{2,1,0:T(8,128)(2,1)}, u32[]{:S(2)}) copy-start(bf16[3,64,384]{2,1,0:T(8,128)(2,1)} %constant.40.clone) | copy-start | bytes 442372
